TPU v7x, 32 devices: a whole 2x2x4 slice. The times are simulated.
32 devices in a mesh: groups: 2 (over y), seq: 4 (over z), beam: 4 (over x, core).
Axes of the slice: x: 2, y: 2, z: 4, core: 2. Of those that a mesh axis runs over, the one named last changes fastest.
Arguments:
- prompt_values: bfloat16 [2048, 8192], P(('groups', 'seq'), 'beam'), parts along dimension 0, may hold values from -6 to 6
- prompt_keys: bfloat16 [2048, 128], P(('groups', 'seq')), parts along dimension 0, may hold values from -0.31445312 to 0.31445312
- prompt_queries: bfloat16 [2048, 128], P(('groups', 'seq')), parts along dimension 0, may hold values from -0.31445312 to 0.31445312
- logarithm_state_decay: float32 [2048, 128], P(('groups', 'seq'), 'beam'), parts along dimension 0, may hold values from -1 to 0
- step_values: bfloat16 [8, 4, 8192], P('groups', 'beam', 'seq'), parts along dimension 0, may hold values from -6 to 6
- step_keys: bfloat16 [8, 4, 128], P('groups', 'beam'), parts along dimension 0, may hold values from -6 to 6
- step_queries: bfloat16 [8, 4, 128], P('groups', 'beam'), parts along dimension 0, may hold values from -0.31445312 to 0.31445312
- step_decay: float32 [8, 4, 128], P('groups', 'beam', 'seq'), parts along dimension 0, may hold values from -0.6 to -0.02
- step_logprob: float32 [8, 4], P('groups', 'beam'), parts along dimension 0, may hold values from -6 to -0.05
- parents: int32 [8, 4], P('groups', 'beam'), parts along dimension 0, may hold values from 0 to 3
- finished: int32 [8, 4], P('groups', 'beam'), parts along dimension 0, may hold values 0 or 1
- lengths: int32 [8], P(('groups', 'beam')), parts along dimension 0, may hold values from 1 to 59
- init_score: float32 [8], P(('groups', 'beam')), parts along dimension 0, may hold values from -20 to -2
Outputs:
- prompt_output: bfloat16 [2048, 8192], P(('groups', 'seq'), 'beam'), parts along dimension 0
- step_output: bfloat16 [8, 4, 8192], P('groups', 'beam', 'seq'), parts along dimension 0
- ranked: float32 [8, 4], P('groups', 'beam'), parts along dimension 0
- beam_states: float32 [8, 8192, 128], P(('groups', 'beam'), 'seq'), parts along dimension 0
There are 2 independent parts, one for each index of `groups`. A program takes and returns all parts, laid end to end along the dimension named above; each array names one. Nothing has to cross between parts.
All inputs are finite; a program needn't handle non-finite values. No bound on the sum of `finished` on one device may be relied on, other than what follows from the above.
Results may differ from a plain program's by a relative error of at most 0.0056.
Values sent between devices are 32-bit elements; how exact they have to be, the bound alone decides.
No kernel may reach another device: no remote copies, remote signals or barrier semaphores. Data moves between devices by JAX's collectives and lax.ppermute only.
A program may use at most 64 MiB of HBM per device.

v0:
```python
import jax
import jax.numpy as jnp
from jax import lax
from jax.sharding import PartitionSpec as P

P_SIZE = 64
N = 128
STEPS = 4
SPAN = 256


def on_device(
    prompt_values,
    prompt_keys,
    prompt_queries,
    logarithm_state_decay,
    step_values,
    step_keys,
    step_queries,
    step_decay,
    step_logprob,
    parents,
    finished,
    lengths,
    init_score,
):
    token_rows = prompt_values.shape[0]
    head_count = logarithm_state_decay.shape[1]
    block_count = token_rows // SPAN
    values_blocks = prompt_values.reshape(block_count, SPAN, head_count, P_SIZE)
    keys_blocks = prompt_keys.reshape(block_count, SPAN, N)
    query_blocks = prompt_queries.reshape(block_count, SPAN, N)
    decay_sums = jnp.cumsum(logarithm_state_decay.reshape(block_count, SPAN, head_count), axis=1)
    lower = jnp.tril(jnp.ones((SPAN, SPAN), dtype=bool))

    def within(item):
        values_one, keys_one, query_one, sums_one = item
        scores = jnp.dot(query_one, keys_one.T, preferred_element_type=jnp.float32)
        spread = jnp.where(lower[:, :, None], sums_one[:, None, :] - sums_one[None, :, :], -jnp.inf)
        weights = (scores[:, :, None] * jnp.exp(spread)).astype(jnp.bfloat16)
        return jnp.einsum("ijh,jhp->ihp", weights, values_one, preferred_element_type=jnp.float32)

    inner_out = lax.map(within, (values_blocks, keys_blocks, query_blocks, decay_sums))
    tail_decay = jnp.exp(decay_sums[:, -1:, :] - decay_sums)
    scaled = (values_blocks * tail_decay[:, :, :, None]).astype(jnp.bfloat16)
    block_states = jnp.einsum(
        "kjhp,kjn->khpn", scaled, keys_blocks, preferred_element_type=jnp.float32
    )
    block_decay = jnp.exp(decay_sums[:, -1, :])

    def advance(carry, item):
        state_now, current_shrink_factor = carry
        single_token_decay, state_one = item
        return (
            (
                single_token_decay[:, None, None] * state_now + state_one,
                current_shrink_factor * single_token_decay,
            ),
            (state_now, current_shrink_factor),
        )

    zero_state = jnp.zeros((head_count, P_SIZE, N), jnp.float32)
    unit_decay = jnp.ones((head_count,), jnp.float32)
    (segment_finish, total_decay), (before, prior) = lax.scan(
        advance, (zero_state, unit_decay), (block_decay, block_states)
    )
    seq_index = lax.axis_index("seq")
    all_decays, all_states = (
        lax.all_gather(total_decay[None], "seq", axis=0, tiled=True),
        lax.all_gather(segment_finish[None], "seq", axis=0, tiled=True),
    )
    piece_ids = jnp.arange(all_decays.shape[0], dtype=jnp.int32)

    def collect(carry, item):
        running, mine = carry
        decay_one, state_one, piece_id = item
        mine = jnp.where(piece_id == seq_index, running, mine)
        running = decay_one[:, None, None] * running + state_one
        return ((running, mine), None)

    (full_block, arriving_input), unused = lax.scan(
        collect, (zero_state, zero_state), (all_decays, all_states, piece_ids)
    )
    starts = prior[:, :, None, None] * arriving_input[None] + before
    carried = (
        jnp.einsum(
            "kin,khpn->kihp",
            query_blocks,
            starts.astype(jnp.bfloat16),
            preferred_element_type=jnp.float32,
        )
        * jnp.exp(decay_sums)[:, :, :, None]
    )
    prompt_output = (
        (inner_out + carried).astype(jnp.bfloat16).reshape(token_rows, head_count * P_SIZE)
    )
    group_heads = step_values.shape[2] // P_SIZE
    first_head = seq_index * group_heads
    every_head = lax.all_gather(full_block, "beam", axis=0, tiled=True)
    own_heads = lax.dynamic_slice_in_dim(every_head, first_head, group_heads, 0)
    state_now = own_heads
    score_now = init_score
    length_now = lengths.astype(jnp.float32)
    step_list = []
    ranked_list = []
    for step_index in range(STEPS):
        parent_now = parents[step_index, 0]
        pieces = (
            lax.all_gather(state_now[None], "beam", axis=0, tiled=True),
            lax.all_gather(score_now, "beam", axis=0, tiled=True),
            lax.all_gather(length_now, "beam", axis=0, tiled=True),
        )
        slot_ids = jnp.arange(pieces[0].shape[0], dtype=jnp.int32)
        picked = (slot_ids == parent_now).astype(jnp.float32)
        state_part = jnp.sum(picked[:, None, None, None] * pieces[0], axis=0, keepdims=True)
        score_part = jnp.sum(picked * pieces[1]).reshape(1)
        length_part = jnp.sum(picked * pieces[2]).reshape(1)
        done = finished[step_index, 0] == 1
        live = (1 - finished[step_index]).astype(jnp.float32)
        values_now = step_values[step_index, 0].astype(jnp.float32).reshape(group_heads, P_SIZE)
        keys_now = step_keys[step_index, 0].astype(jnp.float32)
        updated = (
            jnp.exp(step_decay[step_index, 0])[:, None, None] * state_part[0]
            + values_now[:, :, None] * keys_now[None, None, :]
        )
        state_now = jnp.where(done, state_part[0], updated)
        output_now = jnp.einsum(
            "hpn,n->hp",
            state_now.astype(jnp.bfloat16),
            step_queries[step_index, 0],
            preferred_element_type=jnp.float32,
        )
        output_now = jnp.where(done, jnp.float32(0.0), output_now)
        step_list.append(output_now.reshape(1, group_heads * P_SIZE).astype(jnp.bfloat16))
        score_now = score_part + live * step_logprob[step_index]
        length_now = length_part + live
        normed = score_now / ((5.0 + length_now) / 6.0) ** 0.6
        best = lax.pmax(normed, "beam")
        ranked_list.append(normed - best)
    step_output = jnp.stack(step_list)
    ranked = jnp.stack(ranked_list)
    beam_states = state_now.reshape(1, group_heads * P_SIZE, N)
    return (prompt_output, step_output, ranked, beam_states)


def solution(mesh):
    return jax.shard_map(
        on_device,
        mesh=mesh,
        in_specs=(
            P(("groups", "seq"), "beam"),
            P(("groups", "seq"), None),
            P(("groups", "seq"), None),
            P(("groups", "seq"), "beam"),
            P("groups", "beam", "seq"),
            P("groups", "beam", None),
            P("groups", "beam", None),
            P("groups", "beam", "seq"),
            P("groups", "beam"),
            P("groups", "beam"),
            P("groups", "beam"),
            P(("groups", "beam")),
            P(("groups", "beam")),
        ),
        out_specs=(
            P(("groups", "seq"), "beam"),
            P("groups", "beam", "seq"),
            P("groups", "beam"),
            P(("groups", "beam"), "seq", None),
        ),
        check_vma=False,
    )
```

profile of v0, /device:TPU:25, one launch (start us, length us, event | category | flops | bytes accessed | tf_op | source)
XLA Modules:
  0.0 358.6 jit_solution(6325629616704435772)
XLA Ops:
  9.1 1.5 copy.50
  10.8 1.4 convolution_add_fusion
  12.3 5.6 %all-gather = f32[4,1,32]{2,1,0:T(1,128)S(1)} all-gather(f32[1,1,32]{2,1,0:T(1,128)S(1)} %get-tuple-element.163), channel_id=2, replica_groups=mesh['groups'=2,'seq'=4,'beam'=4] {'seq'}, dimensions={0}, use_global_device_ids=true | all-gather | bytes 640 | tf_op jit(solution)/shard_map/all_gather | solution.py:69
  17.9 73.6 %all-gather.18.cloned.1.call-done = f32[128,64,128]{2,1,0:T(8,128)} async-done(((f32[32,64,128]{2,1,0:T(8,128)}), f32[128,64,128]{2,1,0:T(8,128)}) %all-gather.18.cloned.1.call-update) | async-done | bytes 4194320 | tf_op jit(solution)/shard_map/all_gather | solution.py:70
  91.6 11.8 %while.3 = (s32[]{:T(128)}, f32[32,64,128]{2,1,0:T(8,128)S(1)}, bf16[32,64,128]{2,1,0:T(8,128)(2,1)S(1)}, f32[4,32]{1,0:T(4,128)S(1)}, f32[4,32,64,128]{3,2,1,0:...) while((s32[]{:T(128)}, f32[32,64,128]{2,1,0:T(8,128)S(1)}, ...), condition=%wide.region_3.4_spmd.clone, body=%wide.region_2.3_spmd.clone.sunk | while | flops 1572868 | bytes 5243406 | solution.py:81
  93.1 1.4 bitcast_add_fusion.7
  96.0 1.4 bitcast_add_fusion.7
  99.0 1.4 bitcast_add_fusion.7
  101.9 1.4 bitcast_add_fusion.7
  104.4 36.0 %all-gather.10.cloned.1.call-done = f32[128,64,128]{2,1,0:T(8,128)} async-done(((f32[32,64,128]{2,1,0:T(8,128)}), f32[128,64,128]{2,1,0:T(8,128)}) %all-gather.10.cloned.1.call-update) | async-done | bytes 4194320 | tf_op jit(solution)/shard_map/all_gather | solution.py:99
  140.4 2.3 constant_dynamic-slice_fusion
  145.6 31.8 %all-gather.20.cloned.1.call-done = f32[128,64,128]{2,1,0:T(8,128)} async-done(((f32[32,64,128]{2,1,0:T(8,128)}), f32[128,64,128]{2,1,0:T(8,128)}) %all-gather.20.cloned.1.call-update) | async-done | bytes 4194320 | tf_op jit(solution)/shard_map/all_gather | solution.py:109
  177.4 2.9 multiply_reduce_fusion.3
  180.2 1.3 bitcast_select_fusion.3
  183.0 33.2 %all-gather.12.cloned.1.call-done = f32[4,32,64,128]{3,2,1,0:T(8,128)} async-done(((f32[1,32,64,128]{3,2,1,0:T(8,128)}), f32[4,32,64,128]{3,2,1,0:T(8,128)}) %all-gather.12.cloned.1.call-update) | async-done | bytes 4194320 | tf_op jit(solution)/shard_map/all_gather | solution.py:109
  216.2 2.9 multiply_reduce_fusion.2
  220.1 1.4 bitcast_select_fusion.2
  222.9 33.2 %all-gather.14.cloned.1.call-done = f32[4,32,64,128]{3,2,1,0:T(8,128)} async-done(((f32[1,32,64,128]{3,2,1,0:T(8,128)}), f32[4,32,64,128]{3,2,1,0:T(8,128)}) %all-gather.14.cloned.1.call-update) | async-done | bytes 4194320 | tf_op jit(solution)/shard_map/all_gather | solution.py:109
  256.1 2.9 multiply_reduce_fusion.1
  260.0 1.4 bitcast_select_fusion.1
  264.8 5.3 %all-reduce.11 = (f32[4]{0:T(128)S(1)}, f32[4]{0:T(128)S(1)}) all-reduce(f32[4]{0:T(128)S(1)} %dynamic-update-slice, f32[4]{0:T(128)S(1)} %convert_dynamic-update-slice_fusion), channel_id=1, replica_groups=mesh['groups'=2,'seq'=4,'beam'=4] {'beam'}, use_global_device_ids=true, to_apply=%add | all-reduce | flops 8 | bytes 64
  270.7 1.3 select_reduce_fusion.6
  272.0 1.2 fusion.49
  274.6 1.7 fusion.50
  276.3 1.4 dynamic-update-slice.2
  277.7 1.4 dynamic-update-slice.3
  279.2 6.3 %all-reduce.10 = (f32[4]{0:T(128)S(1)}, f32[4]{0:T(128)S(1)}) all-reduce(f32[4]{0:T(128)S(1)} %dynamic-update-slice.2, f32[4]{0:T(128)S(1)} %dynamic-update-slice.3), channel_id=1, replica_groups=mesh['groups'=2,'seq'=4,'beam'=4] {'beam'}, use_global_device_ids=true, to_apply=%add.2 | all-reduce | flops 8 | bytes 64
  286.1 1.3 select_reduce_fusion.4
  287.3 1.2 fusion.47
  289.2 1.3 select_reduce_fusion.5
  290.5 1.7 fusion.48
  292.2 1.4 dynamic-update-slice.4
  293.6 1.4 dynamic-update-slice.5
  295.0 6.2 %all-reduce.9 = (f32[4]{0:T(128)S(1)}, f32[4]{0:T(128)S(1)}) all-reduce(f32[4]{0:T(128)S(1)} %dynamic-update-slice.4, f32[4]{0:T(128)S(1)} %dynamic-update-slice.5), channel_id=1, replica_groups=mesh['groups'=2,'seq'=4,'beam'=4] {'beam'}, use_global_device_ids=true, to_apply=%add.4 | all-reduce | flops 8 | bytes 64
  301.8 1.2 select_reduce_fusion.2
  304.9 1.2 select_reduce_fusion.3
  306.2 1.9 fusion.46
  308.1 1.4 dynamic-update-slice.6
  309.5 1.3 dynamic-update-slice.7
  310.8 6.0 %all-reduce.8 = (f32[4]{0:T(128)S(1)}, f32[4]{0:T(128)S(1)}) all-reduce(f32[4]{0:T(128)S(1)} %dynamic-update-slice.6, f32[4]{0:T(128)S(1)} %dynamic-update-slice.7), channel_id=1, replica_groups=mesh['groups'=2,'seq'=4,'beam'=4] {'beam'}, use_global_device_ids=true, to_apply=%add.6 | all-reduce | flops 8 | bytes 64
  318.1 1.2 select_reduce_fusion
  320.1 1.2 select_reduce_fusion.1
  322.0 7.2 %all-reduce.12 = (f32[1]{0:T(128)}, f32[1]{0:T(128)}, f32[1]{0:T(128)}, f32[1]{0:T(128)}) all-reduce(f32[1]{0:T(128)S(6)} %div.31, f32[1]{0:T(128)} %get-tuple-element.186, f32[1]{0:T(128)} %get-tuple-element.190, f32[1]{0:T(128)} %get-tuple-element.194), channel_id=1, replica_groups=mesh['groups'=2,'seq'=4,'beam'=4] {'beam'}, use_global_device_ids=true, to_apply=%region_19.20 | all-reduce | flops 4 | bytes 32 | tf_op jit(solution)/shard_map/pmax | solution.py:138
  336.6 3.7 %fusion.7 = bf16[256,32,64]{0,2,1:T(8,128)(2,1)} fusion(f32[32,64,256]{2,1,0:T(8,128)S(1)} %fusion.13, bf16[256,32,64]{0,2,1:T(8,128)(2,1)S(1)} %bitcast.193, f32[256,32]{0,1:T(8,128)S(1)} %copy.48, f32[256,256]{1,0:T(8,128)S(1)} %fusion.51, pred[256,256]{1,0:T(8,128)(4,1)S(1)} %iota_compare_fusion, f32[256,32]{0,1:T(8,128)S(1)} %copy.53), kind=kOutput, calls=%fused_computation.16 | convolution fusion | flops 278396928 | bytes 4587520 | tf_op jit(solution)/shard_map/while/body/eval_jaxpr/ijh,jhp->ihp/dot_general | solution.py:41
  340.3 2.4 copy.54
  343.3 1.8 fusion.16
  346.0 2.9 multiply_reduce_fusion
  349.5 1.6 bitcast_select_fusion
  (116 shorter events, 21.2 us)
Async XLA Ops:
  7.2 328.8 %copy-start = (bf16[256,128]{1,0:T(8,128)(2,1)S(1)}, bf16[256,128]{1,0:T(8,128)(2,1)}, u32[]{:S(2)}) copy-start(bf16[256,128]{1,0:T(8,128)(2,1)} %param.17) | copy-start | bytes 196612
  7.2 3.6 %copy-start.5 = (bf16[256,128]{1,0:T(8,128)(2,1)S(1)}, bf16[256,128]{1,0:T(8,128)(2,1)}, u32[]{:S(2)}) copy-start(bf16[256,128]{1,0:T(8,128)(2,1)} %param.16) | copy-start | bytes 196612
  7.2 84.4 %all-gather.18.cloned.1.call-start = ((), (), s32[]{:S(2)}) async-start(), calls=%async_computation.4 | async-start | bytes 5242880 | tf_op jit(solution)/shard_map/all_gather | solution.py:70
  12.3 128.2 %all-gather.10.cloned.1.call-start = ((), (), s32[]{:S(2)}) async-start(), calls=%async_computation | async-start | bytes 5242880 | tf_op jit(solution)/shard_map/all_gather | solution.py:99
  103.3 1.0 copy-start.1
  103.4 39.4 %copy-start.6 = (bf16[4,1,2048]{2,0,1:T(4,128)(2,1)S(1)}, bf16[4,1,2048]{2,0,1:T(4,128)(2,1)}, u32[]{:S(2)}) copy-start(bf16[4,1,2048]{2,0,1:T(4,128)(2,1)} %param.19) | copy-start | bytes 49156
  103.4 39.6 %copy-start.7 = (s32[4,1]{0,1:T(1,128)S(1)}, s32[4,1]{0,1:T(1,128)}, u32[]{:S(2)}) copy-start(s32[4,1]{0,1:T(1,128)} %param.25) | copy-start | bytes 52
  103.4 40.9 %copy-start.8 = (s32[4,1]{0,1:T(1,128)S(1)}, s32[4,1]{0,1:T(1,128)}, u32[]{:S(2)}) copy-start(s32[4,1]{0,1:T(1,128)} %param.24) | copy-start | bytes 52
  103.4 42.2 %copy-start.11 = (f32[4,1,32]{2,1,0:T(1,128)S(1)}, f32[4,1,32]{2,1,0:T(1,128)}, u32[]{:S(2)}) copy-start(f32[4,1,32]{2,1,0:T(1,128)} %param.22) | copy-start | bytes 1540
  103.4 42.2 %copy-start.10 = (bf16[4,1,128]{2,0,1:T(4,128)(2,1)S(1)}, bf16[4,1,128]{2,0,1:T(4,128)(2,1)}, u32[]{:S(2)}) copy-start(bf16[4,1,128]{2,0,1:T(4,128)(2,1)} %param.20) | copy-start | bytes 3076
  104.3 73.0 %all-gather.20.cloned.1.call-start = ((), (), s32[]{:S(2)}) async-start(), calls=%async_computation.5 | async-start | bytes 5242880 | tf_op jit(solution)/shard_map/all_gather | solution.py:109
  142.8 73.5 %all-gather.12.cloned.1.call-start = ((), (), s32[]{:S(2)}) async-start(), calls=%async_computation.1 | async-start | bytes 5242880 | tf_op jit(solution)/shard_map/all_gather | solution.py:109
  181.6 74.5 %all-gather.14.cloned.1.call-start = ((), (), s32[]{:S(2)}) async-start(), calls=%async_computation.2 | async-start | bytes 5242880 | tf_op jit(solution)/shard_map/all_gather | solution.py:109
  219.1 1.0 copy-start.2
  221.5 124.5 %all-gather.16.cloned.1.call-start = ((), (), s32[]{:S(2)}) async-start(), calls=%async_computation.3 | async-start | bytes 5242880 | tf_op jit(solution)/shard_map/all_gather | solution.py:109
  222.9 39.8 %copy-start.13 = (u32[32]{0:T(128)S(1)}, u32[32]{0:T(128)}, u32[]{:S(2)}) copy-start(u32[32]{0:T(128)} %constant.105) | copy-start | bytes 388
  222.9 51.0 %copy-start.9 = (f32[4,1]{0,1:T(1,128)S(1)}, f32[4,1]{0,1:T(1,128)}, u32[]{:S(2)}) copy-start(f32[4,1]{0,1:T(1,128)} %param.23) | copy-start | bytes 52
  259.0 1.0 copy-start.3
  336.6 6.1 %copy-start.12 = (bf16[4,1,128]{2,0,1:T(4,128)(2,1)S(1)}, bf16[4,1,128]{2,0,1:T(4,128)(2,1)}, u32[]{:S(2)}) copy-start(bf16[4,1,128]{2,0,1:T(4,128)(2,1)} %param.21) | copy-start | bytes 3076
  340.3 5.0 %copy-start.4 = (f32[32,64,128]{2,1,0:T(8,128)S(1)}, f32[32,64,128]{2,1,0:T(8,128)}, u32[]{:S(2)}) copy-start(f32[32,64,128]{2,1,0:T(8,128)} %copy-done.3) | copy-start | bytes 3145732
Sparse Core Ops, SparseCore 0:
  12.4 79.1 all-gather.17
  104.5 35.9 all-gather.9
  142.9 34.4 all-gather.19
  181.7 34.4 all-gather.11
  221.6 34.4 all-gather.13
  261.5 34.5 all-gather.15
where the time goes:
time: 362 us; the launch traced here: 359 us
  waiting for transfers between devices  208 us (57%)
  other arithmetic  47.2 us (13%)
  blocking collectives  36.4 us (10%)
  between operations  29.5 us (8%)
  local copies, waits for them, and re-layouts  25.3 us (7%)
  matrix products  9.29 us (3%)
    all_gather x4, waiting for transfers between devices, on_device(): lax.all_gather(state_now[None], 'beam', axis=0, tiled=True)  98.2 us
    all_gather x1, waiting for transfers between devices, on_device(): lax.all_gather(segment_finish[None], 'seq', axis=0, tiled=True)  73.6 us
    all_gather x1, waiting for transfers between devices, on_device(): every_head = lax.all_gather(full_block, 'beam', axis=0, tiled=True)  36 us
    unnamed x4, blocking collectives  23.7 us
    unnamed x46, local copies, waits for them, and re-layouts  16.5 us
    reduce_sum x4, other arithmetic, on_device(): jnp.sum(picked[:, None, None, None] * pieces[0], axis=0, keepdims=True)  11.5 us
  transfers between devices with their start and end apart: 6, of which 5 were waited for; matrix products, arithmetic and copies ran while one was open for 12% of the time, Pallas kernels for 0%

commit v1 on v0

v1 whole, which is shorter than its diff:
```python
import functools

import jax
import jax.numpy as jnp
from jax import lax
from jax.experimental import pallas as pl
from jax.experimental.pallas import tpu as pltpu
from jax.sharding import PartitionSpec as P

LANES = 128
SUB = 8
QUARTERS = 4
F32 = jnp.float32
BF16 = jnp.bfloat16
HIGH = lax.Precision.HIGHEST
TN = (((0,), (0,)), ((), ()))
NT = (((1,), (1,)), ((), ()))

VMEM = pl.BlockSpec(memory_space=pltpu.VMEM)
SMEM = pl.BlockSpec(memory_space=pltpu.SMEM)


def call(body, args, out_shape, in_specs=None, flops=1_000_000, **kwargs):
    return pl.pallas_call(
        body,
        out_shape=out_shape,
        in_specs=in_specs,
        cost_estimate=pl.CostEstimate(flops=flops, bytes_accessed=1_000_000, transcendentals=0),
        **kwargs,
    )(*args)


def iota(shape, axis):
    return lax.broadcasted_iota(jnp.int32, shape, axis)


def head_lanes(heads, first, count, width):
    shape = (heads, count * width)
    return (iota(shape, 0) == first + iota(shape, 1) // width).astype(F32)


def quarter_state(values, keys, sums, first, count, width, out_ref):
    heads = sums.shape[1]
    last = sums[-1:, :]
    tail = jnp.dot(jnp.exp(last - sums), head_lanes(heads, first, count, width), precision=HIGH, preferred_element_type=F32)
    scaled = (values.astype(F32) * tail).astype(BF16)
    rows = count * width
    out_ref[0:rows, :] = lax.dot_general(scaled, keys, TN, preferred_element_type=F32)
    pad = out_ref.shape[0] - rows
    pick = iota((pad, heads), 1) == first + iota((pad, heads), 0)
    total = jnp.sum(jnp.where(pick, last, 0.0), axis=1, keepdims=True)
    out_ref[rows:, :] = jnp.broadcast_to(jnp.exp(total), (pad, LANES))


def first_kernel(quarter_ref, values_ref, keys_ref, decay_ref, sums_ref, out_ref, *, count, width):
    tokens = decay_ref.shape[0]
    lower = (iota((tokens, tokens), 0) >= iota((tokens, tokens), 1)).astype(F32)
    sums = jnp.dot(lower, decay_ref[...], precision=HIGH, preferred_element_type=F32)
    sums_ref[...] = sums
    quarter = quarter_ref[0]
    lanes = count * width
    values = values_ref[:, pl.ds(pl.multiple_of(quarter * lanes, lanes), lanes)]
    quarter_state(values, keys_ref[...], sums, quarter * count, count, width, out_ref)


def rest_kernel(quarter_ref, values_ref, keys_ref, sums_ref, *out_refs, count, width):
    lanes = count * width
    for k, out_ref in enumerate(out_refs):
        quarter = quarter_ref[k + 1]
        values = values_ref[:, pl.ds(pl.multiple_of(quarter * lanes, lanes), lanes)]
        quarter_state(values, keys_ref[...], sums_ref[...], quarter * count, count, width, out_ref)


def inner_kernel(values_ref, keys_ref, queries_ref, sums_ref, out_ref, turned_ref, wide_ref, *, count, width):
    tokens, heads = sums_ref.shape
    half = tokens // 2
    wide_ref[...] = jnp.zeros_like(wide_ref)
    wide_ref[:, 0:heads] = sums_ref[...]
    turned_ref[...] = wide_ref[...].T
    scores = lax.dot_general(queries_ref[...], keys_ref[...], NT, preferred_element_type=F32)
    lower = iota((half, half), 0) >= iota((half, half), 1)
    top = jnp.where(lower, scores[:half, :half], 0.0)
    left = scores[half:, :half]
    bottom = jnp.where(lower, scores[half:, half:], 0.0)
    per_store = LANES // width

    def group(g, carry):
        wide = pltpu.roll(wide_ref[...], lax.rem(LANES - g * count, LANES), 1)
        for k in range(count // per_store):
            place = pl.ds(pl.multiple_of((g * count + k * per_store) * width, LANES), LANES)
            values = values_ref[:, place]
            tops, bottoms = [], []
            for m in range(per_store):
                h = k * per_store + m
                column = wide[:, h : h + 1]
                row = turned_ref[pl.ds(g * count + h, 1), :]
                x = values[:, m * width : (m + 1) * width]
                w0 = (top * jnp.exp(jnp.minimum(column[:half] - row[:, :half], 0.0))).astype(BF16)
                w1 = (left * jnp.exp(column[half:] - row[:, :half])).astype(BF16)
                w2 = (bottom * jnp.exp(jnp.minimum(column[half:] - row[:, half:], 0.0))).astype(BF16)
                tops.append(jnp.dot(w0, x[:half], preferred_element_type=F32))
                bottoms.append(jnp.dot(jnp.concatenate([w1, w2], axis=1), x, preferred_element_type=F32))
            out_ref[0:half, place] = jnp.concatenate(tops, axis=1)
            out_ref[half:, place] = jnp.concatenate(bottoms, axis=1)
        return carry

    lax.fori_loop(0, heads // count, group, 0)


def combine(low, high, out, count, width, decay=True):
    rows = count * width
    for h in range(count):
        place = slice(h * width, (h + 1) * width)
        out[place, :] = high[rows + h : rows + h + 1, :] * low[place, :] + high[place, :]
    if decay:
        out[rows:, :] = low[rows:, :] * high[rows:, :]


def pair_kernel(rank_ref, keep_ref, got_ref, out_ref, *, count, width):
    odd = rank_ref[0] == 1

    @pl.when(odd)
    def _():
        combine(got_ref, keep_ref, out_ref, count, width)

    @pl.when(jnp.logical_not(odd))
    def _():
        combine(keep_ref, got_ref, out_ref, count, width)


def round_kernel(rank_ref, total_ref, got_ref, *refs, bit, first, count, width):
    before_ref, refs = (None, refs) if first else (refs[0], refs[1:])
    before_out, total_out = refs
    upper = rank_ref[bit] == 1
    rows = count * width

    @pl.when(upper)
    def _():
        combine(got_ref, total_ref, total_out, count, width)
        if first:
            before_out[...] = got_ref[...]
        else:
            combine(got_ref, before_ref, before_out, count, width)

    @pl.when(jnp.logical_not(upper))
    def _():
        combine(total_ref, got_ref, total_out, count, width)
        if first:
            before_out[0:rows, :] = jnp.zeros((rows, LANES), F32)
            before_out[rows:, :] = jnp.ones((before_out.shape[0] - rows, LANES), F32)
        else:
            before_out[...] = before_ref[...]


def last_kernel(rank_ref, total_ref, got_ref, keep_ref, swap_ref, *refs, bit, first, pieces, count, width):
    before_ref, refs = (None, refs) if first else (refs[0], refs[1:])
    piece_refs, own_ref, hand_ref, before_now = refs[:pieces], refs[pieces], refs[pieces + 1], refs[pieces + 2]
    upper = rank_ref[bit] == 1
    odd = rank_ref[0] == 1
    rows = count * width
    per_piece = count // pieces

    def final(low, high):
        for h in range(count):
            place = slice(h * width, (h + 1) * width)
            start = (h % per_piece) * width
            piece_refs[h // per_piece][start : start + width, :] = (
                high[rows + h : rows + h + 1, :] * low[place, :] + high[place, :]
            )

    @pl.when(upper)
    def _():
        final(got_ref, total_ref)
        if first:
            before_now[...] = got_ref[0:rows, :]
        else:
            combine(got_ref, before_ref, before_now, count, width, decay=False)

    @pl.when(jnp.logical_not(upper))
    def _():
        final(total_ref, got_ref)
        before_now[...] = jnp.zeros_like(before_now) if first else before_ref[0:rows, :]

    @pl.when(odd)
    def _():
        combine(before_now, swap_ref, own_ref, count, width, decay=False)
        hand_ref[...] = before_now[...]

    @pl.when(jnp.logical_not(odd))
    def _():
        own_ref[...] = before_now[...]
        combine(before_now, keep_ref, hand_ref, count, width, decay=False)


def output_kernel(rank_ref, own_ref, other_ref, queries_ref, sums_ref, inner_ref, *refs, sub, count, width):
    out_ref = refs[-1]
    half = pl.program_id(0)
    heads = sums_ref.shape[1]
    first = (half * 2 + sub) * count

    def emit(state_ref):
        carried = lax.dot_general(queries_ref[...], state_ref[...].astype(BF16), NT, preferred_element_type=F32)
        grown = jnp.dot(
            jnp.exp(sums_ref[...]), head_lanes(heads, first, count, width), precision=HIGH, preferred_element_type=F32
        )
        out_ref[...] = (inner_ref[...] + carried * grown).astype(BF16)

    mine = rank_ref[0] == half

    @pl.when(mine)
    def _():
        emit(own_ref)

    @pl.when(jnp.logical_not(mine))
    def _():
        emit(other_ref)


def lineage_kernel(
    beam_ref, scalar_ref, rows_ref, queries_ref, grow_ref, part_ref, outer_ref, key_ref, shrink_ref, ranked_ref,
    scores, counts, *, slots, steps, wide, width
):
    me = beam_ref[0]
    done = lambda slot, step: scalar_ref[slot * steps + step, 2]
    parent = lambda slot, step: scalar_ref[slot * steps + step, 1].astype(jnp.int32)
    for slot in range(slots):
        scores[0, slot] = scalar_ref[slot * steps, 4]
        counts[0, slot] = scalar_ref[slot * steps, 3]
    lane = iota((1, LANES), 1)
    for step in range(steps):
        score_row = jnp.zeros((1, LANES), F32)
        count_row = jnp.zeros((1, LANES), F32)
        for slot in range(slots):
            source = parent(slot, step)
            live = 1.0 - done(slot, step)
            score = scores[step, source] + live * scalar_ref[slot * steps + step, 0]
            tally = counts[step, source] + live
            scores[step + 1, slot] = score
            counts[step + 1, slot] = tally
            score_row = jnp.where(lane == slot, score, score_row)
            count_row = jnp.where(lane == slot, tally, count_row)
        normed = score_row * jnp.exp(-0.6 * jnp.log((5.0 + count_row) / 6.0))
        best = jnp.max(jnp.where(lane < slots, normed, -jnp.inf), axis=1, keepdims=True)
        mine = jnp.sum(jnp.where(lane == me, normed, 0.0), axis=1, keepdims=True)
        ranked_ref[step : step + 1, :] = jnp.broadcast_to(mine - best, (1, LANES))

    for ref in (grow_ref, part_ref, outer_ref, key_ref):
        ref[...] = jnp.zeros_like(ref)
    for step in range(steps):
        slot = me
        factor = jnp.ones((1, wide), F32)
        part = jnp.zeros((1, wide), F32)
        query = queries_ref[step : step + 1, :].astype(F32)
        live_now = 1.0 - done(me, step)
        for back in range(step, -1, -1):
            record = rows_ref[slot * steps + back]
            live = 1.0 - done(slot, back)
            values = record[:, 0:wide]
            key = record[:, 2 * wide : 2 * wide + LANES]
            weight = factor * (values * live)
            part = part + weight * jnp.sum(key * query, axis=1, keepdims=True)
            if step == steps - 1:
                outer_ref[back : back + 1, :] = weight
                key_ref[back : back + 1, :] = key
            factor = factor * jnp.exp(record[:, wide : 2 * wide] * live)
            slot = parent(slot, back)
        grow_ref[step : step + 1, :] = factor * live_now
        part_ref[step : step + 1, :] = part * live_now
        if step == steps - 1:
            count = shrink_ref.shape[0]
            pick = iota((count, wide), 1) == iota((count, wide), 0) * width
            shrink_ref[...] = jnp.broadcast_to(
                jnp.sum(jnp.where(pick, factor, 0.0), axis=1, keepdims=True), (count, LANES)
            )


def decode_kernel(final_ref, queries_ref, grow_ref, part_ref, outer_ref, key_ref, shrink_ref, *refs, count, width):
    state_ref, out_ref = refs[-2:]
    final = final_ref[...]
    product = lax.dot_general(queries_ref[...], final.astype(BF16), NT, preferred_element_type=F32)
    steps = out_ref.shape[0]
    out_ref[...] = (grow_ref[0:steps, :] * product[0:steps, :] + part_ref[0:steps, :]).astype(BF16)
    fresh = lax.dot_general(outer_ref[...], key_ref[...], TN, precision=HIGH, preferred_element_type=F32)
    for h in range(count):
        place = slice(h * width, (h + 1) * width)
        state_ref[place, :] = shrink_ref[h : h + 1, :] * final[place, :] + fresh[place, :]


def on_device(
    prompt_values, prompt_keys, prompt_queries, logarithm_state_decay, step_values, step_keys, step_queries, step_decay,
    step_logprob, parents, finished, lengths, init_score, *, ranks, slots
):
    tokens, heads = logarithm_state_decay.shape
    width = prompt_values.shape[1] // heads
    steps = step_values.shape[0]
    wide = step_values.shape[2]
    own_heads = wide // width
    count = heads // QUARTERS
    rows = count * width
    message = jax.ShapeDtypeStruct((rows + -(-count // SUB) * SUB, LANES), F32)
    state = jax.ShapeDtypeStruct((rows, LANES), F32)
    sizes = dict(count=count, width=width)
    levels = ranks.bit_length() - 1
    rank = lax.axis_index("seq")
    beam = lax.axis_index("beam").astype(jnp.int32)[None]
    bits = jnp.stack([(rank >> k) & 1 for k in range(levels)]).astype(jnp.int32)
    quarters = jnp.stack([2 - 2 * bits[0], 3 - 2 * bits[0], 2 * bits[0], 2 * bits[0] + 1]).astype(jnp.int32)

    sums, send_a = call(
        functools.partial(first_kernel, **sizes),
        (quarters, prompt_values, prompt_keys, logarithm_state_decay),
        (jax.ShapeDtypeStruct((tokens, heads), F32), message),
        [SMEM, VMEM, VMEM, VMEM],
    )
    swap = [(k, k ^ 1) for k in range(ranks)]
    got_a = lax.ppermute(send_a, "seq", swap)
    send_b, keep_a, keep_b = call(
        functools.partial(rest_kernel, **sizes),
        (quarters, prompt_values, prompt_keys, sums),
        (message,) * 3,
        [SMEM, VMEM, VMEM, VMEM],
    )
    got_b = lax.ppermute(send_b, "seq", swap)
    keeps, swaps = (keep_a, keep_b), (got_a, got_b)

    whole = jnp.concatenate([lengths.astype(F32), init_score])[None]
    scalars = jnp.concatenate(
        [step_logprob, parents.astype(F32), finished.astype(F32), jnp.broadcast_to(whole, (steps, 2))], axis=1
    )
    packed = jnp.concatenate(
        [
            step_values[:, 0].astype(F32),
            jnp.repeat(step_decay[:, 0], width, axis=1),
            step_keys[:, 0].astype(F32),
            jnp.pad(scalars, ((0, 0), (0, LANES - scalars.shape[1]))),
        ],
        axis=1,
    )[:, None, :]
    gathered = lax.all_gather(packed, "beam", axis=0, tiled=True)
    queries = jnp.pad(step_queries[:, 0], ((0, -steps % SUB), (0, 0)))
    line = jax.ShapeDtypeStruct((SUB, wide), F32)
    grow, part, outer, key_rows, shrink, ranked = call(
        functools.partial(lineage_kernel, slots=slots, steps=steps, wide=wide, width=width),
        (beam, gathered[:, 0, 2 * wide + LANES :], gathered, queries),
        (
            line, line, line, jax.ShapeDtypeStruct((SUB, LANES), F32), jax.ShapeDtypeStruct((own_heads, LANES), F32),
            jax.ShapeDtypeStruct((steps, LANES), F32),
        ),
        [SMEM, SMEM, VMEM, VMEM],
        scratch_shapes=[pltpu.SMEM((steps + 1, slots), F32), pltpu.SMEM((steps + 1, slots), F32)],
    )
    ranked = ranked[:, :1]

    inner = call(
        functools.partial(inner_kernel, **sizes),
        (prompt_values, prompt_keys, prompt_queries, sums),
        jax.ShapeDtypeStruct((tokens, heads * width), F32),
        [VMEM] * 4,
        scratch_shapes=[pltpu.VMEM((LANES, tokens), F32), pltpu.VMEM((tokens, LANES), F32)],
        flops=100_000_000,
    )

    direct = ranks == slots
    pieces = slots // 2 if direct else 1
    piece = jax.ShapeDtypeStruct((rows // pieces, LANES), F32)
    out = states = step_out = None
    halves = []
    for sub in range(2):
        total = call(
            functools.partial(pair_kernel, **sizes), (bits, keeps[sub], swaps[sub]), message, [SMEM, VMEM, VMEM]
        )
        before = ()
        for level in range(1, levels):
            got = lax.ppermute(total, "seq", [(k, k ^ (1 << level)) for k in range(ranks)])
            if level < levels - 1:
                before_now, total = call(
                    functools.partial(round_kernel, bit=level, first=level == 1, **sizes),
                    (bits, total, got) + before,
                    (message, message),
                    [SMEM] + [VMEM] * (2 + len(before)),
                )
                before = (before_now,)
        *final, own, hand = call(
            functools.partial(last_kernel, bit=levels - 1, first=levels == 2, pieces=pieces, **sizes),
            (bits, total, got, keeps[sub], swaps[sub]) + before,
            (piece,) * pieces + (state, state),
            [SMEM] + [VMEM] * (4 + len(before)),
            scratch_shapes=[pltpu.VMEM((rows, LANES), F32)],
        )
        halves.append(final)
        if direct:
            landed = None
            for k in range(pieces):
                pairs = [
                    ((g // 2 * 2 + half) * slots + g, g * slots + half * pieces + k)
                    for g in range(ranks)
                    for half in range(2)
                ]
                arrived = lax.ppermute(final[k], ("seq", "beam"), pairs)
                landed = arrived if landed is None else landed + arrived
        back = lax.ppermute(hand, "seq", [(k, k ^ 1) for k in range(1, ranks) if k != 1] + [(0, 1)])
        if direct:
            full = lax.all_gather(landed, "beam", axis=0, tiled=True)
            states, step_out = emit_states(
                full, queries, grow, part, outer, key_rows, shrink, states, step_out, sub, steps, wide, sizes
            )
        columns = pl.BlockSpec((tokens, rows), lambda j, sub=sub: (0, 2 * j + sub))
        out = call(
            functools.partial(output_kernel, sub=sub, **sizes),
            (bits, own, back, prompt_queries, sums, inner) + (() if out is None else (out,)),
            jax.ShapeDtypeStruct((tokens, heads * width), BF16),
            [SMEM] + [VMEM] * 4 + [columns] + ([] if out is None else [pl.BlockSpec(memory_space=pl.ANY)]),
            grid=(2,),
            out_specs=columns,
            input_output_aliases={} if out is None else {6: 0},
        )
    if not direct:
        half = jnp.concatenate([halves[0][0], halves[1][0]])
        other = lax.ppermute(half, "seq", swap)
        first = jnp.where(bits[0] == 0, half, other)
        second = jnp.where(bits[0] == 0, other, half)
        every = lax.all_gather(jnp.concatenate([first, second]), "beam", axis=0, tiled=True)
        full = lax.dynamic_slice_in_dim(every, rank * wide, wide, 0)
        states, step_out = emit_states(
            full, queries, grow, part, outer, key_rows, shrink, None, None, None, steps, wide,
            dict(count=own_heads, width=width)
        )
    return out, step_out.reshape(steps, 1, wide), ranked, states.reshape(1, wide, LANES)


def emit_states(full, queries, grow, part, outer, key_rows, shrink, states, step_out, sub, steps, wide, sizes):
    count, width = sizes["count"], sizes["width"]
    rows = count * width
    at = (lambda j: 0) if sub is None else (lambda j: 2 * j + sub)
    tall = pl.BlockSpec((rows, LANES), lambda j: (at(j), 0))
    flat = lambda height: pl.BlockSpec((height, rows), lambda j: (0, at(j)))
    given = () if states is None else (states, step_out)
    return call(
        functools.partial(decode_kernel, **sizes),
        (full, queries, grow, part, outer, key_rows, shrink) + given,
        (jax.ShapeDtypeStruct((wide, LANES), F32), jax.ShapeDtypeStruct((steps, wide), BF16)),
        [
            pl.BlockSpec((rows, LANES), lambda j: (j, 0)), VMEM, flat(SUB), flat(SUB), flat(SUB), VMEM,
            pl.BlockSpec((count, LANES), lambda j: (at(j), 0)),
        ] + [pl.BlockSpec(memory_space=pl.ANY)] * len(given),
        grid=(1 if sub is None else 2,),
        out_specs=(tall, flat(steps)),
        input_output_aliases={7: 0, 8: 1} if given else {},
    )


def solution(mesh):
    ranks, slots = mesh.shape["seq"], mesh.shape["beam"]
    return jax.shard_map(
        functools.partial(on_device, ranks=ranks, slots=slots),
        mesh=mesh,
        in_specs=(
            P(("groups", "seq"), "beam"),
            P(("groups", "seq"), None),
            P(("groups", "seq"), None),
            P(("groups", "seq"), "beam"),
            P("groups", "beam", "seq"),
            P("groups", "beam", None),
            P("groups", "beam", None),
            P("groups", "beam", "seq"),
            P("groups", "beam"),
            P("groups", "beam"),
            P("groups", "beam"),
            P(("groups", "beam")),
            P(("groups", "beam")),
        ),
        out_specs=(
            P(("groups", "seq"), "beam"),
            P("groups", "beam", "seq"),
            P("groups", "beam"),
            P(("groups", "beam"), "seq", None),
        ),
        check_vma=False,
    )
```

time: 362 us -> 119 us (0.33)
  waiting for transfers between devices: 208 us -> 24.9 us
  other arithmetic: 47.2 us -> 1.46 us
  Pallas kernels: 0 us -> 35.6 us
  between operations: 29.5 us -> 2.19 us
  local copies, waits for them, and re-layouts: 25.3 us -> 9.07 us
  starting transfers between devices: 0.25 us -> 13 us
  matrix products: 9.29 us -> 0 us
  blocking collectives: 36.4 us -> 32.4 us
    all_gather x6 -> x0, waiting for transfers between devices: 208 us -> none  [the longest x4 98.2 us: on_device(): lax.all_gather(state_now[None], 'beam', axis=0, tiled=True)]
    pallas_call x0 -> x12, Pallas kernels: none -> 35.6 us  [call(): pl.pallas_call(body, out_shape=out_shape, in_specs=in_specs, cost_estimat...]
    all_gather x1 -> x3, blocking collectives: 5.59 us -> 32.4 us  [the longest x2 22.3 us: on_device(): full = lax.all_gather(landed, 'beam', axis=0, tiled=True)]
    ppermute x0 -> x10, waiting for transfers between devices: none -> 24.9 us  [the longest x2 15.6 us: on_device(): lax.ppermute(total, 'seq', [(k, k ^ 1 << level) for k in range(ranks)])]
    unnamed x4 -> x0, blocking collectives: 23.7 us -> none
    reduce_sum x11 -> x0, other arithmetic: 20.3 us -> none  [the longest x4 11.5 us: on_device(): jnp.sum(picked[:, None, None, None] * pieces[0], axis=0, keepdims=True)]
    ppermute x0 -> x10, starting transfers between devices: none -> 13 us  [the longest x2 5.27 us: on_device(): lax.ppermute(hand, 'seq', [(k, k ^ 1) for k in range(1, ranks) if k != 1]...]
    unnamed x46 -> x33, local copies, waits for them, and re-layouts: 16.5 us -> 7.15 us
  transfers between devices with their start and end apart: 6 -> 10, of which waited for: 5 -> 2; matrix products, arithmetic and copies ran while one was open for 12% -> 4% of each run, Pallas kernels for 0% -> 21%
where the time goes in v1:
time: 119 us
  Pallas kernels  35.6 us (30%)
  blocking collectives  32.4 us (27%)
  waiting for transfers between devices  24.9 us (21%)
  starting transfers between devices  13 us (11%)
  local copies, waits for them, and re-layouts  9.07 us (8%)
  between operations  2.19 us (2%)
  other arithmetic  1.46 us (1%)
    pallas_call x12, Pallas kernels, call(): pl.pallas_call(body, out_shape=out_shape, in_specs=in_specs, cost_estimat...  35.6 us
    all_gather x2, blocking collectives, on_device(): full = lax.all_gather(landed, 'beam', axis=0, tiled=True)  22.3 us
    ppermute x2, waiting for transfers between devices, on_device(): lax.ppermute(total, 'seq', [(k, k ^ 1 << level) for k in range(ranks)])  15.6 us
    all_gather x1, blocking collectives, on_device(): gathered = lax.all_gather(packed, 'beam', axis=0, tiled=True)  10.1 us
    ppermute x1, waiting for transfers between devices, on_device(): got_a = lax.ppermute(send_a, 'seq', swap)  9.37 us
    unnamed x33, local copies, waits for them, and re-layouts  7.15 us
    ppermute x2, starting transfers between devices, on_device(): lax.ppermute(hand, 'seq', [(k, k ^ 1) for k in range(1, ranks) if k != 1]...  5.27 us
    ppermute x4, starting transfers between devices, on_device(): arrived = lax.ppermute(final[k], ('seq', 'beam'), pairs)  3.91 us
  transfers between devices with their start and end apart: 10, of which 2 were waited for; matrix products, arithmetic and copies ran while one was open for 4% of the time, Pallas kernels for 21%

profile of v1, /device:TPU:25, one launch (start us, length us, event | category | flops | bytes accessed | tf_op | source)
XLA Modules:
  0.0 118.6 jit_solution(6570847571037866192)
XLA Ops:
  0.7 1.5 %copy.25.decay_ref = f32[256,32]{1,0:T(8,128)} copy(f32[256,32]{0,1:T(8,128)} %param.16) | data formatting | bytes 65536 | tf_op args[3]
  2.2 0.6 pad_add_fusion.1.quarter_ref
  2.8 3.6 %shard_map.156 = (f32[256,32]{1,0:T(8,128)}, f32[520,128]{1,0:T(8,128)}) custom-call(s32[4]{0:T(128)} %pad_add_fusion.1.quarter_ref, bf16[256,2048]{1,0:T(8,128)(2,1)} %values_ref.5, bf16[256,128]{1,0:T(8,128)(2,1)} %keys_ref.5, f32[256,32]{1,0:T(8,128)} %copy.25.decay_ref), custom_call_target="tpu_custom_call" | custom-call | flops 1000000 | bytes 1000000 | tf_op jit(solution)/shard_map/pallas_call | solution.py:24
  6.4 4.2 %shard_map.157 = (f32[520,128]{1,0:T(8,128)}, f32[520,128]{1,0:T(8,128)}, f32[520,128]{1,0:T(8,128)}) custom-call(s32[4]{0:T(128)} %pad_add_fusion.1.quarter_ref, bf16[256,2048]{1,0:T(8,128)(2,1)} %values_ref.5, bf16[256,128]{1,0:T(8,128)(2,1)} %keys_ref.5, f32[256,32]{1,0:T(8,128)} %get-tuple-element.27.sums_ref), custom_call_target="tpu_custom_call" | custom-call | flops 1000000 | bytes 1000000 | tf_op jit(solution)/shard_map/pallas_call | solution.py:24
  10.6 0.2 collective-permute-start
  10.8 1.3 %collective-permute-start.3 = (f32[520,128]{1,0:T(8,128)}, f32[520,128]{1,0:T(8,128)S(1)}, u32[]{:S(2)}, u32[]{:S(2)}) collective-permute-start(f32[520,128]{1,0:T(8,128)} %get-tuple-element.33), channel_id=1, source_target_pairs={{0,4},{4,0},{8,12},{12,8},{1,5},{5,1},{9,13},{13,9},{2,6},{6,2},{1... | collective-permute-start | bytes 798728 | tf_op jit(solution)/shard_map/ppermute | solution.py:316
  12.1 0.1 copy.28
  12.2 0.1 copy.27
  12.3 0.1 copy.26
  13.7 0.7 pad_add_fusion.rank_ref
  14.3 0.1 pad_maximum_fusion
  14.4 9.4 %collective-permute-done.3.got_ref.swap_ref = f32[520,128]{1,0:T(8,128)S(1)} collective-permute-done((f32[520,128]{1,0:T(8,128)}, f32[520,128]{1,0:T(8,128)S(1)}, u32[]{:S(2)}, u32[]{:S(2)}) %collective-permute-start.3) | collective-permute-done | bytes 266272 | tf_op jit(solution)/shard_map/ppermute | solution.py:316
  23.8 0.7 copy-done.2
  24.5 1.8 %shard_map.161.total_ref = f32[520,128]{1,0:T(8,128)} custom-call(s32[2]{0:T(128)} %pad_add_fusion.rank_ref, f32[520,128]{1,0:T(8,128)} %get-tuple-element.32.keep_ref, f32[520,128]{1,0:T(8,128)} %copy-done.2), custom_call_target="tpu_custom_call" | custom-call | flops 1000000 | bytes 1000000 | tf_op jit(solution)/shard_map/pallas_call | solution.py:24
  26.3 0.1 collective-permute-start.4
  26.3 0.1 maximum_maximum_fusion
  26.4 0.1 broadcast_in_dim.16
  26.5 0.1 reshape.22
  26.6 0.0 copy-start.1
  26.6 0.7 copy-done.1
  27.3 1.8 %shard_map.158.total_ref = f32[520,128]{1,0:T(8,128)} custom-call(s32[2]{0:T(128)} %pad_add_fusion.rank_ref, f32[520,128]{1,0:T(8,128)} %get-tuple-element.28.keep_ref, f32[520,128]{1,0:T(8,128)} %copy-done.1), custom_call_target="tpu_custom_call" | custom-call | flops 1000000 | bytes 1000000 | tf_op jit(solution)/shard_map/pallas_call | solution.py:24
  29.1 2.3 %collective-permute-start.1 = (f32[520,128]{1,0:T(8,128)}, f32[520,128]{1,0:T(8,128)S(1)}, u32[]{:S(2)}, u32[]{:S(2)}) collective-permute-start(f32[520,128]{1,0:T(8,128)} %shard_map.158.total_ref), channel_id=1, source_target_pairs={{0,8},{4,12},{8,0},{12,4},{1,9},{5,13},{9,1},{13,5},{2,10},{6,14},... | collective-permute-start | bytes 798728 | tf_op jit(solution)/shard_map/ppermute | solution.py:374
  31.4 15.6 %collective-permute-done.4.got_ref = f32[520,128]{1,0:T(8,128)S(1)} collective-permute-done((f32[520,128]{1,0:T(8,128)}, f32[520,128]{1,0:T(8,128)S(1)}, u32[]{:S(2)}, u32[]{:S(2)}) %collective-permute-start.4) | collective-permute-done | bytes 266272 | tf_op jit(solution)/shard_map/ppermute | solution.py:374
  47.0 0.7 copy-done.4
  47.7 2.2 %shard_map.162 = (f32[256,128]{1,0:T(8,128)}, f32[256,128]{1,0:T(8,128)}, f32[512,128]{1,0:T(8,128)}, f32[512,128]{1,0:T(8,128)}) custom-call(s32[2]{0:T(128)} %pad_add_fusion.rank_ref, f32[520,128]{1,0:T(8,128)} %shard_map.161.total_ref, f32[520,128]{1,0:T(8,128)} %copy-done.4, f32[520,128]{1,0:T(8,128)} %get-tuple-element.32.keep_ref, f32[520,128]{1,0:T(8,128)} %copy-done.2), custom_call_target="tpu_custom_call" | custom-call | flops 1000000 | bytes 1000000 | tf_op jit(solution)/shard_map/pallas_call | solution.py:24
  49.9 0.7 collective-permute-start.8
  50.6 1.3 %collective-permute-start.9 = (f32[256,128]{1,0:T(8,128)}, f32[256,128]{1,0:T(8,128)S(1)}, u32[]{:S(2)}, u32[]{:S(2)}) collective-permute-start(f32[256,128]{1,0:T(8,128)} %get-tuple-element.44), channel_id=1, source_target_pairs={{0,1},{4,3},{1,5},{5,7},{10,9},{14,11},{11,13},{15,15},{16,17},{20... | collective-permute-start | bytes 393224 | tf_op jit(solution)/shard_map/ppermute | solution.py:399
  51.9 10.1 %all-gather.1 = f32[4,4,4352]{2,1,0:T(4,128)S(1)} all-gather(f32[1,4,4352]{2,1,0:T(4,128)S(1)} %fusion), channel_id=2, replica_groups=mesh['groups'=2,'seq'=4,'beam'=4] {'beam'}, dimensions={0}, use_global_device_ids=true | all-gather | bytes 348160 | tf_op jit(solution)/shard_map/all_gather | solution.py:339
  62.0 0.3 reshape.27.rows_ref
  62.3 0.6 slice.8
  63.0 0.6 pad.8.queries_ref
  63.6 1.8 %shard_map.165 = (f32[8,2048]{1,0:T(8,128)}, f32[8,2048]{1,0:T(8,128)}, f32[8,2048]{1,0:T(8,128)}, f32[8,128]{1,0:T(8,128)}, f32[32,128]{1,0:T(8,128)}, /*index=5*/f32[4,128]{1,0:T(4,128)}) custom-call(s32[1]{0:T(128)} %bitcast.7.beam_ref, f32[16,128]{1,0:T(8,128)} %bitcast.22, f32[16,1,4352]{2,1,0:T(1,128)} %copy-done, bf16[8,128]{1,0:T(8,128)(2,1)} %pad.8.queries_ref), custom_call_target="tpu_custom_call" | custom-call | flops 1000000 | bytes 1000000 | tf_op jit(solution)/shard_map/pallas_call | solution.py:24
  65.4 1.3 %copy.29 = f32[4,1]{0,1:T(1,128)} copy(f32[4,1]{1,0:T(4,128)} %bitcast.25) | data formatting | bytes 32
  66.6 6.2 %shard_map.160.inner_ref = f32[256,2048]{1,0:T(8,128)} custom-call(bf16[256,2048]{1,0:T(8,128)(2,1)} %values_ref.5, bf16[256,128]{1,0:T(8,128)(2,1)} %keys_ref.5, bf16[256,128]{1,0:T(8,128)(2,1)} %queries_ref.5, f32[256,32]{1,0:T(8,128)} %get-tuple-element.27.sums_ref), custom_call_target="tpu_custom_call" | custom-call | flops 100000000 | bytes 1000000 | tf_op jit(solution)/shard_map/pallas_call | solution.py:24
  72.9 0.7 copy-done.3
  73.6 2.2 %shard_map.159 = (f32[256,128]{1,0:T(8,128)}, f32[256,128]{1,0:T(8,128)}, f32[512,128]{1,0:T(8,128)}, f32[512,128]{1,0:T(8,128)}) custom-call(s32[2]{0:T(128)} %pad_add_fusion.rank_ref, f32[520,128]{1,0:T(8,128)} %shard_map.158.total_ref, f32[520,128]{1,0:T(8,128)} %copy-done.3, f32[520,128]{1,0:T(8,128)} %get-tuple-element.28.keep_ref, f32[520,128]{1,0:T(8,128)} %copy-done.1), custom_call_target="tpu_custom_call" | custom-call | flops 1000000 | bytes 1000000 | tf_op jit(solution)/shard_map/pallas_call | solution.py:24
  75.8 1.9 %collective-permute-start.2 = (f32[512,128]{1,0:T(8,128)}, f32[512,128]{1,0:T(8,128)S(1)}, u32[]{:S(2)}, u32[]{:S(2)}) collective-permute-start(f32[512,128]{1,0:T(8,128)} %get-tuple-element.31), channel_id=1, source_target_pairs={{8,12},{12,8},{0,4},{9,13},{13,9},{1,5},{10,14},{14,10},{2,6},{11,... | collective-permute-start | bytes 786440 | tf_op jit(solution)/shard_map/ppermute | solution.py:401
  77.7 3.4 %collective-permute-start.5 = (f32[512,128]{1,0:T(8,128)S(1)}, f32[512,128]{1,0:T(8,128)S(1)}, u32[]{:S(2)}, u32[]{:S(2)}) collective-permute-start(f32[512,128]{1,0:T(8,128)S(1)} %copy-done.12), channel_id=1, source_target_pairs={{8,12},{12,8},{0,4},{9,13},{13,9},{1,5},{10,14},{14,10},{2,6},{11,... | collective-permute-start | bytes 786440 | tf_op jit(solution)/shard_map/ppermute | solution.py:401
  81.1 0.7 collective-permute-start.6
  81.7 1.3 %collective-permute-start.7 = (f32[256,128]{1,0:T(8,128)}, f32[256,128]{1,0:T(8,128)S(1)}, u32[]{:S(2)}, u32[]{:S(2)}) collective-permute-start(f32[256,128]{1,0:T(8,128)} %get-tuple-element.37), channel_id=1, source_target_pairs={{0,1},{4,3},{1,5},{5,7},{10,9},{14,11},{11,13},{15,15},{16,17},{20... | collective-permute-start | bytes 393224 | tf_op jit(solution)/shard_map/ppermute | solution.py:399
  83.1 14.6 %all_gather.11.final_ref = f32[1024,128]{1,0:T(8,128)} all-gather(f32[256,128]{1,0:T(8,128)S(1)} %add.15), channel_id=1, replica_groups=mesh['groups'=2,'seq'=4,'beam'=4] {'beam'}, dimensions={0}, use_global_device_ids=true | all-gather | bytes 655360 | tf_op jit(solution)/shard_map/all_gather | solution.py:403
  97.7 2.6 %shard_map.166 = (f32[2048,128]{1,0:T(8,128)}, bf16[4,2048]{1,0:T(4,128)(2,1)}) custom-call(f32[1024,128]{1,0:T(8,128)} %all_gather.11.final_ref, bf16[8,128]{1,0:T(8,128)(2,1)} %pad.8.queries_ref, f32[8,2048]{1,0:T(8,128)} %get-tuple-element.38.grow_ref, f32[8,2048]{1,0:T(8,128)} %get-tuple-element.39.part_ref, f32[8,2048]{1,0:T(8,128)} %get-tuple-element.40.outer_ref, ...), custom_call_target="tpu_custom_call" | custom-call | flops 1000000 | bytes 1000000 | tf_op jit(solution)/shard_map/pallas_call | solution.py:24
  100.3 7.7 %all_gather.9.final_ref = f32[1024,128]{1,0:T(8,128)} all-gather(f32[256,128]{1,0:T(8,128)S(1)} %add.14), channel_id=1, replica_groups=mesh['groups'=2,'seq'=4,'beam'=4] {'beam'}, dimensions={0}, use_global_device_ids=true | all-gather | bytes 655360 | tf_op jit(solution)/shard_map/all_gather | solution.py:403
  108.0 2.6 %shard_map.167 = (f32[2048,128]{1,0:T(8,128)}, bf16[4,2048]{1,0:T(4,128)(2,1)}) custom-call(f32[1024,128]{1,0:T(8,128)} %all_gather.9.final_ref, bf16[8,128]{1,0:T(8,128)(2,1)} %pad.8.queries_ref, f32[8,2048]{1,0:T(8,128)} %get-tuple-element.38.grow_ref, f32[8,2048]{1,0:T(8,128)} %get-tuple-element.39.part_ref, ...), custom_call_target="tpu_custom_call", output_to_operand_aliasing={{0}: (7, {}), {1}: (8, {})} | custom-call | flops 1000000 | bytes 1000000 | tf_op jit(solution)/shard_map/pallas_call | solution.py:24
  110.7 0.7 copy-done.6
  111.3 3.3 %shard_map.163.refs_0_ = bf16[256,2048]{1,0:T(8,128)(2,1)} custom-call(s32[2]{0:T(128)} %pad_add_fusion.rank_ref, f32[512,128]{1,0:T(8,128)} %get-tuple-element.34.own_ref, f32[512,128]{1,0:T(8,128)} %copy-done.6, bf16[256,128]{1,0:T(8,128)(2,1)} %queries_ref.5, f32[256,32]{1,0:T(8,128)} %get-tuple-element.27.sums_ref, f32[256,2048]{1,0:T(8,128)} %shard_map.160.inner_ref), custom_call_target="tpu_custom_call" | custom-call | flops 1000000 | bytes 1000000 | tf_op jit(solution)/shard_map/pallas_call | solution.py:24
  114.7 0.7 copy-done.5
  115.4 3.3 %shard_map.164 = bf16[256,2048]{1,0:T(8,128)(2,1)} custom-call(s32[2]{0:T(128)} %pad_add_fusion.rank_ref, f32[512,128]{1,0:T(8,128)} %get-tuple-element.30.own_ref, f32[512,128]{1,0:T(8,128)} %copy-done.5, bf16[256,128]{1,0:T(8,128)(2,1)} %queries_ref.5, f32[256,32]{1,0:T(8,128)} %get-tuple-element.27.sums_ref, ...), custom_call_target="tpu_custom_call", output_to_operand_aliasing={{}: (6, {})} | custom-call | flops 1000000 | bytes 1000000 | tf_op jit(solution)/shard_map/pallas_call | solution.py:24
  (38 shorter events, 0.1 us)
Async XLA Ops:
  0.6 11.4 %copy-start.7 = (bf16[4,1,2048]{2,0,1:T(4,128)(2,1)S(1)}, bf16[4,1,2048]{2,0,1:T(4,128)(2,1)}, u32[]{:S(2)}) copy-start(bf16[4,1,2048]{2,0,1:T(4,128)(2,1)} %param.17) | copy-start | bytes 49156
  0.6 11.4 %copy-start.13 = (s32[4,1]{0,1:T(1,128)S(1)}, s32[4,1]{0,1:T(1,128)}, u32[]{:S(2)}) copy-start(s32[4,1]{0,1:T(1,128)} %param.23) | copy-start | bytes 52
  0.7 11.5 %copy-start.14 = (s32[4,1]{0,1:T(1,128)S(1)}, s32[4,1]{0,1:T(1,128)}, u32[]{:S(2)}) copy-start(s32[4,1]{0,1:T(1,128)} %param.22) | copy-start | bytes 52
  0.7 11.6 %copy-start.11 = (f32[4,1]{0,1:T(1,128)S(1)}, f32[4,1]{0,1:T(1,128)}, u32[]{:S(2)}) copy-start(f32[4,1]{0,1:T(1,128)} %param.21) | copy-start | bytes 52
  0.7 25.7 %copy-start.8 = (f32[4,1,32]{2,1,0:T(1,128)S(1)}, f32[4,1,32]{2,1,0:T(1,128)}, u32[]{:S(2)}) copy-start(f32[4,1,32]{2,1,0:T(1,128)} %param.20) | copy-start | bytes 1540
  0.7 25.9 %copy-start.9 = (bf16[4,1,128]{2,0,1:T(4,128)(2,1)S(1)}, bf16[4,1,128]{2,0,1:T(4,128)(2,1)}, u32[]{:S(2)}) copy-start(bf16[4,1,128]{2,0,1:T(4,128)(2,1)} %param.18) | copy-start | bytes 3076
  10.6 52.4 %copy-start.10 = (bf16[4,1,128]{2,0,1:T(4,128)(2,1)S(1)}, bf16[4,1,128]{2,0,1:T(4,128)(2,1)}, u32[]{:S(2)}) copy-start(bf16[4,1,128]{2,0,1:T(4,128)(2,1)} %param.19) | copy-start | bytes 3076
  10.6 16.0 %collective-permute-start = (f32[520,128]{1,0:T(8,128)}, f32[520,128]{1,0:T(8,128)S(1)}, u32[]{:S(2)}, u32[]{:S(2)}) collective-permute-start(f32[520,128]{1,0:T(8,128)} %get-tuple-element.29), channel_id=1, source_target_pairs={{0,4},{4,0},{8,12},{12,8},{1,5},{5,1},{9,13},{13,9},{2,6},{6,2},{1... | collective-permute-start | bytes 798728 | tf_op jit(solution)/shard_map/ppermute | solution.py:323
  10.8 13.0 %collective-permute-start.3 = (f32[520,128]{1,0:T(8,128)}, f32[520,128]{1,0:T(8,128)S(1)}, u32[]{:S(2)}, u32[]{:S(2)}) collective-permute-start(f32[520,128]{1,0:T(8,128)} %get-tuple-element.33), channel_id=1, source_target_pairs={{0,4},{4,0},{8,12},{12,8},{1,5},{5,1},{9,13},{13,9},{2,6},{6,2},{1... | collective-permute-start | bytes 798728 | tf_op jit(solution)/shard_map/ppermute | solution.py:316
  23.8 0.7 copy-start.2
  26.3 20.7 %collective-permute-start.4 = (f32[520,128]{1,0:T(8,128)}, f32[520,128]{1,0:T(8,128)S(1)}, u32[]{:S(2)}, u32[]{:S(2)}) collective-permute-start(f32[520,128]{1,0:T(8,128)} %shard_map.161.total_ref), channel_id=1, source_target_pairs={{0,8},{4,12},{8,0},{12,4},{1,9},{5,13},{9,1},{13,5},{2,10},{6,14},... | collective-permute-start | bytes 798728 | tf_op jit(solution)/shard_map/ppermute | solution.py:374
  26.6 0.7 copy-start.1
  29.1 43.7 %collective-permute-start.1 = (f32[520,128]{1,0:T(8,128)}, f32[520,128]{1,0:T(8,128)S(1)}, u32[]{:S(2)}, u32[]{:S(2)}) collective-permute-start(f32[520,128]{1,0:T(8,128)} %shard_map.158.total_ref), channel_id=1, source_target_pairs={{0,8},{4,12},{8,0},{12,4},{1,9},{5,13},{9,1},{13,5},{2,10},{6,14},... | collective-permute-start | bytes 798728 | tf_op jit(solution)/shard_map/ppermute | solution.py:374
  47.0 0.7 copy-start.4
  49.9 31.8 %collective-permute-start.8 = (f32[256,128]{1,0:T(8,128)}, f32[256,128]{1,0:T(8,128)S(1)}, u32[]{:S(2)}, u32[]{:S(2)}) collective-permute-start(f32[256,128]{1,0:T(8,128)} %get-tuple-element.43), channel_id=1, source_target_pairs={{0,0},{4,2},{1,4},{5,6},{10,8},{14,10},{11,12},{15,14},{16,16},{20... | collective-permute-start | bytes 393224 | tf_op jit(solution)/shard_map/ppermute | solution.py:399
  50.6 32.5 %collective-permute-start.9 = (f32[256,128]{1,0:T(8,128)}, f32[256,128]{1,0:T(8,128)S(1)}, u32[]{:S(2)}, u32[]{:S(2)}) collective-permute-start(f32[256,128]{1,0:T(8,128)} %get-tuple-element.44), channel_id=1, source_target_pairs={{0,1},{4,3},{1,5},{5,7},{10,9},{14,11},{11,13},{15,15},{16,17},{20... | collective-permute-start | bytes 393224 | tf_op jit(solution)/shard_map/ppermute | solution.py:399
  62.3 1.2 %copy-start = (f32[16,1,4352]{2,1,0:T(1,128)}, f32[16,1,4352]{2,1,0:T(1,128)S(1)}, u32[]{:S(2)}) copy-start(f32[16,1,4352]{2,1,0:T(1,128)S(1)} %reshape.27.rows_ref) | copy-start | bytes 835588
  66.6 11.0 %copy-start.12 = (f32[512,128]{1,0:T(8,128)S(1)}, f32[512,128]{1,0:T(8,128)}, u32[]{:S(2)}) copy-start(f32[512,128]{1,0:T(8,128)} %get-tuple-element.35) | copy-start | bytes 786436
  72.9 0.7 copy-start.3
  75.8 38.9 %collective-permute-start.2 = (f32[512,128]{1,0:T(8,128)}, f32[512,128]{1,0:T(8,128)S(1)}, u32[]{:S(2)}, u32[]{:S(2)}) collective-permute-start(f32[512,128]{1,0:T(8,128)} %get-tuple-element.31), channel_id=1, source_target_pairs={{8,12},{12,8},{0,4},{9,13},{13,9},{1,5},{10,14},{14,10},{2,6},{11,... | collective-permute-start | bytes 786440 | tf_op jit(solution)/shard_map/ppermute | solution.py:401
  77.7 33.0 %collective-permute-start.5 = (f32[512,128]{1,0:T(8,128)S(1)}, f32[512,128]{1,0:T(8,128)S(1)}, u32[]{:S(2)}, u32[]{:S(2)}) collective-permute-start(f32[512,128]{1,0:T(8,128)S(1)} %copy-done.12), channel_id=1, source_target_pairs={{8,12},{12,8},{0,4},{9,13},{13,9},{1,5},{10,14},{14,10},{2,6},{11,... | collective-permute-start | bytes 786440 | tf_op jit(solution)/shard_map/ppermute | solution.py:401
  81.1 16.6 %collective-permute-start.6 = (f32[256,128]{1,0:T(8,128)}, f32[256,128]{1,0:T(8,128)S(1)}, u32[]{:S(2)}, u32[]{:S(2)}) collective-permute-start(f32[256,128]{1,0:T(8,128)} %get-tuple-element.36), channel_id=1, source_target_pairs={{0,0},{4,2},{1,4},{5,6},{10,8},{14,10},{11,12},{15,14},{16,16},{20... | collective-permute-start | bytes 393224 | tf_op jit(solution)/shard_map/ppermute | solution.py:399
  81.7 15.9 %collective-permute-start.7 = (f32[256,128]{1,0:T(8,128)}, f32[256,128]{1,0:T(8,128)S(1)}, u32[]{:S(2)}, u32[]{:S(2)}) collective-permute-start(f32[256,128]{1,0:T(8,128)} %get-tuple-element.37), channel_id=1, source_target_pairs={{0,1},{4,3},{1,5},{5,7},{10,9},{14,11},{11,13},{15,15},{16,17},{20... | collective-permute-start | bytes 393224 | tf_op jit(solution)/shard_map/ppermute | solution.py:399
  110.6 0.7 copy-start.6
  114.7 0.7 copy-start.5

commit v2 on v1

v2 whole, which is shorter than its diff:
```python
import functools

import jax
import jax.numpy as jnp
from jax import lax
from jax.experimental import pallas as pl
from jax.experimental.pallas import tpu as pltpu
from jax.sharding import PartitionSpec as P


LANES = 128
SUB = 8
QUARTERS = 4
F32 = jnp.float32
BF16 = jnp.bfloat16
HIGH = lax.Precision.HIGHEST
TN = (((0,), (0,)), ((), ()))
NT = (((1,), (1,)), ((), ()))

VMEM = pl.BlockSpec(memory_space=pltpu.VMEM)
HBM = pl.BlockSpec(memory_space=pltpu.HBM)
SMEM = pl.BlockSpec(memory_space=pltpu.SMEM)


def call(body, args, out_shape, in_specs=None, flops=1_000_000, **kwargs):
    return pl.pallas_call(
        body,
        out_shape=out_shape,
        in_specs=in_specs,
        cost_estimate=pl.CostEstimate(flops=flops, bytes_accessed=1_000_000, transcendentals=0),
        compiler_params=pltpu.CompilerParams(vmem_limit_bytes=8 * 2**20),
        **kwargs,
    )(*args)


def gather(array):
    return lax.all_gather(array, "beam", axis=0, tiled=True)


def iota(shape, axis):
    return lax.broadcasted_iota(jnp.int32, shape, axis)


def head_lanes(heads, first, count, width):
    shape = (heads, count * width)
    return (iota(shape, 0) == first + iota(shape, 1) // width).astype(F32)


def quarter_state(values, keys, sums, first, count, width, out_ref):
    heads = sums.shape[1]
    last = sums[-1:, :]
    tail = jnp.dot(jnp.exp(last - sums), head_lanes(heads, first, count, width), precision=HIGH, preferred_element_type=F32)
    scaled = (values.astype(F32) * tail).astype(BF16)
    rows = count * width
    out_ref[0:rows, :] = lax.dot_general(scaled, keys, TN, preferred_element_type=F32)
    pad = out_ref.shape[0] - rows
    pick = iota((pad, heads), 1) == first + iota((pad, heads), 0)
    total = jnp.sum(jnp.where(pick, last, 0.0), axis=1, keepdims=True)
    out_ref[rows:, :] = jnp.broadcast_to(jnp.exp(total), (pad, LANES))


def rank_bit(k):
    return (lax.axis_index("seq") >> k) & 1


def quarter_at(place):
    return ((place // 2) ^ 1 ^ rank_bit(0)) * 2 + place % 2


def fetch(arrived, *pairs):
    copies = [pltpu.make_async_copy(source, target, arrived.at[k]) for k, (source, target) in enumerate(pairs)]
    for copy in copies:
        copy.start()
    return copies


def first_kernel(values_hbm, keys_hbm, decay_hbm, sums_ref, turned_ref, out_ref, values, keys, decay, arrived, *, count, width):
    tokens = decay.shape[1]
    lanes = count * width
    quarter = quarter_at(0)
    columns = values_hbm.at[:, pl.ds(pl.multiple_of(quarter * lanes, lanes), lanes)]
    copies = fetch(arrived, (decay_hbm, decay), (columns, values), (keys_hbm, keys))
    copies[0].wait()
    upper = (iota((tokens, tokens), 0) <= iota((tokens, tokens), 1)).astype(F32)
    turned = jnp.dot(decay[...], upper, precision=HIGH, preferred_element_type=F32)
    turned_ref[...] = turned
    sums = turned.T
    sums_ref[...] = sums
    for copy in copies[1:]:
        copy.wait()
    quarter_state(values[...], keys[...], sums, quarter * count, count, width, out_ref)


def rest_kernel(values_hbm, keys_hbm, sums_ref, *refs, count, width):
    *out_refs, values_ref, keys_ref, arrived = refs
    lanes = count * width
    for copy in fetch(arrived, (values_hbm, values_ref), (keys_hbm, keys_ref)):
        copy.wait()
    for k, out_ref in enumerate(out_refs):
        quarter = quarter_at(k + 1)
        values = values_ref[:, pl.ds(pl.multiple_of(quarter * lanes, lanes), lanes)]
        quarter_state(values, keys_ref[...], sums_ref[...], quarter * count, count, width, out_ref)


def inner_kernel(
    values_hbm, keys_hbm, queries_hbm, sums_ref, turned_ref, out_ref, grown_ref,
    values_ref, keys_ref, queries_ref, wide_ref, arrived, *, count, width
):
    copies = fetch(arrived, (keys_hbm, keys_ref), (queries_hbm, queries_ref), (values_hbm, values_ref))
    tokens, heads = sums_ref.shape
    half = tokens // 2
    wide_ref[...] = jnp.zeros_like(wide_ref)
    wide_ref[:, 0:heads] = sums_ref[...]
    for copy in copies:
        copy.wait()
    scores = lax.dot_general(queries_ref[...], keys_ref[...], NT, preferred_element_type=F32)
    lower = iota((half, half), 0) >= iota((half, half), 1)
    top = jnp.where(lower, scores[:half, :half], 0.0)
    left = scores[half:, :half]
    bottom = jnp.where(lower, scores[half:, half:], 0.0)
    per_store = LANES // width
    lane = iota((tokens, LANES), 1) // width

    def group(g, carry):
        wide = pltpu.roll(wide_ref[...], lax.rem(LANES - g * count, LANES), 1)
        for k in range(count // per_store):
            place = pl.ds(pl.multiple_of((g * count + k * per_store) * width, LANES), LANES)
            values = values_ref[:, place]
            tops, bottoms = [], []
            grown = wide[:, k * per_store : k * per_store + 1]
            for m in range(1, per_store):
                grown = jnp.where(lane == m, wide[:, k * per_store + m : k * per_store + m + 1], grown)
            grown_ref[:, place] = jnp.exp(jnp.broadcast_to(grown, (tokens, LANES)))
            for m in range(per_store):
                h = k * per_store + m
                column = wide[:, h : h + 1]
                row = turned_ref[pl.ds(g * count + h, 1), :]
                x = values[:, m * width : (m + 1) * width]
                w0 = (top * jnp.exp(jnp.minimum(column[:half] - row[:, :half], 0.0))).astype(BF16)
                w1 = (left * jnp.exp(column[half:] - row[:, :half])).astype(BF16)
                w2 = (bottom * jnp.exp(jnp.minimum(column[half:] - row[:, half:], 0.0))).astype(BF16)
                tops.append(jnp.dot(w0, x[:half], preferred_element_type=F32))
                bottoms.append(jnp.dot(jnp.concatenate([w1, w2], axis=1), x, preferred_element_type=F32))
            out_ref[0:half, place] = jnp.concatenate(tops, axis=1)
            out_ref[half:, place] = jnp.concatenate(bottoms, axis=1)
        return carry

    lax.fori_loop(0, heads // count, group, 0)


def combine(low, high, out, count, width, decay=True):
    rows = count * width
    for h in range(count):
        place = slice(h * width, (h + 1) * width)
        out[place, :] = high[rows + h : rows + h + 1, :] * low[place, :] + high[place, :]
    if decay:
        out[rows:, :] = low[rows:, :] * high[rows:, :]


def pair_kernel(keep_ref, got_ref, out_ref, *, count, width):
    odd = rank_bit(0) == 1

    @pl.when(odd)
    def _():
        combine(got_ref, keep_ref, out_ref, count, width)

    @pl.when(jnp.logical_not(odd))
    def _():
        combine(keep_ref, got_ref, out_ref, count, width)


def round_kernel(total_ref, got_ref, *refs, bit, first, count, width):
    before_ref, refs = (None, refs) if first else (refs[0], refs[1:])
    before_out, total_out = refs
    upper = rank_bit(bit) == 1
    rows = count * width

    @pl.when(upper)
    def _():
        combine(got_ref, total_ref, total_out, count, width)
        if first:
            before_out[...] = got_ref[...]
        else:
            combine(got_ref, before_ref, before_out, count, width)

    @pl.when(jnp.logical_not(upper))
    def _():
        combine(total_ref, got_ref, total_out, count, width)
        if first:
            before_out[0:rows, :] = jnp.zeros((rows, LANES), F32)
            before_out[rows:, :] = jnp.ones((before_out.shape[0] - rows, LANES), F32)
        else:
            before_out[...] = before_ref[...]


def last_kernel(total_ref, got_ref, keep_ref, swap_ref, *refs, bit, first, pieces, count, width):
    before_ref, refs = (None, refs) if first else (refs[0], refs[1:])
    piece_refs, own_ref, hand_ref, before_now = refs[:pieces], refs[pieces], refs[pieces + 1], refs[pieces + 2]
    upper = rank_bit(bit) == 1
    odd = rank_bit(0) == 1
    rows = count * width
    per_piece = count // pieces

    def final(low, high):
        for h in range(count):
            place = slice(h * width, (h + 1) * width)
            start = (h % per_piece) * width
            piece_refs[h // per_piece][start : start + width, :] = (
                high[rows + h : rows + h + 1, :] * low[place, :] + high[place, :]
            )

    @pl.when(upper)
    def _():
        final(got_ref, total_ref)
        if first:
            before_now[...] = got_ref[0:rows, :]
        else:
            combine(got_ref, before_ref, before_now, count, width, decay=False)

    @pl.when(jnp.logical_not(upper))
    def _():
        final(total_ref, got_ref)
        before_now[...] = jnp.zeros_like(before_now) if first else before_ref[0:rows, :]

    @pl.when(odd)
    def _():
        combine(before_now, swap_ref, own_ref, count, width, decay=False)
        hand_ref[...] = before_now[...]

    @pl.when(jnp.logical_not(odd))
    def _():
        own_ref[...] = before_now[...]
        combine(before_now, keep_ref, hand_ref, count, width, decay=False)


def output_kernel(own_ref, other_ref, queries_ref, grown_ref, inner_ref, *refs):
    out_ref = refs[-1]

    def emit(state_ref):
        carried = lax.dot_general(queries_ref[...], state_ref[...].astype(BF16), NT, preferred_element_type=F32)
        out_ref[...] = (inner_ref[...] + carried * grown_ref[...]).astype(BF16)

    mine = rank_bit(0) == pl.program_id(0)

    @pl.when(mine)
    def _():
        emit(own_ref)

    @pl.when(jnp.logical_not(mine))
    def _():
        emit(other_ref)


def pack_kernel(values_ref, decay_ref, keys_ref, scalar_ref, tail_ref, out_ref, *, width):
    steps, wide = values_ref.shape
    heads = decay_ref.shape[1]
    out_ref[0, :, 0:wide] = values_ref[...].astype(F32)
    out_ref[0, :, wide : 2 * wide] = jnp.dot(
        decay_ref[...], head_lanes(heads, 0, heads, width), precision=HIGH, preferred_element_type=F32
    )
    out_ref[0, :, 2 * wide : 2 * wide + LANES] = keys_ref[...].astype(F32)
    lane, line = iota((steps, LANES), 1), iota((steps, LANES), 0)
    row = jnp.zeros((steps, LANES), F32)
    for step in range(steps):
        for k in range(scalar_ref.shape[0]):
            row = jnp.where((lane == k) & (line == step), scalar_ref[k, step], row)
    for k in range(tail_ref.shape[0]):
        row = jnp.where(lane == scalar_ref.shape[0] + k, tail_ref[k], row)
    out_ref[0, :, 2 * wide + LANES :] = row


def join_kernel(*refs):
    *parts, out_ref = refs
    out_ref[...] = functools.reduce(lambda a, b: a + b, [part[...] for part in parts])


def lineage_kernel(
    rows_ref, queries_ref, grow_ref, part_ref, fresh_ref, shrink_ref, ranked_ref,
    outer_ref, key_ref, scores, counts, scalar_ref, arrived, *, slots, steps, wide, width
):
    (copy,) = fetch(arrived, (rows_ref.at[:, :, pl.ds(2 * wide + LANES, LANES)], scalar_ref))
    copy.wait()
    me = lax.axis_index("beam")
    ranks_row = jnp.zeros((1, LANES), F32)
    done = lambda slot, step: scalar_ref[slot, step, 2]
    parent = lambda slot, step: scalar_ref[slot, step, 1].astype(jnp.int32)
    for slot in range(slots):
        scores[0, slot] = scalar_ref[slot, 0, 4]
        counts[0, slot] = scalar_ref[slot, 0, 3]
    lane = iota((1, LANES), 1)
    for step in range(steps):
        score_row = jnp.zeros((1, LANES), F32)
        count_row = jnp.zeros((1, LANES), F32)
        for slot in range(slots):
            source = parent(slot, step)
            live = 1.0 - done(slot, step)
            score = scores[step, source] + live * scalar_ref[slot, step, 0]
            tally = counts[step, source] + live
            scores[step + 1, slot] = score
            counts[step + 1, slot] = tally
            score_row = jnp.where(lane == slot, score, score_row)
            count_row = jnp.where(lane == slot, tally, count_row)
        normed = score_row * jnp.exp(-0.6 * jnp.log((5.0 + count_row) / 6.0))
        best = jnp.max(jnp.where(lane < slots, normed, -jnp.inf), axis=1, keepdims=True)
        mine = jnp.sum(jnp.where(lane == me, normed, 0.0), axis=1, keepdims=True)
        ranks_row = jnp.where(lane == step, mine - best, ranks_row)
    ranked_ref[...] = ranks_row[:, 0:steps]

    for ref in (grow_ref, part_ref, outer_ref, key_ref):
        ref[...] = jnp.zeros_like(ref)
    for step in range(steps):
        slot = me
        factor = jnp.ones((1, wide), F32)
        part = jnp.zeros((1, wide), F32)
        query = queries_ref[step : step + 1, :].astype(F32)
        live_now = 1.0 - done(me, step)
        for back in range(step, -1, -1):
            record = rows_ref[slot, back : back + 1, :]
            live = 1.0 - done(slot, back)
            values = record[:, 0:wide]
            key = record[:, 2 * wide : 2 * wide + LANES]
            weight = factor * (values * live)
            part = part + weight * jnp.sum(key * query, axis=1, keepdims=True)
            if step == steps - 1:
                outer_ref[back : back + 1, :] = weight
                key_ref[back : back + 1, :] = key
            factor = factor * jnp.exp(record[:, wide : 2 * wide] * live)
            slot = parent(slot, back)
        grow_ref[step : step + 1, :] = factor * live_now
        part_ref[step : step + 1, :] = part * live_now
        if step == steps - 1:
            fresh_ref[...] = lax.dot_general(outer_ref[...], key_ref[...], TN, precision=HIGH, preferred_element_type=F32)
            count = shrink_ref.shape[0]
            pick = iota((count, wide), 1) == iota((count, wide), 0) * width
            shrink_ref[...] = jnp.broadcast_to(
                jnp.sum(jnp.where(pick, factor, 0.0), axis=1, keepdims=True), (count, LANES)
            )


def decode_kernel(final_ref, queries_ref, grow_ref, part_ref, fresh_ref, shrink_ref, *refs, count, width):
    state_ref, out_ref = refs[-2:]
    final = final_ref[...]
    product = lax.dot_general(queries_ref[...], final.astype(BF16), NT, preferred_element_type=F32)
    steps = out_ref.shape[0]
    out_ref[...] = (grow_ref[0:steps, :] * product[0:steps, :] + part_ref[0:steps, :]).astype(BF16)
    for h in range(count):
        place = slice(h * width, (h + 1) * width)
        state_ref[place, :] = shrink_ref[h : h + 1, :] * final[place, :] + fresh_ref[place, :]


def on_device(
    prompt_values, prompt_keys, prompt_queries, logarithm_state_decay, step_values, step_keys, step_queries, step_decay,
    step_logprob, parents, finished, lengths, init_score, *, ranks, slots
):
    tokens, heads = logarithm_state_decay.shape
    width = prompt_values.shape[1] // heads
    steps = step_values.shape[0]
    wide = step_values.shape[2]
    own_heads = wide // width
    count = heads // QUARTERS
    rows = count * width
    message = jax.ShapeDtypeStruct((rows + -(-count // SUB) * SUB, LANES), F32)
    state = jax.ShapeDtypeStruct((rows, LANES), F32)
    sizes = dict(count=count, width=width)
    levels = ranks.bit_length() - 1
    rank = lax.axis_index("seq")

    turned_shape = jax.ShapeDtypeStruct((heads, tokens), F32)
    sums, turned, send_a = call(
        functools.partial(first_kernel, **sizes),
        (prompt_values, prompt_keys, logarithm_state_decay.T),
        (jax.ShapeDtypeStruct((tokens, heads), F32), turned_shape, message),
        [HBM] * 3,
        scratch_shapes=[
            pltpu.VMEM((tokens, count * width), BF16),
            pltpu.VMEM((tokens, LANES), BF16),
            pltpu.VMEM((heads, tokens), F32),
            pltpu.SemaphoreType.DMA((3,)),
        ],
    )
    swap = [(k, k ^ 1) for k in range(ranks)]
    got_a = lax.ppermute(send_a, "seq", swap)
    send_b, keep_a, keep_b = call(
        functools.partial(rest_kernel, **sizes),
        (prompt_values, prompt_keys, sums),
        (message,) * 3,
        [HBM, HBM, VMEM],
        scratch_shapes=[
            pltpu.VMEM(prompt_values.shape, BF16), pltpu.VMEM((tokens, LANES), BF16), pltpu.SemaphoreType.DMA((2,))
        ],
    )
    got_b = lax.ppermute(send_b, "seq", swap)
    keeps, swaps = (keep_a, keep_b), (got_a, got_b)

    scalars = jnp.concatenate([step_logprob.T, parents.T.astype(F32), finished.T.astype(F32)])
    packed = call(
        functools.partial(pack_kernel, width=width),
        (step_values[:, 0], step_decay[:, 0], step_keys[:, 0], scalars, jnp.concatenate([lengths.astype(F32), init_score])),
        jax.ShapeDtypeStruct((1, steps, 2 * wide + 2 * LANES), F32),
        [VMEM, VMEM, VMEM, SMEM, SMEM],
    )
    gathered = gather(packed)
    queries = step_queries[:, 0]
    line = jax.ShapeDtypeStruct((SUB, wide), F32)
    grow, part, fresh, shrink, ranked = call(
        functools.partial(lineage_kernel, slots=slots, steps=steps, wide=wide, width=width),
        (gathered, queries),
        (
            line, line, jax.ShapeDtypeStruct((wide, LANES), F32), jax.ShapeDtypeStruct((own_heads, LANES), F32),
            jax.ShapeDtypeStruct((1, steps), F32),
        ),
        [VMEM, VMEM],
        scratch_shapes=[
            pltpu.VMEM((SUB, wide), F32), pltpu.VMEM((SUB, LANES), F32),
            pltpu.SMEM((steps + 1, slots), F32), pltpu.SMEM((steps + 1, slots), F32),
            pltpu.SMEM((slots, steps, LANES), F32), pltpu.SemaphoreType.DMA((1,)),
        ],
    )
    ranked = ranked.reshape(steps, 1)

    inner, grown = call(
        functools.partial(inner_kernel, **sizes),
        (prompt_values, prompt_keys, prompt_queries, sums, turned),
        (jax.ShapeDtypeStruct((tokens, heads * width), F32),) * 2,
        [HBM, HBM, HBM, VMEM, VMEM],
        scratch_shapes=[
            pltpu.VMEM(prompt_values.shape, BF16), pltpu.VMEM((tokens, LANES), BF16), pltpu.VMEM((tokens, LANES), BF16),
            pltpu.VMEM((tokens, LANES), F32), pltpu.SemaphoreType.DMA((3,)),
        ],
        flops=100_000_000,
    )

    direct = ranks == slots
    pieces = slots // 2 if direct else 1
    piece = jax.ShapeDtypeStruct((rows // pieces, LANES), F32)
    out = states = step_out = None
    halves = []
    for sub in range(2):
        total = call(functools.partial(pair_kernel, **sizes), (keeps[sub], swaps[sub]), message, [VMEM] * 2)
        before = ()
        for level in range(1, levels):
            got = lax.ppermute(total, "seq", [(k, k ^ (1 << level)) for k in range(ranks)])
            if level < levels - 1:
                before_now, total = call(
                    functools.partial(round_kernel, bit=level, first=level == 1, **sizes),
                    (total, got) + before,
                    (message, message),
                    [VMEM] * (2 + len(before)),
                )
                before = (before_now,)
        *final, own, hand = call(
            functools.partial(last_kernel, bit=levels - 1, first=levels == 2, pieces=pieces, **sizes),
            (total, got, keeps[sub], swaps[sub]) + before,
            (piece,) * pieces + (state, state),
            [VMEM] * (4 + len(before)),
            scratch_shapes=[pltpu.VMEM((rows, LANES), F32)],
        )
        halves.append(final)
        if direct:
            landed = []
            for k in range(pieces):
                pairs = [
                    ((g // 2 * 2 + half) * slots + g, g * slots + half * pieces + k)
                    for g in range(ranks)
                    for half in range(2)
                ]
                landed.append(lax.ppermute(final[k], ("seq", "beam"), pairs))
            landed = call(join_kernel, landed, piece, [VMEM] * pieces)
        back = lax.ppermute(hand, "seq", [(k, k ^ 1) for k in range(1, ranks) if k != 1] + [(0, 1)])
        if direct:
            full = gather(landed)
            states, step_out = emit_states(
                full, queries, grow, part, fresh, shrink, states, step_out, sub, steps, wide, sizes
            )
        columns = pl.BlockSpec((tokens, rows), lambda j, sub=sub: (0, 2 * j + sub))
        out = call(
            output_kernel,
            (own, back, prompt_queries, grown, inner) + (() if out is None else (out,)),
            jax.ShapeDtypeStruct((tokens, heads * width), BF16),
            [VMEM] * 3 + [columns] * 2 + ([] if out is None else [pl.BlockSpec(memory_space=pl.ANY)]),
            grid=(2,),
            out_specs=columns,
            input_output_aliases={} if out is None else {5: 0},
        )
    if not direct:
        half = jnp.concatenate([halves[0][0], halves[1][0]])
        other = lax.ppermute(half, "seq", swap)
        odd = rank_bit(0) == 1
        first, second = jnp.where(odd, other, half), jnp.where(odd, half, other)
        every = lax.all_gather(jnp.concatenate([first, second]), "beam", axis=0, tiled=True)
        full = lax.dynamic_slice_in_dim(every, rank * wide, wide, 0)
        states, step_out = emit_states(
            full, queries, grow, part, fresh, shrink, None, None, None, steps, wide,
            dict(count=own_heads, width=width)
        )
    return out, step_out.reshape(steps, 1, wide), ranked, states.reshape(1, wide, LANES)


def emit_states(full, queries, grow, part, fresh, shrink, states, step_out, sub, steps, wide, sizes):
    count, width = sizes["count"], sizes["width"]
    rows = count * width
    at = (lambda j: 0) if sub is None else (lambda j: 2 * j + sub)
    tall = pl.BlockSpec((rows, LANES), lambda j: (at(j), 0))
    flat = lambda height: pl.BlockSpec((height, rows), lambda j: (0, at(j)))
    given = () if states is None else (states, step_out)
    return call(
        functools.partial(decode_kernel, **sizes),
        (full, queries, grow, part, fresh, shrink) + given,
        (jax.ShapeDtypeStruct((wide, LANES), F32), jax.ShapeDtypeStruct((steps, wide), BF16)),
        [
            pl.BlockSpec((rows, LANES), lambda j: (j, 0)), VMEM, flat(SUB), flat(SUB), tall,
            pl.BlockSpec((count, LANES), lambda j: (at(j), 0)),
        ] + [pl.BlockSpec(memory_space=pl.ANY)] * len(given),
        grid=(1 if sub is None else 2,),
        out_specs=(tall, flat(steps)),
        input_output_aliases={6: 0, 7: 1} if given else {},
    )


def solution(mesh):
    ranks, slots = mesh.shape["seq"], mesh.shape["beam"]

    def body(*args):
        return on_device(*args, ranks=ranks, slots=slots)

    return jax.shard_map(
        body,
        mesh=mesh,
        in_specs=(
            P(("groups", "seq"), "beam"),
            P(("groups", "seq"), None),
            P(("groups", "seq"), None),
            P(("groups", "seq"), "beam"),
            P("groups", "beam", "seq"),
            P("groups", "beam", None),
            P("groups", "beam", None),
            P("groups", "beam", "seq"),
            P("groups", "beam"),
            P("groups", "beam"),
            P("groups", "beam"),
            P(("groups", "beam")),
            P(("groups", "beam")),
        ),
        out_specs=(
            P(("groups", "seq"), "beam"),
            P("groups", "beam", "seq"),
            P("groups", "beam"),
            P(("groups", "beam"), "seq", None),
        ),
        check_vma=False,
    )
```

time: 119 us -> 88.3 us (0.74)
  Pallas kernels: 35.6 us -> 15.6 us
  local copies, waits for them, and re-layouts: 9.07 us -> 2.88 us
  waiting for transfers between devices: 24.9 us -> 20 us
  blocking collectives: 32.4 us -> 35.8 us
  starting transfers between devices: 13 us -> 11.3 us
  other arithmetic: 1.46 us -> 0.09 us
    pallas_call x12 -> x15, Pallas kernels: 35.6 us -> 15.6 us  [call(): pl.pallas_call(body, out_shape=out_shape, in_specs=in_specs, cost_estimat...]
    ppermute x1, waiting for transfers between devices: 0.01 us -> 8.47 us  [on_device(): got_b = lax.ppermute(send_b, 'seq', swap)]
    ppermute x2, waiting for transfers between devices: 15.6 us -> 8.13 us  [on_device(): lax.ppermute(total, 'seq', [(k, k ^ 1 << level) for k in range(ranks)])]
    ppermute x1, waiting for transfers between devices: 9.37 us -> 3.43 us  [on_device(): got_a = lax.ppermute(send_a, 'seq', swap)]
    unnamed x33 -> x26, local copies, waits for them, and re-layouts: 7.15 us -> 2.88 us
    all_gather x3, blocking collectives: 32.4 us -> 35.8 us  [gather(): return lax.all_gather(array, 'beam', axis=0, tiled=True)]
    ppermute x2, starting transfers between devices: 2.36 us -> 0.48 us  [on_device(): lax.ppermute(total, 'seq', [(k, k ^ 1 << level) for k in range(ranks)])]
    another operation x2 -> x0, other arithmetic: 1.24 us -> none  [the longest x1 0.65 us: on_device(): bits = jnp.stack([rank >> k & 1 for k in range(levels)]).astype(jnp.int32)]
  transfers between devices with their start and end apart: 10 -> 10, of which waited for: 2 -> 3; matrix products, arithmetic and copies ran while one was open for 4% -> 0% of each run, Pallas kernels for 21% -> 15%
where the time goes in v2:
time: 88.3 us; the launch traced here: 87.9 us
  blocking collectives  35.8 us (41%)
  waiting for transfers between devices  20 us (23%)
  Pallas kernels  15.6 us (18%)
  starting transfers between devices  11.3 us (13%)
  local copies, waits for them, and re-layouts  2.88 us (3%)
  between operations  2.18 us (2%)
    all_gather x3, blocking collectives, gather(): return lax.all_gather(array, 'beam', axis=0, tiled=True)  35.8 us
    pallas_call x15, Pallas kernels, call(): pl.pallas_call(body, out_shape=out_shape, in_specs=in_specs, cost_estimat...  15.6 us
    ppermute x1, waiting for transfers between devices, on_device(): got_b = lax.ppermute(send_b, 'seq', swap)  8.47 us
    ppermute x2, waiting for transfers between devices, on_device(): lax.ppermute(total, 'seq', [(k, k ^ 1 << level) for k in range(ranks)])  8.13 us
    ppermute x2, starting transfers between devices, on_device(): lax.ppermute(hand, 'seq', [(k, k ^ 1) for k in range(1, ranks) if k != 1]...  5.28 us
    ppermute x4, starting transfers between devices, on_device(): landed.append(lax.ppermute(final[k], ('seq', 'beam'), pairs))  3.92 us
    ppermute x1, waiting for transfers between devices, on_device(): got_a = lax.ppermute(send_a, 'seq', swap)  3.43 us
    unnamed x26, local copies, waits for them, and re-layouts  2.88 us
  transfers between devices with their start and end apart: 10, of which 3 were waited for; matrix products, arithmetic and copies ran while one was open for 0% of the time, Pallas kernels for 15%

profile of v2, /device:TPU:25, one launch (start us, length us, event | category | flops | bytes accessed | tf_op | source)
XLA Modules:
  0.0 87.9 jit_solution(17434257610556402912)
XLA Ops:
  0.6 0.0 copy-start.11
  0.6 0.0 copy-start.12
  0.7 0.0 copy-start.10
  0.7 0.0 copy-start
  0.7 1.2 %copy-done = bf16[256,2048]{1,0:T(8,128)(2,1)S(1)} copy-done((bf16[256,2048]{1,0:T(8,128)(2,1)S(1)}, bf16[256,2048]{1,0:T(8,128)(2,1)}, u32[]{:S(2)}) %copy-start) | copy-done | bytes 1048600
  1.9 0.8 copy-done.3
  2.7 0.8 copy-done.5
  3.5 1.4 %shard_map.156 = (f32[256,32]{1,0:T(8,128)S(1)}, f32[32,256]{1,0:T(8,128)S(1)}, f32[520,128]{1,0:T(8,128)S(1)}) custom-call(bf16[256,2048]{1,0:T(8,128)(2,1)S(1)} %copy-done, bf16[256,128]{1,0:T(8,128)(2,1)S(1)} %copy-done.3, f32[32,256]{1,0:T(8,128)S(1)} %bitcast.13), custom_call_target="tpu_custom_call" | custom-call | flops 1000000 | bytes 1000000 | tf_op jit(solution)/shard_map/pallas_call | solution.py:26
  4.9 0.0 copy-start.6
  4.9 0.0 copy-start.8
  5.0 0.0 copy-start.9
  5.0 0.2 collective-permute-start.3
  5.2 2.3 %shard_map.157 = (f32[520,128]{1,0:T(8,128)S(1)}, f32[520,128]{1,0:T(8,128)S(1)}, f32[520,128]{1,0:T(8,128)S(1)}) custom-call(bf16[256,2048]{1,0:T(8,128)(2,1)S(1)} %copy-done, bf16[256,128]{1,0:T(8,128)(2,1)S(1)} %copy-done.3, f32[256,32]{1,0:T(8,128)S(1)} %get-tuple-element.29.sums_ref), custom_call_target="tpu_custom_call" | custom-call | flops 1000000 | bytes 1000000 | tf_op jit(solution)/shard_map/pallas_call | solution.py:26
  7.5 1.4 %collective-permute-start = (f32[520,128]{1,0:T(8,128)S(1)}, f32[520,128]{1,0:T(8,128)S(1)}, u32[]{:S(2)}, u32[]{:S(2)}) collective-permute-start(f32[520,128]{1,0:T(8,128)S(1)} %get-tuple-element.31), channel_id=1, source_target_pairs={{0,4},{4,0},{8,12},{12,8},{1,5},{5,1},{9,13},{13,9},{2,6},{6,2},{1... | collective-permute-start | bytes 798728 | tf_op jit(solution)/shard_map/ppermute | solution.py:392
  8.9 3.4 %collective-permute-done.3.got_ref.swap_ref = f32[520,128]{1,0:T(8,128)S(1)} collective-permute-done((f32[520,128]{1,0:T(8,128)S(1)}, f32[520,128]{1,0:T(8,128)S(1)}, u32[]{:S(2)}, u32[]{:S(2)}) %collective-permute-start.3) | collective-permute-done | bytes 266272 | tf_op jit(solution)/shard_map/ppermute | solution.py:382
  12.4 0.1 collective-permute-start.4
  12.5 0.0 copy-done.11
  12.5 0.0 copy-done.12
  12.5 8.5 %collective-permute-done.got_ref.swap_ref = f32[520,128]{1,0:T(8,128)S(1)} collective-permute-done((f32[520,128]{1,0:T(8,128)S(1)}, f32[520,128]{1,0:T(8,128)S(1)}, u32[]{:S(2)}, u32[]{:S(2)}) %collective-permute-start) | collective-permute-done | bytes 266272 | tf_op jit(solution)/shard_map/ppermute | solution.py:392
  21.0 0.4 collective-permute-start.1
  22.7 8.1 %collective-permute-done.4.got_ref = f32[520,128]{1,0:T(8,128)S(1)} collective-permute-done((f32[520,128]{1,0:T(8,128)S(1)}, f32[520,128]{1,0:T(8,128)S(1)}, u32[]{:S(2)}, u32[]{:S(2)}) %collective-permute-start.4) | collective-permute-done | bytes 266272 | tf_op jit(solution)/shard_map/ppermute | solution.py:442
  30.8 0.1 shard_map.162
  30.9 0.7 collective-permute-start.8
  31.6 1.3 %collective-permute-start.9 = (f32[256,128]{1,0:T(8,128)S(1)}, f32[256,128]{1,0:T(8,128)S(1)}, u32[]{:S(2)}, u32[]{:S(2)}) collective-permute-start(f32[256,128]{1,0:T(8,128)S(1)} %get-tuple-element.48), channel_id=1, source_target_pairs={{0,1},{4,3},{1,5},{5,7},{10,9},{14,11},{11,13},{15,15},{16,17},{20... | collective-permute-start | bytes 393224 | tf_op jit(solution)/shard_map/ppermute | solution.py:467
  32.9 0.1 pad_maximum_fusion.1.tail_ref
  32.9 0.0 copy-done.6
  32.9 0.8 shard_map.166
  33.8 14.4 %all_gather.10.rows_ref = f32[4,4,4352]{2,1,0:T(4,128)S(1)} all-gather(f32[1,4,4352]{2,1,0:T(4,128)S(1)} %shard_map.166), channel_id=1, replica_groups=mesh['groups'=2,'seq'=4,'beam'=4] {'beam'}, dimensions={0}, use_global_device_ids=true | all-gather | bytes 348160 | tf_op jit(solution)/shard_map/all_gather | solution.py:37
  48.2 2.2 %shard_map.167 = (f32[8,2048]{1,0:T(8,128)S(1)}, f32[8,2048]{1,0:T(8,128)S(1)}, f32[2048,128]{1,0:T(8,128)S(1)}, f32[32,128]{1,0:T(8,128)S(1)}, f32[1,4]{1,0:T(1,128)}) custom-call(f32[4,4,4352]{2,1,0:T(4,128)S(1)} %all_gather.10.rows_ref, bf16[4,128]{1,0:T(4,128)(2,1)S(1)} %bitcast.15), custom_call_target="tpu_custom_call" | custom-call | flops 1000000 | bytes 1000000 | tf_op jit(solution)/shard_map/pallas_call | solution.py:26
  50.5 3.9 %shard_map.160 = (f32[256,2048]{1,0:T(8,128)S(1)}, f32[256,2048]{1,0:T(8,128)S(1)}) custom-call(bf16[256,2048]{1,0:T(8,128)(2,1)S(1)} %copy-done.1, bf16[256,128]{1,0:T(8,128)(2,1)S(1)} %copy-done.4, bf16[256,128]{1,0:T(8,128)(2,1)S(1)} %copy-done.2, f32[256,32]{1,0:T(8,128)S(1)} %get-tuple-element.29.sums_ref, f32[32,256]{1,0:T(8,128)S(1)} %get-tuple-element.34.turned_ref), custom_call_target="tpu_custom_call" | custom-call | flops 100000000 | bytes 1000000 | tf_op jit(solution)/shard_map/pallas_call | solution.py:26
  54.4 0.0 collective-permute-done.1.got_ref
  54.4 0.1 shard_map.159
  54.5 1.9 %collective-permute-start.2 = (f32[512,128]{1,0:T(8,128)S(1)}, f32[512,128]{1,0:T(8,128)S(1)}, u32[]{:S(2)}, u32[]{:S(2)}) collective-permute-start(f32[512,128]{1,0:T(8,128)S(1)} %get-tuple-element.33), channel_id=1, source_target_pairs={{8,12},{12,8},{0,4},{9,13},{13,9},{1,5},{10,14},{14,10},{2,6},{11,... | collective-permute-start | bytes 786440 | tf_op jit(solution)/shard_map/ppermute | solution.py:469
  56.5 3.4 %collective-permute-start.5 = (f32[512,128]{1,0:T(8,128)S(1)}, f32[512,128]{1,0:T(8,128)S(1)}, u32[]{:S(2)}, u32[]{:S(2)}) collective-permute-start(f32[512,128]{1,0:T(8,128)S(1)} %get-tuple-element.40), channel_id=1, source_target_pairs={{8,12},{12,8},{0,4},{9,13},{13,9},{1,5},{10,14},{14,10},{2,6},{11,... | collective-permute-start | bytes 786440 | tf_op jit(solution)/shard_map/ppermute | solution.py:469
  59.8 0.7 collective-permute-start.6
  60.5 0.0 collective-permute-done.8.refs_0_
  60.5 1.3 %collective-permute-start.7 = (f32[256,128]{1,0:T(8,128)S(1)}, f32[256,128]{1,0:T(8,128)S(1)}, u32[]{:S(2)}, u32[]{:S(2)}) collective-permute-start(f32[256,128]{1,0:T(8,128)S(1)} %get-tuple-element.42), channel_id=1, source_target_pairs={{0,1},{4,3},{1,5},{5,7},{10,9},{14,11},{11,13},{15,15},{16,17},{20... | collective-permute-start | bytes 393224 | tf_op jit(solution)/shard_map/ppermute | solution.py:467
  61.8 0.0 collective-permute-done.9.refs_1_
  61.9 14.1 %all_gather.11.final_ref = f32[1024,128]{1,0:T(8,128)S(1)} all-gather(f32[256,128]{1,0:T(8,128)S(1)} %shard_map.168), channel_id=1, replica_groups=mesh['groups'=2,'seq'=4,'beam'=4] {'beam'}, dimensions={0}, use_global_device_ids=true | all-gather | bytes 655360 | tf_op jit(solution)/shard_map/all_gather | solution.py:37
  76.0 0.9 %shard_map.169 = (f32[2048,128]{1,0:T(8,128)}, bf16[4,2048]{1,0:T(4,128)(2,1)}) custom-call(f32[1024,128]{1,0:T(8,128)S(1)} %all_gather.11.final_ref, bf16[4,128]{1,0:T(4,128)(2,1)S(1)} %bitcast.16, f32[8,2048]{1,0:T(8,128)S(1)} %get-tuple-element.43.grow_ref, f32[8,2048]{1,0:T(8,128)S(1)} %get-tuple-element.44.part_ref, ...), custom_call_target="tpu_custom_call" | custom-call | flops 1000000 | bytes 1000000 | tf_op jit(solution)/shard_map/pallas_call | solution.py:26
  76.9 0.0 collective-permute-done.6.refs_0_
  76.9 0.0 collective-permute-done.7.refs_1_
  76.9 7.3 %all_gather.9.final_ref = f32[1024,128]{1,0:T(8,128)S(1)} all-gather(f32[256,128]{1,0:T(8,128)S(1)} %shard_map.165), channel_id=1, replica_groups=mesh['groups'=2,'seq'=4,'beam'=4] {'beam'}, dimensions={0}, use_global_device_ids=true | all-gather | bytes 655360 | tf_op jit(solution)/shard_map/all_gather | solution.py:37
  84.2 0.9 %shard_map.170 = (f32[2048,128]{1,0:T(8,128)}, bf16[4,2048]{1,0:T(4,128)(2,1)}) custom-call(f32[1024,128]{1,0:T(8,128)S(1)} %all_gather.9.final_ref, bf16[4,128]{1,0:T(4,128)(2,1)S(1)} %bitcast.17, f32[8,2048]{1,0:T(8,128)S(1)} %get-tuple-element.43.grow_ref, ...), custom_call_target="tpu_custom_call", output_to_operand_aliasing={{0}: (6, {}), {1}: (7, {})} | custom-call | flops 1000000 | bytes 1000000 | tf_op jit(solution)/shard_map/pallas_call | solution.py:26
  85.1 0.0 collective-permute-done.5.other_ref
  85.2 1.4 %shard_map.163.refs_0_ = bf16[256,2048]{1,0:T(8,128)(2,1)} custom-call(f32[512,128]{1,0:T(8,128)S(1)} %get-tuple-element.39.own_ref, f32[512,128]{1,0:T(8,128)S(1)} %collective-permute-done.5.other_ref, bf16[256,128]{1,0:T(8,128)(2,1)S(1)} %copy-done.2, f32[256,2048]{1,0:T(8,128)S(1)} %get-tuple-element.35.grown_ref, f32[256,2048]{1,0:T(8,128)S(1)} %get-tuple-element.36.inner_ref), custom_call_target="tpu_custom_call" | custom-call | flops 1000000 | bytes 1000000 | tf_op jit(solution)/shard_map/pallas_call | solution.py:26
  86.5 0.0 collective-permute-done.2.other_ref
  86.5 1.4 %shard_map.164 = bf16[256,2048]{1,0:T(8,128)(2,1)} custom-call(f32[512,128]{1,0:T(8,128)S(1)} %get-tuple-element.32.own_ref, f32[512,128]{1,0:T(8,128)S(1)} %collective-permute-done.2.other_ref, bf16[256,128]{1,0:T(8,128)(2,1)S(1)} %copy-done.2, f32[256,2048]{1,0:T(8,128)S(1)} %get-tuple-element.35.grown_ref, ...), custom_call_target="tpu_custom_call", output_to_operand_aliasing={{}: (5, {})} | custom-call | flops 1000000 | bytes 1000000 | tf_op jit(solution)/shard_map/pallas_call | solution.py:26
  (19 shorter events, 0.1 us)
Async XLA Ops:
  0.6 11.8 %copy-start.11 = (s32[4,1]{0,1:T(1,128)S(1)}, s32[4,1]{0,1:T(1,128)}, u32[]{:S(2)}) copy-start(s32[4,1]{0,1:T(1,128)} %param.23) | copy-start | bytes 52
  0.6 11.8 %copy-start.12 = (s32[4,1]{0,1:T(1,128)S(1)}, s32[4,1]{0,1:T(1,128)}, u32[]{:S(2)}) copy-start(s32[4,1]{0,1:T(1,128)} %param.22) | copy-start | bytes 52
  0.7 20.7 %copy-start.10 = (f32[4,1]{0,1:T(1,128)S(1)}, f32[4,1]{0,1:T(1,128)}, u32[]{:S(2)}) copy-start(f32[4,1]{0,1:T(1,128)} %param.21) | copy-start | bytes 52
  0.7 1.2 %copy-start = (bf16[256,2048]{1,0:T(8,128)(2,1)S(1)}, bf16[256,2048]{1,0:T(8,128)(2,1)}, u32[]{:S(2)}) copy-start(bf16[256,2048]{1,0:T(8,128)(2,1)} %values_hbm.5) | copy-start | bytes 3145732
  1.9 0.8 copy-start.3
  2.7 0.8 copy-start.5
  4.9 28.0 %copy-start.6 = (bf16[4,1,2048]{2,0,1:T(4,128)(2,1)S(1)}, bf16[4,1,2048]{2,0,1:T(4,128)(2,1)}, u32[]{:S(2)}) copy-start(bf16[4,1,2048]{2,0,1:T(4,128)(2,1)} %param.17) | copy-start | bytes 49156
  4.9 28.0 %copy-start.8 = (f32[4,1,32]{2,1,0:T(1,128)S(1)}, f32[4,1,32]{2,1,0:T(1,128)}, u32[]{:S(2)}) copy-start(f32[4,1,32]{2,1,0:T(1,128)} %param.20) | copy-start | bytes 1540
  5.0 28.0 %copy-start.9 = (bf16[4,1,128]{2,0,1:T(4,128)(2,1)S(1)}, bf16[4,1,128]{2,0,1:T(4,128)(2,1)}, u32[]{:S(2)}) copy-start(bf16[4,1,128]{2,0,1:T(4,128)(2,1)} %param.18) | copy-start | bytes 3076
  5.0 7.3 %collective-permute-start.3 = (f32[520,128]{1,0:T(8,128)S(1)}, f32[520,128]{1,0:T(8,128)S(1)}, u32[]{:S(2)}, u32[]{:S(2)}) collective-permute-start(f32[520,128]{1,0:T(8,128)S(1)} %get-tuple-element.38), channel_id=1, source_target_pairs={{0,4},{4,0},{8,12},{12,8},{1,5},{5,1},{9,13},{13,9},{2,6},{6,2},{1... | collective-permute-start | bytes 798728 | tf_op jit(solution)/shard_map/ppermute | solution.py:382
  5.2 43.0 %copy-start.7 = (bf16[4,1,128]{2,0,1:T(4,128)(2,1)S(1)}, bf16[4,1,128]{2,0,1:T(4,128)(2,1)}, u32[]{:S(2)}) copy-start(bf16[4,1,128]{2,0,1:T(4,128)(2,1)} %param.19) | copy-start | bytes 3076
  5.2 45.3 %copy-start.1 = (bf16[256,2048]{1,0:T(8,128)(2,1)S(1)}, bf16[256,2048]{1,0:T(8,128)(2,1)}, u32[]{:S(2)}) copy-start(bf16[256,2048]{1,0:T(8,128)(2,1)} %values_hbm.5) | copy-start | bytes 3145732
  5.2 45.3 %copy-start.2 = (bf16[256,128]{1,0:T(8,128)(2,1)S(1)}, bf16[256,128]{1,0:T(8,128)(2,1)}, u32[]{:S(2)}) copy-start(bf16[256,128]{1,0:T(8,128)(2,1)} %queries_ref.3) | copy-start | bytes 196612
  5.2 45.3 %copy-start.4 = (bf16[256,128]{1,0:T(8,128)(2,1)S(1)}, bf16[256,128]{1,0:T(8,128)(2,1)}, u32[]{:S(2)}) copy-start(bf16[256,128]{1,0:T(8,128)(2,1)} %keys_hbm.5) | copy-start | bytes 196612
  7.5 13.4 %collective-permute-start = (f32[520,128]{1,0:T(8,128)S(1)}, f32[520,128]{1,0:T(8,128)S(1)}, u32[]{:S(2)}, u32[]{:S(2)}) collective-permute-start(f32[520,128]{1,0:T(8,128)S(1)} %get-tuple-element.31), channel_id=1, source_target_pairs={{0,4},{4,0},{8,12},{12,8},{1,5},{5,1},{9,13},{13,9},{2,6},{6,2},{1... | collective-permute-start | bytes 798728 | tf_op jit(solution)/shard_map/ppermute | solution.py:392
  12.4 18.4 %collective-permute-start.4 = (f32[520,128]{1,0:T(8,128)S(1)}, f32[520,128]{1,0:T(8,128)S(1)}, u32[]{:S(2)}, u32[]{:S(2)}) collective-permute-start(f32[520,128]{1,0:T(8,128)S(1)} %shard_map.161.total_ref), channel_id=1, source_target_pairs={{0,8},{4,12},{8,0},{12,4},{1,9},{5,13},{9,1},{13,5},{2,10},{6,14},... | collective-permute-start | bytes 798728 | tf_op jit(solution)/shard_map/ppermute | solution.py:442
  21.0 33.4 %collective-permute-start.1 = (f32[520,128]{1,0:T(8,128)S(1)}, f32[520,128]{1,0:T(8,128)S(1)}, u32[]{:S(2)}, u32[]{:S(2)}) collective-permute-start(f32[520,128]{1,0:T(8,128)S(1)} %shard_map.158.total_ref), channel_id=1, source_target_pairs={{0,8},{4,12},{8,0},{12,4},{1,9},{5,13},{9,1},{13,5},{2,10},{6,14},... | collective-permute-start | bytes 798728 | tf_op jit(solution)/shard_map/ppermute | solution.py:442
  30.9 29.6 %collective-permute-start.8 = (f32[256,128]{1,0:T(8,128)S(1)}, f32[256,128]{1,0:T(8,128)S(1)}, u32[]{:S(2)}, u32[]{:S(2)}) collective-permute-start(f32[256,128]{1,0:T(8,128)S(1)} %get-tuple-element.47), channel_id=1, source_target_pairs={{0,0},{4,2},{1,4},{5,6},{10,8},{14,10},{11,12},{15,14},{16,16},{20... | collective-permute-start | bytes 393224 | tf_op jit(solution)/shard_map/ppermute | solution.py:467
  31.6 30.3 %collective-permute-start.9 = (f32[256,128]{1,0:T(8,128)S(1)}, f32[256,128]{1,0:T(8,128)S(1)}, u32[]{:S(2)}, u32[]{:S(2)}) collective-permute-start(f32[256,128]{1,0:T(8,128)S(1)} %get-tuple-element.48), channel_id=1, source_target_pairs={{0,1},{4,3},{1,5},{5,7},{10,9},{14,11},{11,13},{15,15},{16,17},{20... | collective-permute-start | bytes 393224 | tf_op jit(solution)/shard_map/ppermute | solution.py:467
  54.5 32.0 %collective-permute-start.2 = (f32[512,128]{1,0:T(8,128)S(1)}, f32[512,128]{1,0:T(8,128)S(1)}, u32[]{:S(2)}, u32[]{:S(2)}) collective-permute-start(f32[512,128]{1,0:T(8,128)S(1)} %get-tuple-element.33), channel_id=1, source_target_pairs={{8,12},{12,8},{0,4},{9,13},{13,9},{1,5},{10,14},{14,10},{2,6},{11,... | collective-permute-start | bytes 786440 | tf_op jit(solution)/shard_map/ppermute | solution.py:469
  56.5 28.7 %collective-permute-start.5 = (f32[512,128]{1,0:T(8,128)S(1)}, f32[512,128]{1,0:T(8,128)S(1)}, u32[]{:S(2)}, u32[]{:S(2)}) collective-permute-start(f32[512,128]{1,0:T(8,128)S(1)} %get-tuple-element.40), channel_id=1, source_target_pairs={{8,12},{12,8},{0,4},{9,13},{13,9},{1,5},{10,14},{14,10},{2,6},{11,... | collective-permute-start | bytes 786440 | tf_op jit(solution)/shard_map/ppermute | solution.py:469
  59.8 17.1 %collective-permute-start.6 = (f32[256,128]{1,0:T(8,128)S(1)}, f32[256,128]{1,0:T(8,128)S(1)}, u32[]{:S(2)}, u32[]{:S(2)}) collective-permute-start(f32[256,128]{1,0:T(8,128)S(1)} %get-tuple-element.41), channel_id=1, source_target_pairs={{0,0},{4,2},{1,4},{5,6},{10,8},{14,10},{11,12},{15,14},{16,16},{20... | collective-permute-start | bytes 393224 | tf_op jit(solution)/shard_map/ppermute | solution.py:467
  60.5 16.4 %collective-permute-start.7 = (f32[256,128]{1,0:T(8,128)S(1)}, f32[256,128]{1,0:T(8,128)S(1)}, u32[]{:S(2)}, u32[]{:S(2)}) collective-permute-start(f32[256,128]{1,0:T(8,128)S(1)} %get-tuple-element.42), channel_id=1, source_target_pairs={{0,1},{4,3},{1,5},{5,7},{10,9},{14,11},{11,13},{15,15},{16,17},{20... | collective-permute-start | bytes 393224 | tf_op jit(solution)/shard_map/ppermute | solution.py:467

commit v3 on v2

v3 whole, which is shorter than its diff:
```python
import functools

import jax
import jax.numpy as jnp
from jax import lax
from jax.experimental import pallas as pl
from jax.experimental.pallas import tpu as pltpu
from jax.sharding import PartitionSpec as P


LANES = 128
SUB = 8
HALVES = 2
SHORT = 2
INNER = 4
F32 = jnp.float32
BF16 = jnp.bfloat16
TN = (((0,), (0,)), ((), ()))
NT = (((1,), (1,)), ((), ()))

VMEM = pl.BlockSpec(memory_space=pltpu.VMEM)
HBM = pl.BlockSpec(memory_space=pltpu.HBM)
SMEM = pl.BlockSpec(memory_space=pltpu.SMEM)


def call(body, args, out_shape, in_specs=None, flops=1_000_000, **kwargs):
    return pl.pallas_call(
        body,
        out_shape=out_shape,
        in_specs=in_specs,
        cost_estimate=pl.CostEstimate(flops=flops, bytes_accessed=1_000_000, transcendentals=0),
        compiler_params=pltpu.CompilerParams(vmem_limit_bytes=8 * 2**20),
        **kwargs,
    )(*args)


def permute(array, axis, pairs):
    return lax.ppermute(array, axis, pairs)


def gather(array):
    return lax.all_gather(array, "beam", axis=0, tiled=True)


def iota(shape, axis):
    return lax.broadcasted_iota(jnp.int32, shape, axis)


def head_lanes(heads, first, count, width):
    shape = (heads, count * width)
    return (iota(shape, 0) == first + iota(shape, 1) // width).astype(F32)


def thirds(x, axis):
    high = x.astype(BF16)
    rest = x - high.astype(F32)
    middle = rest.astype(BF16)
    return jnp.concatenate([high, middle, (rest - middle.astype(F32)).astype(BF16)], axis=axis)


def spread(x, first, count, width):
    hot = head_lanes(x.shape[1], first, count, width).astype(BF16)
    return jnp.dot(thirds(x, 1), jnp.concatenate([hot] * 3, axis=0), preferred_element_type=F32)


def part_state(values, keys, sums, first, count, width, out_ref):
    heads = sums.shape[1]
    last = sums[-1:, :]
    scaled = (values.astype(F32) * spread(jnp.exp(last - sums), first, count, width)).astype(BF16)
    rows = count * width
    out_ref[0:rows, :] = lax.dot_general(scaled, keys, TN, preferred_element_type=F32)
    pad = out_ref.shape[0] - rows
    pick = iota((pad, heads), 1) == first + iota((pad, heads), 0)
    total = jnp.sum(jnp.where(pick, last, 0.0), axis=1, keepdims=True)
    out_ref[rows:, :] = jnp.broadcast_to(jnp.exp(total), (pad, LANES))


def rank_bit(k):
    return (lax.axis_index("seq") >> k) & 1


def half_start(kept, heads):
    return (rank_bit(0) if kept else rank_bit(0) ^ 1) * (heads // HALVES)


def fetch(arrived, *pairs):
    copies = [pltpu.make_async_copy(source, target, arrived.at[k]) for k, (source, target) in enumerate(pairs)]
    for copy in copies:
        copy.start()
    return copies


def first_kernel(values_hbm, keys_hbm, decay_hbm, sums_ref, turned_ref, out_ref, values, keys, decay, arrived, *, count, width):
    heads, tokens = decay.shape
    start = half_start(False, heads)
    columns = values_hbm.at[:, pl.ds(pl.multiple_of(start * width, LANES), count * width)]
    copies = fetch(arrived, (decay_hbm, decay), (columns, values), (keys_hbm, keys))
    copies[0].wait()
    upper = (iota((tokens, tokens), 0) <= iota((tokens, tokens), 1)).astype(F32).astype(BF16)
    terms = jnp.dot(thirds(decay[...], 0), upper, preferred_element_type=F32)
    turned = terms[0:heads] + (terms[heads : 2 * heads] + terms[2 * heads :])
    turned_ref[...] = turned
    sums = turned.T
    sums_ref[...] = sums
    for copy in copies[1:]:
        copy.wait()
    part_state(values[...], keys[...], sums, start, count, width, out_ref)


def state_kernel(values_hbm, keys_hbm, sums_ref, *refs, kept, offset, counts, width):
    *out_refs, values_ref, keys_ref, arrived = refs
    start = half_start(kept, sums_ref.shape[1]) + offset
    columns = pl.ds(pl.multiple_of(start * width, LANES), sum(counts) * width)
    for copy in fetch(arrived, (values_hbm.at[:, columns], values_ref), (keys_hbm, keys_ref)):
        copy.wait()
    done = 0
    for count, out_ref in zip(counts, out_refs, strict=True):
        values = values_ref[:, done * width : (done + count) * width]
        part_state(values, keys_ref[...], sums_ref[...], start + done, count, width, out_ref)
        done += count


def inner_kernel(
    values_hbm, keys_hbm, queries_hbm, sums_ref, turned_ref, out_ref, grown_ref,
    values_ref, keys_ref, queries_ref, wide_ref, arrived, *, count, width
):
    copies = fetch(arrived, (keys_hbm, keys_ref), (queries_hbm, queries_ref), (values_hbm, values_ref))
    tokens, heads = sums_ref.shape
    half = tokens // 2
    wide_ref[...] = jnp.zeros_like(wide_ref)
    wide_ref[:, 0:heads] = sums_ref[...]
    for copy in copies:
        copy.wait()
    scores = lax.dot_general(queries_ref[...], keys_ref[...], NT, preferred_element_type=F32)
    lower = iota((half, half), 0) >= iota((half, half), 1)
    top = jnp.where(lower, scores[:half, :half], 0.0)
    left = scores[half:, :half]
    bottom = jnp.where(lower, scores[half:, half:], 0.0)
    per_store = LANES // width
    lane = iota((tokens, LANES), 1) // width

    def group(g, carry):
        wide = pltpu.roll(wide_ref[...], lax.rem(LANES - g * count, LANES), 1)
        for k in range(count // per_store):
            place = pl.ds(pl.multiple_of((g * count + k * per_store) * width, LANES), LANES)
            values = values_ref[:, place]
            tops, bottoms = [], []
            grown = wide[:, k * per_store : k * per_store + 1]
            for m in range(1, per_store):
                grown = jnp.where(lane == m, wide[:, k * per_store + m : k * per_store + m + 1], grown)
            grown_ref[:, place] = jnp.exp(jnp.broadcast_to(grown, (tokens, LANES)))
            for m in range(per_store):
                h = k * per_store + m
                column = wide[:, h : h + 1]
                row = turned_ref[pl.ds(g * count + h, 1), :]
                x = values[:, m * width : (m + 1) * width]
                w0 = (top * jnp.exp(jnp.minimum(column[:half] - row[:, :half], 0.0))).astype(BF16)
                w1 = (left * jnp.exp(column[half:] - row[:, :half])).astype(BF16)
                w2 = (bottom * jnp.exp(jnp.minimum(column[half:] - row[:, half:], 0.0))).astype(BF16)
                tops.append(jnp.dot(w0, x[:half], preferred_element_type=F32))
                bottoms.append(jnp.dot(jnp.concatenate([w1, w2], axis=1), x, preferred_element_type=F32))
            out_ref[0:half, place] = jnp.concatenate(tops, axis=1)
            out_ref[half:, place] = jnp.concatenate(bottoms, axis=1)
        return carry

    lax.fori_loop(0, heads // count, group, 0)


def combine(low, high, out, count, width, decay=True):
    rows = count * width
    for h in range(count):
        place = slice(h * width, (h + 1) * width)
        out[place, :] = high[rows + h : rows + h + 1, :] * low[place, :] + high[place, :]
    if decay:
        out[rows:, :] = low[rows:, :] * high[rows:, :]


def pair_kernel(keep_ref, got_ref, out_ref, *, count, width):
    odd = rank_bit(0) == 1

    @pl.when(odd)
    def _():
        combine(got_ref, keep_ref, out_ref, count, width)

    @pl.when(jnp.logical_not(odd))
    def _():
        combine(keep_ref, got_ref, out_ref, count, width)


def round_kernel(total_ref, got_ref, *refs, bit, first, count, width):
    before_ref, refs = (None, refs) if first else (refs[0], refs[1:])
    before_out, total_out = refs
    upper = rank_bit(bit) == 1
    rows = count * width

    @pl.when(upper)
    def _():
        combine(got_ref, total_ref, total_out, count, width)
        if first:
            before_out[...] = got_ref[...]
        else:
            combine(got_ref, before_ref, before_out, count, width)

    @pl.when(jnp.logical_not(upper))
    def _():
        combine(total_ref, got_ref, total_out, count, width)
        if first:
            before_out[0:rows, :] = jnp.zeros((rows, LANES), F32)
            before_out[rows:, :] = jnp.ones((before_out.shape[0] - rows, LANES), F32)
        else:
            before_out[...] = before_ref[...]


def last_kernel(total_ref, got_ref, keep_ref, swap_ref, *refs, bit, first, count, width):
    before_ref, refs = (None, refs) if first else (refs[0], refs[1:])
    final_ref, own_ref, hand_ref, before_now = refs
    upper = rank_bit(bit) == 1
    odd = rank_bit(0) == 1
    rows = count * width

    @pl.when(upper)
    def _():
        combine(got_ref, total_ref, final_ref, count, width, decay=False)
        if first:
            before_now[...] = got_ref[0:rows, :]
        else:
            combine(got_ref, before_ref, before_now, count, width, decay=False)

    @pl.when(jnp.logical_not(upper))
    def _():
        combine(total_ref, got_ref, final_ref, count, width, decay=False)
        before_now[...] = jnp.zeros_like(before_now) if first else before_ref[0:rows, :]

    @pl.when(odd)
    def _():
        combine(before_now, swap_ref, own_ref, count, width, decay=False)
        hand_ref[...] = before_now[...]

    @pl.when(jnp.logical_not(odd))
    def _():
        own_ref[...] = before_now[...]
        combine(before_now, keep_ref, hand_ref, count, width, decay=False)


def output_kernel(own_ref, other_ref, queries_ref, grown_ref, inner_ref, *refs, offset, width):
    out_hbm, held, sent = refs[-3:]
    lanes = own_ref.shape[0]
    copies = []
    for half in range(HALVES):
        columns = slice(half * out_hbm.shape[1] // HALVES + offset * width, None)
        columns = slice(columns.start, columns.start + lanes)

        def emit(state_ref):
            carried = lax.dot_general(queries_ref[...], state_ref[...].astype(BF16), NT, preferred_element_type=F32)
            held[half] = (inner_ref[:, columns] + carried * grown_ref[:, columns]).astype(BF16)

        mine = rank_bit(0) == half

        @pl.when(mine)
        def _():
            emit(own_ref)

        @pl.when(jnp.logical_not(mine))
        def _():
            emit(other_ref)

        copies.append(pltpu.make_async_copy(held.at[half], out_hbm.at[:, pl.ds(columns.start, lanes)], sent.at[half]))
        copies[-1].start()
    for copy in copies:
        copy.wait()


def pack_kernel(
    values_ref, decay_ref, keys_ref, score_ref, parent_ref, done_ref, length_ref, first_ref, out_ref, *, width
):
    steps, wide = values_ref.shape
    heads = decay_ref.shape[1]
    decays = spread(decay_ref[...], 0, heads, width)
    values = values_ref[...].astype(F32)
    lane = iota((1, LANES), 1)
    lines = wide // LANES
    for step in range(steps):
        row = jnp.zeros((1, LANES), F32)
        for k, ref in enumerate((score_ref, parent_ref, done_ref, length_ref, first_ref)):
            place = step if ref.shape[1] > 1 else 0
            row = jnp.where(lane == k, ref[0:1, place : place + 1].astype(F32), row)
        out_ref[step : step + 1, :] = row
        start = 2 * steps + step * 2 * lines
        for k in range(lines):
            lanes = slice(k * LANES, (k + 1) * LANES)
            out_ref[start + k : start + k + 1, :] = values[step : step + 1, lanes]
            out_ref[start + lines + k : start + lines + k + 1, :] = decays[step : step + 1, lanes]
    out_ref[steps : 2 * steps, :] = keys_ref[...].astype(F32)


def whole_kernel(final_ref, next_ref, far_ref, out_ref):
    home = lax.axis_index("seq") == lax.axis_index("beam")
    for half in range(HALVES):
        local = rank_bit(0) == half

        @pl.when(home & local)
        def _():
            out_ref[half] = final_ref[...]

        @pl.when(home ^ local)
        def _():
            out_ref[half] = next_ref[...]

        @pl.when(jnp.logical_not(home | local))
        def _():
            out_ref[half] = far_ref[...]


def either_kernel(mine_ref, got_ref, out_ref, *, bits):
    has = ((lax.axis_index("seq") ^ lax.axis_index("beam")) & bits) == 0

    @pl.when(has)
    def _():
        out_ref[...] = mine_ref[...]

    @pl.when(jnp.logical_not(has))
    def _():
        out_ref[...] = got_ref[...]


def lineage_kernel(
    rows_ref, queries_ref, grow_ref, part_ref, fresh_ref, shrink_ref, ranked_ref,
    outer_ref, key_ref, scores, counts, scalar_ref, arrived, *, slots, steps, wide, width
):
    (copy,) = fetch(arrived, (rows_ref.at[:, pl.ds(0, 2 * steps), :], scalar_ref))
    copy.wait()
    lines = wide // LANES
    flat = lambda x: jnp.concatenate([x[k : k + 1, :] for k in range(lines)], axis=1)
    me = lax.axis_index("beam")
    ranks_row = jnp.zeros((1, LANES), F32)
    done = lambda slot, step: scalar_ref[slot, step, 2]
    parent = lambda slot, step: scalar_ref[slot, step, 1].astype(jnp.int32)
    for slot in range(slots):
        scores[0, slot] = scalar_ref[slot, 0, 4]
        counts[0, slot] = scalar_ref[slot, 0, 3]
    lane = iota((1, LANES), 1)
    for step in range(steps):
        score_row = jnp.zeros((1, LANES), F32)
        count_row = jnp.zeros((1, LANES), F32)
        for slot in range(slots):
            source = parent(slot, step)
            live = 1.0 - done(slot, step)
            score = scores[step, source] + live * scalar_ref[slot, step, 0]
            tally = counts[step, source] + live
            scores[step + 1, slot] = score
            counts[step + 1, slot] = tally
            score_row = jnp.where(lane == slot, score, score_row)
            count_row = jnp.where(lane == slot, tally, count_row)
        normed = score_row * jnp.exp(-0.6 * jnp.log((5.0 + count_row) / 6.0))
        best = jnp.max(jnp.where(lane < slots, normed, -jnp.inf), axis=1, keepdims=True)
        mine = jnp.sum(jnp.where(lane == me, normed, 0.0), axis=1, keepdims=True)
        ranks_row = jnp.where(lane == step, mine - best, ranks_row)
    ranked_ref[...] = ranks_row[:, 0:steps]

    for ref in (grow_ref, part_ref, outer_ref, key_ref):
        ref[...] = jnp.zeros_like(ref)
    for step in range(steps):
        slot = me
        factor = jnp.ones((lines, LANES), F32)
        part = jnp.zeros((lines, LANES), F32)
        query = queries_ref[step : step + 1, :].astype(F32)
        live_now = 1.0 - done(me, step)
        for back in range(step, -1, -1):
            start = 2 * steps + back * 2 * lines
            live = 1.0 - done(slot, back)
            values = rows_ref[slot, start : start + lines, :]
            key = rows_ref[slot, steps + back : steps + back + 1, :]
            weight = factor * (values * live)
            part = part + weight * jnp.sum(key * query, axis=1, keepdims=True)
            if step == steps - 1:
                outer_ref[back : back + 1, :] = flat(weight)
                key_ref[back : back + 1, :] = key
            factor = factor * jnp.exp(rows_ref[slot, start + lines : start + 2 * lines, :] * live)
            slot = parent(slot, back)
        grow_ref[step : step + 1, :] = flat(factor * live_now)
        part_ref[step : step + 1, :] = flat(part * live_now)
        if step == steps - 1:
            keys = jnp.concatenate([key_ref[...].astype(BF16)] * 3, axis=0)
            fresh_ref[...] = lax.dot_general(thirds(outer_ref[...], 0), keys, TN, preferred_element_type=F32)
            count = shrink_ref.shape[0]
            pick = iota((count, wide), 1) == iota((count, wide), 0) * width
            shrink_ref[...] = jnp.broadcast_to(
                jnp.sum(jnp.where(pick, flat(factor), 0.0), axis=1, keepdims=True), (count, LANES)
            )


def decode_kernel(
    final_ref, queries_ref, grow_ref, part_ref, fresh_ref, shrink_ref, *refs, stretches, offset, count, width, last, given
):
    if given:
        earlier_ref, refs = refs[0], refs[2:]
    states_hbm, out_ref, held, sent = refs
    steps = queries_ref.shape[0]
    rows = count * width
    stretch = grow_ref.shape[1] // stretches
    copies = []
    for k in range(stretches):
        start = k * stretch + offset * width
        final = final_ref[k]
        product = lax.dot_general(queries_ref[...], final.astype(BF16), NT, preferred_element_type=F32)
        lanes = slice(start, start + rows)
        result = (grow_ref[0:steps, lanes] * product + part_ref[0:steps, lanes]).astype(BF16)
        if last:
            out_ref[:, lanes] = result
        else:
            out_ref[:, k * rows : (k + 1) * rows] = result
        for h in range(count):
            inside = slice(h * width, (h + 1) * width)
            head = start // width + h
            held[k, inside, :] = (
                shrink_ref[head : head + 1, :] * final[inside, :] + fresh_ref[start + h * width : start + (h + 1) * width, :]
            )
        copies.append(pltpu.make_async_copy(held.at[k], states_hbm.at[pl.ds(start, rows), :], sent.at[k]))
        copies[-1].start()
        if given:
            before = earlier_ref.shape[1] // stretches
            out_ref[:, k * stretch : k * stretch + before] = earlier_ref[:, k * before : (k + 1) * before]
    for copy in copies:
        copy.wait()


def emit_states(final, offset, count, width, lines, earlier, last):
    wide, steps = lines[1].shape[1], lines[0].shape[0]
    rows, stretches = count * width, final.shape[0]
    given = () if earlier is None else (earlier[1], earlier[0])
    return call(
        functools.partial(
            decode_kernel, stretches=stretches, offset=offset, count=count, width=width, last=last, given=bool(given)
        ),
        (final,) + lines + given,
        (
            jax.ShapeDtypeStruct((wide, LANES), F32),
            jax.ShapeDtypeStruct((steps, wide if last else stretches * rows), BF16),
        ),
        [VMEM] * 6 + [VMEM, HBM][: len(given)],
        out_specs=(HBM, VMEM),
        scratch_shapes=[pltpu.VMEM((stretches, rows, LANES), F32), pltpu.SemaphoreType.DMA((stretches,))],
        input_output_aliases={7: 0} if given else {},
    )


def on_device(
    prompt_values, prompt_keys, prompt_queries, logarithm_state_decay, step_values, step_keys, step_queries, step_decay,
    step_logprob, parents, finished, lengths, init_score, *, ranks, slots
):
    here = lambda x: pltpu.with_memory_space_constraint(x, pltpu.HBM)
    prompt_values, prompt_keys, prompt_queries = here(prompt_values), here(prompt_keys), here(prompt_queries)
    tokens, heads = logarithm_state_decay.shape
    width = prompt_values.shape[1] // heads
    steps = step_values.shape[0]
    wide = step_values.shape[2]
    own_heads = wide // width
    half_heads = heads // HALVES
    counts = (half_heads // SHORT, half_heads - half_heads // SHORT)
    offsets = (0, counts[0])
    array = lambda *shape, dtype=F32: jax.ShapeDtypeStruct(shape, dtype)
    messages = [array(count * width + -(-count // SUB) * SUB, LANES) for count in counts]
    levels = ranks.bit_length() - 1
    rank = lax.axis_index("seq")

    sums, turned, send_a = call(
        functools.partial(first_kernel, count=counts[0], width=width),
        (prompt_values, prompt_keys, here(logarithm_state_decay.T)),
        (array(tokens, heads), array(heads, tokens), messages[0]),
        [HBM] * 3,
        scratch_shapes=[
            pltpu.VMEM((tokens, counts[0] * width), BF16), pltpu.VMEM((tokens, LANES), BF16), pltpu.VMEM((heads, tokens), F32),
            pltpu.SemaphoreType.DMA((3,)),
        ],
    )
    swap = [(k, k ^ 1) for k in range(ranks)]
    got_a = permute(send_a, "seq", swap)

    def more_states(kept, offset, parts):
        return call(
            functools.partial(state_kernel, kept=kept, offset=offset, counts=[counts[sub] for sub in parts], width=width),
            (prompt_values, prompt_keys, sums),
            [messages[sub] for sub in parts],
            [HBM, HBM, VMEM],
            scratch_shapes=[
                pltpu.VMEM((tokens, sum(counts[sub] for sub in parts) * width), BF16), pltpu.VMEM((tokens, LANES), BF16),
                pltpu.SemaphoreType.DMA((2,)),
            ],
        )

    (send_b,) = more_states(False, offsets[1], (1,))
    got_b = permute(send_b, "seq", swap)
    keep_a, keep_b = more_states(True, 0, (0, 1))
    keeps, swaps = (keep_a, keep_b), (got_a, got_b)

    packed = call(
        functools.partial(pack_kernel, width=width),
        (
            step_values[:, 0], step_decay[:, 0], step_keys[:, 0], step_logprob.T, parents.T, finished.T, lengths[None],
            init_score[None],
        ),
        array(2 * steps * (1 + wide // LANES), LANES),
        [VMEM] * 8,
    )
    queries = step_queries[:, 0]

    *lines, ranked = call(
        functools.partial(lineage_kernel, slots=slots, steps=steps, wide=wide, width=width),
        (gather(packed).reshape(slots, -1, LANES), queries),
        (array(SUB, wide), array(SUB, wide), array(wide, LANES), array(own_heads, LANES), array(1, steps)),
        [VMEM, VMEM],
        scratch_shapes=[
            pltpu.VMEM((SUB, wide), F32), pltpu.VMEM((SUB, LANES), F32),
            pltpu.SMEM((steps + 1, slots), F32), pltpu.SMEM((steps + 1, slots), F32),
            pltpu.SMEM((slots, 2 * steps, LANES), F32), pltpu.SemaphoreType.DMA((1,)),
        ],
    )
    lines, ranked = (queries, *lines), ranked.reshape(steps, 1)

    inner, grown = call(
        functools.partial(inner_kernel, count=heads // INNER, width=width),
        (prompt_values, prompt_keys, prompt_queries, sums, turned),
        (array(tokens, heads * width),) * 2,
        [HBM, HBM, HBM, VMEM, VMEM],
        scratch_shapes=[
            pltpu.VMEM(prompt_values.shape, BF16), pltpu.VMEM((tokens, LANES), BF16), pltpu.VMEM((tokens, LANES), BF16),
            pltpu.VMEM((tokens, LANES), F32), pltpu.SemaphoreType.DMA((3,)),
        ],
        flops=100_000_000,
    )

    direct = ranks == slots
    out = states = step_out = None
    finals = []
    for sub, count in enumerate(counts):
        sizes = dict(count=count, width=width)
        rows, message = count * width, messages[sub]
        total = call(functools.partial(pair_kernel, **sizes), (keeps[sub], swaps[sub]), message, [VMEM] * 2)
        before = ()
        for level in range(1, levels):
            got = permute(total, "seq", [(k, k ^ (1 << level)) for k in range(ranks)])
            if level < levels - 1:
                before_now, total = call(
                    functools.partial(round_kernel, bit=level, first=level == 1, **sizes),
                    (total, got) + before,
                    (message, message),
                    [VMEM] * (2 + len(before)),
                )
                before = (before_now,)
        final, own, hand = call(
            functools.partial(last_kernel, bit=levels - 1, first=levels == 2, **sizes),
            (total, got, keeps[sub], swaps[sub]) + before,
            (array(rows, LANES),) * 3,
            [VMEM] * (4 + len(before)),
            scratch_shapes=[pltpu.VMEM((rows, LANES), F32)],
        )
        finals.append(final)
        if direct:
            far = slots // HALVES
            near = [((g ^ 1) * slots + g, g * slots + g) for g in range(ranks)]
            near += [(g * slots + g, g * slots + (g ^ far)) for g in range(ranks)]
            across = permute(final, ("seq", "beam"), [((g ^ 1) * slots + g, g * slots + (g ^ far)) for g in range(ranks)])
            came = permute(final, ("seq", "beam"), near)
            full = call(whole_kernel, (final, came, across), array(HALVES, rows, LANES), [VMEM] * 3)
            bit = 1
            while bit < far:
                have = [b for b in range(slots) if b & (far - 1) < bit]
                pairs = [(g * slots + (g ^ b), g * slots + (g ^ b ^ bit)) for g in range(ranks) for b in have]
                handed = permute(full, ("seq", "beam"), pairs)
                full = call(
                    functools.partial(either_kernel, bits=bit), (full, handed), array(HALVES, rows, LANES),
                    [VMEM] * 2,
                )
                bit *= 2
        back = permute(hand, "seq", [(k, k ^ 1) for k in range(1, ranks) if k != 1] + [(0, 1)])
        if direct:
            states, step_out = emit_states(
                full, offsets[sub], count, width, lines, (states, step_out) if sub else None, sub == 1
            )
        given = () if out is None else (out,)
        out = call(
            functools.partial(output_kernel, offset=offsets[sub], width=width),
            (own, back, prompt_queries, grown, inner) + given,
            array(tokens, heads * width, dtype=BF16),
            [VMEM] * 5 + [HBM] * len(given),
            out_specs=HBM,
            scratch_shapes=[pltpu.VMEM((HALVES, tokens, rows), BF16), pltpu.SemaphoreType.DMA((HALVES,))],
            input_output_aliases={5: 0} if given else {},
        )
    if not direct:
        half = jnp.concatenate(finals)
        other = lax.ppermute(half, "seq", swap)
        odd = rank_bit(0) == 1
        both = jnp.concatenate([jnp.where(odd, other, half), jnp.where(odd, half, other)])
        every = gather(both)
        full = lax.dynamic_slice_in_dim(every, rank * wide, wide, 0)[None]
        states, step_out = emit_states(full, 0, own_heads, width, lines, None, True)
    return out, step_out.reshape(steps, 1, wide), ranked, states.reshape(1, wide, LANES)


def solution(mesh):
    ranks, slots = mesh.shape["seq"], mesh.shape["beam"]

    def body(*args):
        return on_device(*args, ranks=ranks, slots=slots)

    return jax.shard_map(
        body,
        mesh=mesh,
        in_specs=(
            P(("groups", "seq"), "beam"),
            P(("groups", "seq"), None),
            P(("groups", "seq"), None),
            P(("groups", "seq"), "beam"),
            P("groups", "beam", "seq"),
            P("groups", "beam", None),
            P("groups", "beam", None),
            P("groups", "beam", "seq"),
            P("groups", "beam"),
            P("groups", "beam"),
            P("groups", "beam"),
            P(("groups", "beam")),
            P(("groups", "beam")),
        ),
        out_specs=(
            P(("groups", "seq"), "beam"),
            P("groups", "beam", "seq"),
            P("groups", "beam"),
            P(("groups", "beam"), "seq", None),
        ),
        check_vma=False,
    )
```

time: 88.3 us -> 78.4 us (0.89)
  the two profiles are of different devices: /device:TPU:25 before, /device:TPU:21 now
where the time goes in v3:
time: 78.4 us; the launch traced here: 77.9 us
  starting transfers between devices  28.1 us (36%)
  waiting for transfers between devices  20.2 us (26%)
  Pallas kernels  18.8 us (24%)
  blocking collectives  8.46 us (11%)
  between operations  2.28 us (3%)
    ppermute x12, starting transfers between devices, permute(): return lax.ppermute(array, axis, pairs)  28.1 us
    ppermute x12, waiting for transfers between devices, permute(): return lax.ppermute(array, axis, pairs)  20.2 us
    pallas_call x18, Pallas kernels, call(): pl.pallas_call(body, out_shape=out_shape, in_specs=in_specs, cost_estimat...  18.8 us
    all_gather x1, blocking collectives, gather(): return lax.all_gather(array, 'beam', axis=0, tiled=True)  8.46 us
  transfers between devices with their start and end apart: 12, of which 4 were waited for; matrix products, arithmetic and copies ran while one was open for 0% of the time, Pallas kernels for 20%

profile of v3, /device:TPU:21, one launch (start us, length us, event | category | flops | bytes accessed | tf_op | source)
XLA Modules:
  0.0 77.9 jit_solution(8486962883219944392)
XLA Ops:
  0.6 1.6 %shard_map.156 = (f32[256,32]{1,0:T(8,128)S(1)}, f32[32,256]{1,0:T(8,128)S(1)}, f32[520,128]{1,0:T(8,128)S(1)}) custom-call(bf16[256,2048]{1,0:T(8,128)(2,1)} %values_hbm.7, bf16[256,128]{1,0:T(8,128)(2,1)} %keys_hbm.7, f32[32,256]{1,0:T(8,128)} %bitcast.27), custom_call_target="tpu_custom_call" | custom-call | flops 1000000 | bytes 1000000 | tf_op jit(solution)/shard_map/pallas_call | solution.py:27
  2.2 1.4 %collective-permute-start.3 = (f32[520,128]{1,0:T(8,128)S(1)}, f32[520,128]{1,0:T(8,128)S(1)}, u32[]{:S(2)}, u32[]{:S(2)}) collective-permute-start(f32[520,128]{1,0:T(8,128)S(1)} %get-tuple-element.34), channel_id=1, source_target_pairs={{0,4},{4,0},{8,12},{12,8},{1,5},{5,1},{9,13},{13,9},{2,6},{6,2},{1... | collective-permute-start | bytes 798728 | tf_op jit(solution)/shard_map/ppermute | solution.py:38
  3.6 1.5 %shard_map.158 = f32[520,128]{1,0:T(8,128)S(1)} custom-call(bf16[256,2048]{1,0:T(8,128)(2,1)} %values_hbm.7, bf16[256,128]{1,0:T(8,128)(2,1)} %keys_hbm.7, f32[256,32]{1,0:T(8,128)S(1)} %get-tuple-element.26.sums_ref), custom_call_target="tpu_custom_call" | custom-call | flops 1000000 | bytes 1000000 | tf_op jit(solution)/shard_map/pallas_call | solution.py:27
  5.1 0.2 collective-permute-start
  5.4 1.9 %shard_map.157 = (f32[520,128]{1,0:T(8,128)S(1)}, f32[520,128]{1,0:T(8,128)S(1)}) custom-call(bf16[256,2048]{1,0:T(8,128)(2,1)} %values_hbm.7, bf16[256,128]{1,0:T(8,128)(2,1)} %keys_hbm.7, f32[256,32]{1,0:T(8,128)S(1)} %get-tuple-element.26.sums_ref), custom_call_target="tpu_custom_call" | custom-call | flops 1000000 | bytes 1000000 | tf_op jit(solution)/shard_map/pallas_call | solution.py:27
  7.3 2.3 %collective-permute-done.3.got_ref.swap_ref = f32[520,128]{1,0:T(8,128)S(1)} collective-permute-done((f32[520,128]{1,0:T(8,128)S(1)}, f32[520,128]{1,0:T(8,128)S(1)}, u32[]{:S(2)}, u32[]{:S(2)}) %collective-permute-start.3) | collective-permute-done | bytes 266272 | tf_op jit(solution)/shard_map/ppermute | solution.py:38
  9.6 0.1 collective-permute-start.4
  9.7 7.4 %collective-permute-done.got_ref.swap_ref = f32[520,128]{1,0:T(8,128)S(1)} collective-permute-done((f32[520,128]{1,0:T(8,128)S(1)}, f32[520,128]{1,0:T(8,128)S(1)}, u32[]{:S(2)}, u32[]{:S(2)}) %collective-permute-start) | collective-permute-done | bytes 266272 | tf_op jit(solution)/shard_map/ppermute | solution.py:38
  17.2 3.2 %collective-permute-start.1 = (f32[520,128]{1,0:T(8,128)S(1)}, f32[520,128]{1,0:T(8,128)S(1)}, u32[]{:S(2)}, u32[]{:S(2)}) collective-permute-start(f32[520,128]{1,0:T(8,128)S(1)} %shard_map.159.total_ref), channel_id=1, source_target_pairs={{0,8},{4,12},{8,0},{12,4},{1,9},{5,13},{9,1},{13,5},{2,10},{6,14},... | collective-permute-start | bytes 798728 | tf_op jit(solution)/shard_map/ppermute | solution.py:38
  20.4 0.5 collective-permute-done.4.got_ref
  20.9 0.1 shard_map.163
  21.0 0.0 copy-start
  21.0 0.0 copy-start.2
  21.0 0.0 copy-start.3
  21.1 0.0 copy-start.4
  21.1 0.0 copy-start.5
  21.1 0.0 copy-start.6
  21.1 0.0 copy-start.1
  21.1 0.8 %collective-permute-start.9 = (f32[512,128]{1,0:T(8,128)S(1)}, f32[512,128]{1,0:T(8,128)S(1)}, u32[]{:S(2)}, u32[]{:S(2)}) collective-permute-start(f32[512,128]{1,0:T(8,128)S(1)} %get-tuple-element.42.final_ref), channel_id=1, source_target_pairs={{4,0},{1,5},{14,10},{11,15},{0,2},{5,7},{10,8},{15,13},{20,16},{17... | collective-permute-start | bytes 786440 | tf_op jit(solution)/shard_map/ppermute | solution.py:38
  21.9 0.7 collective-permute-start.10
  22.6 10.0 %collective-permute-done.1.got_ref = f32[520,128]{1,0:T(8,128)S(1)} collective-permute-done((f32[520,128]{1,0:T(8,128)S(1)}, f32[520,128]{1,0:T(8,128)S(1)}, u32[]{:S(2)}, u32[]{:S(2)}) %collective-permute-start.1) | collective-permute-done | bytes 266272 | tf_op jit(solution)/shard_map/ppermute | solution.py:38
  32.6 0.1 shard_map.160
  32.7 0.7 collective-permute-start.6
  33.4 0.7 collective-permute-start.7
  34.1 0.0 collective-permute-done.9.next_ref
  34.1 0.0 collective-permute-done.10.far_ref
  34.1 0.1 shard_map.170.mine_ref
  34.2 1.3 %collective-permute-start.11 = (f32[2,512,128]{2,1,0:T(8,128)S(1)}, f32[2,512,128]{2,1,0:T(8,128)S(1)}, u32[]{:S(2)}, u32[]{:S(2)}) collective-permute-start(f32[2,512,128]{2,1,0:T(8,128)S(1)} %shard_map.170.mine_ref), channel_id=1, source_target_pairs={{0,1},{2,3},{5,4},{7,6},{10,11},{8,9},{15,14},{13,12},{16,17},{18,... | collective-permute-start | bytes 1572872 | tf_op jit(solution)/shard_map/ppermute | solution.py:38
  35.5 0.0 collective-permute-done.6.next_ref
  35.5 0.0 collective-permute-done.7.far_ref
  35.5 0.1 shard_map.166.mine_ref
  35.6 1.3 %collective-permute-start.8 = (f32[2,512,128]{2,1,0:T(8,128)S(1)}, f32[2,512,128]{2,1,0:T(8,128)S(1)}, u32[]{:S(2)}, u32[]{:S(2)}) collective-permute-start(f32[2,512,128]{2,1,0:T(8,128)S(1)} %shard_map.166.mine_ref), channel_id=1, source_target_pairs={{0,1},{2,3},{5,4},{7,6},{10,11},{8,9},{15,14},{13,12},{16,17},{18,... | collective-permute-start | bytes 1572872 | tf_op jit(solution)/shard_map/ppermute | solution.py:38
  36.9 15.8 %collective-permute-start.5 = (f32[512,128]{1,0:T(8,128)S(1)}, f32[512,128]{1,0:T(8,128)S(1)}, u32[]{:S(2)}, u32[]{:S(2)}) collective-permute-start(f32[512,128]{1,0:T(8,128)S(1)} %get-tuple-element.36), channel_id=1, source_target_pairs={{8,12},{12,8},{0,4},{9,13},{13,9},{1,5},{10,14},{14,10},{2,6},{11,... | collective-permute-start | bytes 786440 | tf_op jit(solution)/shard_map/ppermute | solution.py:38
  52.7 1.9 %collective-permute-start.2 = (f32[512,128]{1,0:T(8,128)S(1)}, f32[512,128]{1,0:T(8,128)S(1)}, u32[]{:S(2)}, u32[]{:S(2)}) collective-permute-start(f32[512,128]{1,0:T(8,128)S(1)} %get-tuple-element.29), channel_id=1, source_target_pairs={{8,12},{12,8},{0,4},{9,13},{13,9},{1,5},{10,14},{14,10},{2,6},{11,... | collective-permute-start | bytes 786440 | tf_op jit(solution)/shard_map/ppermute | solution.py:38
  56.0 0.2 shard_map.168
  56.2 8.5 %all_gather.3 = f32[544,128]{1,0:T(8,128)S(1)} all-gather(f32[136,128]{1,0:T(8,128)S(1)} %shard_map.168), channel_id=1, replica_groups=mesh['groups'=2,'seq'=4,'beam'=4] {'beam'}, dimensions={0}, use_global_device_ids=true | all-gather | bytes 348160 | tf_op jit(solution)/shard_map/all_gather | solution.py:42
  64.7 1.7 %shard_map.169 = (f32[8,2048]{1,0:T(8,128)S(1)}, f32[8,2048]{1,0:T(8,128)S(1)}, f32[2048,128]{1,0:T(8,128)S(1)}, f32[32,128]{1,0:T(8,128)S(1)}, f32[1,4]{1,0:T(1,128)}) custom-call(f32[4,136,128]{2,1,0:T(8,128)S(1)} %bitcast.16, bf16[4,128]{1,0:T(4,128)(2,1)S(1)} %bitcast.18), custom_call_target="tpu_custom_call" | custom-call | flops 1000000 | bytes 1000000 | tf_op jit(solution)/shard_map/pallas_call | solution.py:27
  66.3 5.0 %shard_map.161 = (f32[256,2048]{1,0:T(8,128)S(1)}, f32[256,2048]{1,0:T(8,128)S(1)}) custom-call(bf16[256,2048]{1,0:T(8,128)(2,1)} %values_hbm.7, bf16[256,128]{1,0:T(8,128)(2,1)} %keys_hbm.7, bf16[256,128]{1,0:T(8,128)(2,1)} %queries_ref.3, f32[256,32]{1,0:T(8,128)S(1)} %get-tuple-element.26.sums_ref, f32[32,256]{1,0:T(8,128)S(1)} %get-tuple-element.30.turned_ref), custom_call_target="tpu_custom_call" | custom-call | flops 100000000 | bytes 1000000 | tf_op jit(solution)/shard_map/pallas_call | solution.py:27
  71.3 0.0 collective-permute-done.5.other_ref
  71.3 2.0 %shard_map.164.refs_0_ = bf16[256,2048]{1,0:T(8,128)(2,1)} custom-call(f32[512,128]{1,0:T(8,128)S(1)} %get-tuple-element.35.own_ref, f32[512,128]{1,0:T(8,128)S(1)} %collective-permute-done.5.other_ref, bf16[256,128]{1,0:T(8,128)(2,1)} %queries_ref.3, f32[256,2048]{1,0:T(8,128)S(1)} %get-tuple-element.31.grown_ref, f32[256,2048]{1,0:T(8,128)S(1)} %get-tuple-element.32.inner_ref), custom_call_target="tpu_custom_call" | custom-call | flops 1000000 | bytes 1000000 | tf_op jit(solution)/shard_map/pallas_call | solution.py:27
  73.4 0.0 collective-permute-done.2.other_ref
  73.4 2.0 %shard_map.165 = bf16[256,2048]{1,0:T(8,128)(2,1)} custom-call(f32[512,128]{1,0:T(8,128)S(1)} %get-tuple-element.28.own_ref, f32[512,128]{1,0:T(8,128)S(1)} %collective-permute-done.2.other_ref, bf16[256,128]{1,0:T(8,128)(2,1)} %queries_ref.3, f32[256,2048]{1,0:T(8,128)S(1)} %get-tuple-element.31.grown_ref, ...), custom_call_target="tpu_custom_call", output_to_operand_aliasing={{}: (5, {})} | custom-call | flops 1000000 | bytes 1000000 | tf_op jit(solution)/shard_map/pallas_call | solution.py:27
  75.4 0.0 collective-permute-done.11.got_ref
  75.4 0.1 shard_map.171.final_ref
  75.5 0.9 %shard_map.172 = (f32[2048,128]{1,0:T(8,128)}, bf16[4,1024]{1,0:T(4,128)(2,1)S(1)}) custom-call(f32[2,512,128]{2,1,0:T(8,128)S(1)} %shard_map.171.final_ref, bf16[4,128]{1,0:T(4,128)(2,1)S(1)} %bitcast.19, f32[8,2048]{1,0:T(8,128)S(1)} %get-tuple-element.38.grow_ref, f32[8,2048]{1,0:T(8,128)S(1)} %get-tuple-element.39.part_ref, ...), custom_call_target="tpu_custom_call" | custom-call | flops 1000000 | bytes 1000000 | tf_op jit(solution)/shard_map/pallas_call | solution.py:27
  76.3 0.0 collective-permute-done.8.got_ref
  76.4 0.1 shard_map.167.final_ref
  76.4 1.5 %shard_map.173 = (f32[2048,128]{1,0:T(8,128)}, bf16[4,2048]{1,0:T(4,128)(2,1)}) custom-call(f32[2,512,128]{2,1,0:T(8,128)S(1)} %shard_map.167.final_ref, bf16[4,128]{1,0:T(4,128)(2,1)S(1)} %bitcast.20, f32[8,2048]{1,0:T(8,128)S(1)} %get-tuple-element.38.grow_ref, f32[8,2048]{1,0:T(8,128)S(1)} %get-tuple-element.39.part_ref, ...), custom_call_target="tpu_custom_call", output_to_operand_aliasing={{0}: (7, {})} | custom-call | flops 1000000 | bytes 1000000 | tf_op jit(solution)/shard_map/pallas_call | solution.py:27
  (9 shorter events, 0.1 us)
Async XLA Ops:
  2.2 7.3 %collective-permute-start.3 = (f32[520,128]{1,0:T(8,128)S(1)}, f32[520,128]{1,0:T(8,128)S(1)}, u32[]{:S(2)}, u32[]{:S(2)}) collective-permute-start(f32[520,128]{1,0:T(8,128)S(1)} %get-tuple-element.34), channel_id=1, source_target_pairs={{0,4},{4,0},{8,12},{12,8},{1,5},{5,1},{9,13},{13,9},{2,6},{6,2},{1... | collective-permute-start | bytes 798728 | tf_op jit(solution)/shard_map/ppermute | solution.py:38
  5.1 12.1 %collective-permute-start = (f32[520,128]{1,0:T(8,128)S(1)}, f32[520,128]{1,0:T(8,128)S(1)}, u32[]{:S(2)}, u32[]{:S(2)}) collective-permute-start(f32[520,128]{1,0:T(8,128)S(1)} %shard_map.158), channel_id=1, source_target_pairs={{0,4},{4,0},{8,12},{12,8},{1,5},{5,1},{9,13},{13,9},{2,6},{6,2},{1... | collective-permute-start | bytes 798728 | tf_op jit(solution)/shard_map/ppermute | solution.py:38
  9.6 11.3 %collective-permute-start.4 = (f32[520,128]{1,0:T(8,128)S(1)}, f32[520,128]{1,0:T(8,128)S(1)}, u32[]{:S(2)}, u32[]{:S(2)}) collective-permute-start(f32[520,128]{1,0:T(8,128)S(1)} %shard_map.162.total_ref), channel_id=1, source_target_pairs={{0,8},{4,12},{8,0},{12,4},{1,9},{5,13},{9,1},{13,5},{2,10},{6,14},... | collective-permute-start | bytes 798728 | tf_op jit(solution)/shard_map/ppermute | solution.py:38
  17.2 15.4 %collective-permute-start.1 = (f32[520,128]{1,0:T(8,128)S(1)}, f32[520,128]{1,0:T(8,128)S(1)}, u32[]{:S(2)}, u32[]{:S(2)}) collective-permute-start(f32[520,128]{1,0:T(8,128)S(1)} %shard_map.159.total_ref), channel_id=1, source_target_pairs={{0,8},{4,12},{8,0},{12,4},{1,9},{5,13},{9,1},{13,5},{2,10},{6,14},... | collective-permute-start | bytes 798728 | tf_op jit(solution)/shard_map/ppermute | solution.py:38
  21.0 34.9 %copy-start = (bf16[4,1,2048]{2,0,1:T(4,128)(2,1)S(1)}, bf16[4,1,2048]{2,0,1:T(4,128)(2,1)}, u32[]{:S(2)}) copy-start(bf16[4,1,2048]{2,0,1:T(4,128)(2,1)} %param.17) | copy-start | bytes 49156
  21.0 34.9 %copy-start.2 = (f32[4,1,32]{2,1,0:T(1,128)S(1)}, f32[4,1,32]{2,1,0:T(1,128)}, u32[]{:S(2)}) copy-start(f32[4,1,32]{2,1,0:T(1,128)} %param.20) | copy-start | bytes 1540
  21.0 34.9 %copy-start.3 = (bf16[4,1,128]{2,0,1:T(4,128)(2,1)S(1)}, bf16[4,1,128]{2,0,1:T(4,128)(2,1)}, u32[]{:S(2)}) copy-start(bf16[4,1,128]{2,0,1:T(4,128)(2,1)} %param.18) | copy-start | bytes 3076
  21.1 34.9 %copy-start.4 = (f32[4,1]{0,1:T(1,128)S(1)}, f32[4,1]{0,1:T(1,128)}, u32[]{:S(2)}) copy-start(f32[4,1]{0,1:T(1,128)} %param.21) | copy-start | bytes 52
  21.1 34.9 %copy-start.5 = (s32[4,1]{0,1:T(1,128)S(1)}, s32[4,1]{0,1:T(1,128)}, u32[]{:S(2)}) copy-start(s32[4,1]{0,1:T(1,128)} %param.22) | copy-start | bytes 52
  21.1 34.9 %copy-start.6 = (s32[4,1]{0,1:T(1,128)S(1)}, s32[4,1]{0,1:T(1,128)}, u32[]{:S(2)}) copy-start(s32[4,1]{0,1:T(1,128)} %param.23) | copy-start | bytes 52
  21.1 43.6 %copy-start.1 = (bf16[4,1,128]{2,0,1:T(4,128)(2,1)S(1)}, bf16[4,1,128]{2,0,1:T(4,128)(2,1)}, u32[]{:S(2)}) copy-start(bf16[4,1,128]{2,0,1:T(4,128)(2,1)} %param.19) | copy-start | bytes 3076
  21.1 13.0 %collective-permute-start.9 = (f32[512,128]{1,0:T(8,128)S(1)}, f32[512,128]{1,0:T(8,128)S(1)}, u32[]{:S(2)}, u32[]{:S(2)}) collective-permute-start(f32[512,128]{1,0:T(8,128)S(1)} %get-tuple-element.42.final_ref), channel_id=1, source_target_pairs={{4,0},{1,5},{14,10},{11,15},{0,2},{5,7},{10,8},{15,13},{20,16},{17... | collective-permute-start | bytes 786440 | tf_op jit(solution)/shard_map/ppermute | solution.py:38
  21.9 12.2 %collective-permute-start.10 = (f32[512,128]{1,0:T(8,128)S(1)}, f32[512,128]{1,0:T(8,128)S(1)}, u32[]{:S(2)}, u32[]{:S(2)}) collective-permute-start(f32[512,128]{1,0:T(8,128)S(1)} %get-tuple-element.42.final_ref), channel_id=1, source_target_pairs={{4,2},{1,7},{14,8},{11,13},{20,18},{17,23},{30,24},{27,29}} | collective-permute-start | bytes 786440 | tf_op jit(solution)/shard_map/ppermute | solution.py:38
  32.7 2.8 %collective-permute-start.6 = (f32[512,128]{1,0:T(8,128)S(1)}, f32[512,128]{1,0:T(8,128)S(1)}, u32[]{:S(2)}, u32[]{:S(2)}) collective-permute-start(f32[512,128]{1,0:T(8,128)S(1)} %get-tuple-element.37.final_ref), channel_id=1, source_target_pairs={{4,0},{1,5},{14,10},{11,15},{0,2},{5,7},{10,8},{15,13},{20,16},{17... | collective-permute-start | bytes 786440 | tf_op jit(solution)/shard_map/ppermute | solution.py:38
  33.4 2.1 %collective-permute-start.7 = (f32[512,128]{1,0:T(8,128)S(1)}, f32[512,128]{1,0:T(8,128)S(1)}, u32[]{:S(2)}, u32[]{:S(2)}) collective-permute-start(f32[512,128]{1,0:T(8,128)S(1)} %get-tuple-element.37.final_ref), channel_id=1, source_target_pairs={{4,2},{1,7},{14,8},{11,13},{20,18},{17,23},{30,24},{27,29}} | collective-permute-start | bytes 786440 | tf_op jit(solution)/shard_map/ppermute | solution.py:38
  34.2 41.2 %collective-permute-start.11 = (f32[2,512,128]{2,1,0:T(8,128)S(1)}, f32[2,512,128]{2,1,0:T(8,128)S(1)}, u32[]{:S(2)}, u32[]{:S(2)}) collective-permute-start(f32[2,512,128]{2,1,0:T(8,128)S(1)} %shard_map.170.mine_ref), channel_id=1, source_target_pairs={{0,1},{2,3},{5,4},{7,6},{10,11},{8,9},{15,14},{13,12},{16,17},{18,... | collective-permute-start | bytes 1572872 | tf_op jit(solution)/shard_map/ppermute | solution.py:38
  35.6 40.8 %collective-permute-start.8 = (f32[2,512,128]{2,1,0:T(8,128)S(1)}, f32[2,512,128]{2,1,0:T(8,128)S(1)}, u32[]{:S(2)}, u32[]{:S(2)}) collective-permute-start(f32[2,512,128]{2,1,0:T(8,128)S(1)} %shard_map.166.mine_ref), channel_id=1, source_target_pairs={{0,1},{2,3},{5,4},{7,6},{10,11},{8,9},{15,14},{13,12},{16,17},{18,... | collective-permute-start | bytes 1572872 | tf_op jit(solution)/shard_map/ppermute | solution.py:38
  36.9 34.4 %collective-permute-start.5 = (f32[512,128]{1,0:T(8,128)S(1)}, f32[512,128]{1,0:T(8,128)S(1)}, u32[]{:S(2)}, u32[]{:S(2)}) collective-permute-start(f32[512,128]{1,0:T(8,128)S(1)} %get-tuple-element.36), channel_id=1, source_target_pairs={{8,12},{12,8},{0,4},{9,13},{13,9},{1,5},{10,14},{14,10},{2,6},{11,... | collective-permute-start | bytes 786440 | tf_op jit(solution)/shard_map/ppermute | solution.py:38
  52.7 20.7 %collective-permute-start.2 = (f32[512,128]{1,0:T(8,128)S(1)}, f32[512,128]{1,0:T(8,128)S(1)}, u32[]{:S(2)}, u32[]{:S(2)}) collective-permute-start(f32[512,128]{1,0:T(8,128)S(1)} %get-tuple-element.29), channel_id=1, source_target_pairs={{8,12},{12,8},{0,4},{9,13},{13,9},{1,5},{10,14},{14,10},{2,6},{11,... | collective-permute-start | bytes 786440 | tf_op jit(solution)/shard_map/ppermute | solution.py:38

commit v4 on v3

--- a/solution.py
+++ b/solution.py
@@ -11,7 +11,7 @@
 LANES = 128
 SUB = 8
 HALVES = 2
-SHORT = 2
+SHARE = 3 / 8
 INNER = 4
 F32 = jnp.float32
 BF16 = jnp.bfloat16
@@ -242,30 +242,19 @@
         combine(before_now, keep_ref, hand_ref, count, width, decay=False)
 
 
-def output_kernel(own_ref, other_ref, queries_ref, grown_ref, inner_ref, *refs, offset, width):
-    out_hbm, held, sent = refs[-3:]
-    lanes = own_ref.shape[0]
+def output_kernel(*refs, parts, width):
+    states, (queries_ref, grown_ref, inner_ref, *_, out_hbm, held, sent) = refs[: len(parts)], refs[len(parts) :]
     copies = []
-    for half in range(HALVES):
-        columns = slice(half * out_hbm.shape[1] // HALVES + offset * width, None)
-        columns = slice(columns.start, columns.start + lanes)
-
-        def emit(state_ref):
-            carried = lax.dot_general(queries_ref[...], state_ref[...].astype(BF16), NT, preferred_element_type=F32)
-            held[half] = (inner_ref[:, columns] + carried * grown_ref[:, columns]).astype(BF16)
-
-        mine = rank_bit(0) == half
-
-        @pl.when(mine)
-        def _():
-            emit(own_ref)
-
-        @pl.when(jnp.logical_not(mine))
-        def _():
-            emit(other_ref)
-
-        copies.append(pltpu.make_async_copy(held.at[half], out_hbm.at[:, pl.ds(columns.start, lanes)], sent.at[half]))
+    done = 0
+    for k, ((kept, offset), state_ref) in enumerate(zip(parts, states, strict=True)):
+        lanes = state_ref.shape[0]
+        start = (half_start(kept, out_hbm.shape[1] // width) + offset) * width
+        columns = pl.ds(pl.multiple_of(start, LANES), lanes)
+        carried = lax.dot_general(queries_ref[...], state_ref[...].astype(BF16), NT, preferred_element_type=F32)
+        held[:, done : done + lanes] = (inner_ref[:, columns] + carried * grown_ref[:, columns]).astype(BF16)
+        copies.append(pltpu.make_async_copy(held.at[:, done : done + lanes], out_hbm.at[:, columns], sent.at[k]))
         copies[-1].start()
+        done += lanes
     for copy in copies:
         copy.wait()
 
@@ -456,7 +445,9 @@
     wide = step_values.shape[2]
     own_heads = wide // width
     half_heads = heads // HALVES
-    counts = (half_heads // SHORT, half_heads - half_heads // SHORT)
+    unit = LANES // width
+    first_count = int(half_heads // unit * SHARE) * unit
+    counts = (first_count, half_heads - first_count)
     offsets = (0, counts[0])
     array = lambda *shape, dtype=F32: jax.ShapeDtypeStruct(shape, dtype)
     messages = [array(count * width + -(-count // SUB) * SUB, LANES) for count in counts]
@@ -530,8 +521,8 @@
     )
 
     direct = ranks == slots
-    out = states = step_out = None
-    finals = []
+    states = step_out = None
+    finals, owns, backs = [], [], []
     for sub, count in enumerate(counts):
         sizes = dict(count=count, width=width)
         rows, message = count * width, messages[sub]
@@ -559,8 +550,11 @@
             far = slots // HALVES
             near = [((g ^ 1) * slots + g, g * slots + g) for g in range(ranks)]
             near += [(g * slots + g, g * slots + (g ^ far)) for g in range(ranks)]
-            across = permute(final, ("seq", "beam"), [((g ^ 1) * slots + g, g * slots + (g ^ far)) for g in range(ranks)])
             came = permute(final, ("seq", "beam"), near)
+            if sub == 0:
+                across = permute(came, ("seq", "beam"), [(g * slots + g, g * slots + (g ^ far)) for g in range(ranks)])
+            else:
+                across = permute(final, ("seq", "beam"), [((g ^ 1) * slots + g, g * slots + (g ^ far)) for g in range(ranks)])
             full = call(whole_kernel, (final, came, across), array(HALVES, rows, LANES), [VMEM] * 3)
             bit = 1
             while bit < far:
@@ -577,16 +571,23 @@
             states, step_out = emit_states(
                 full, offsets[sub], count, width, lines, (states, step_out) if sub else None, sub == 1
             )
-        given = () if out is None else (out,)
-        out = call(
-            functools.partial(output_kernel, offset=offsets[sub], width=width),
-            (own, back, prompt_queries, grown, inner) + given,
+        owns.append(own)
+        backs.append(back)
+
+    def outputs(states, parts, given):
+        lanes = sum(state.shape[0] for state in states)
+        return call(
+            functools.partial(output_kernel, parts=parts, width=width),
+            (*states, prompt_queries, grown, inner) + given,
             array(tokens, heads * width, dtype=BF16),
-            [VMEM] * 5 + [HBM] * len(given),
+            [VMEM] * (len(states) + 3) + [HBM] * len(given),
             out_specs=HBM,
-            scratch_shapes=[pltpu.VMEM((HALVES, tokens, rows), BF16), pltpu.SemaphoreType.DMA((HALVES,))],
-            input_output_aliases={5: 0} if given else {},
+            scratch_shapes=[pltpu.VMEM((tokens, lanes), BF16), pltpu.SemaphoreType.DMA((len(states),))],
+            input_output_aliases={len(states) + 3: 0} if given else {},
         )
+
+    out = outputs((*owns, backs[0]), ((True, offsets[0]), (True, offsets[1]), (False, offsets[0])), ())
+    out = outputs((backs[1],), ((False, offsets[1]),), (out,))
     if not direct:
         half = jnp.concatenate(finals)
         other = lax.ppermute(half, "seq", swap)

time: 78.4 us -> 85 us (1.084)
  the two profiles are of different devices: /device:TPU:21 before, /device:TPU:17 now
where the time goes in v4:
time: 85 us; the launch traced here: 84.5 us
  starting transfers between devices  30.8 us (36%)
  waiting for transfers between devices  24.8 us (29%)
  Pallas kernels  18.8 us (22%)
  blocking collectives  7.78 us (9%)
  between operations  2.27 us (3%)
    ppermute x12, starting transfers between devices, permute(): return lax.ppermute(array, axis, pairs)  30.8 us
    ppermute x12, waiting for transfers between devices, permute(): return lax.ppermute(array, axis, pairs)  24.8 us
    pallas_call x18, Pallas kernels, call(): pl.pallas_call(body, out_shape=out_shape, in_specs=in_specs, cost_estimat...  18.8 us
    all_gather x1, blocking collectives, gather(): return lax.all_gather(array, 'beam', axis=0, tiled=True)  7.78 us
  transfers between devices with their start and end apart: 12, of which 4 were waited for; matrix products, arithmetic and copies ran while one was open for 0% of the time, Pallas kernels for 16%

profile of v4, /device:TPU:17, one launch (start us, length us, event | category | flops | bytes accessed | tf_op | source)
XLA Modules:
  0.0 84.5 jit_solution(14301025507174259392)
XLA Ops:
  0.6 1.6 %shard_map.156 = (f32[256,32]{1,0:T(8,128)S(1)}, f32[32,256]{1,0:T(8,128)S(1)}, f32[392,128]{1,0:T(8,128)S(1)}) custom-call(bf16[256,2048]{1,0:T(8,128)(2,1)} %values_hbm.7, bf16[256,128]{1,0:T(8,128)(2,1)} %keys_hbm.7, f32[32,256]{1,0:T(8,128)} %bitcast.27), custom_call_target="tpu_custom_call" | custom-call | flops 1000000 | bytes 1000000 | tf_op jit(solution)/shard_map/pallas_call | solution.py:27
  2.2 1.6 %shard_map.158 = f32[656,128]{1,0:T(8,128)S(1)} custom-call(bf16[256,2048]{1,0:T(8,128)(2,1)} %values_hbm.7, bf16[256,128]{1,0:T(8,128)(2,1)} %keys_hbm.7, f32[256,32]{1,0:T(8,128)S(1)} %get-tuple-element.26.sums_ref), custom_call_target="tpu_custom_call" | custom-call | flops 1000000 | bytes 1000000 | tf_op jit(solution)/shard_map/pallas_call | solution.py:27
  3.8 1.4 %collective-permute-start = (f32[656,128]{1,0:T(8,128)S(1)}, f32[656,128]{1,0:T(8,128)S(1)}, u32[]{:S(2)}, u32[]{:S(2)}) collective-permute-start(f32[656,128]{1,0:T(8,128)S(1)} %shard_map.158), channel_id=1, source_target_pairs={{0,4},{4,0},{8,12},{12,8},{1,5},{5,1},{9,13},{13,9},{2,6},{6,2},{1... | collective-permute-start | bytes 1007624 | tf_op jit(solution)/shard_map/ppermute | solution.py:38
  5.1 2.0 %shard_map.157 = (f32[392,128]{1,0:T(8,128)S(1)}, f32[656,128]{1,0:T(8,128)S(1)}) custom-call(bf16[256,2048]{1,0:T(8,128)(2,1)} %values_hbm.7, bf16[256,128]{1,0:T(8,128)(2,1)} %keys_hbm.7, f32[256,32]{1,0:T(8,128)S(1)} %get-tuple-element.26.sums_ref), custom_call_target="tpu_custom_call" | custom-call | flops 1000000 | bytes 1000000 | tf_op jit(solution)/shard_map/pallas_call | solution.py:27
  7.1 5.5 %collective-permute-done.got_ref.swap_ref = f32[656,128]{1,0:T(8,128)S(1)} collective-permute-done((f32[656,128]{1,0:T(8,128)S(1)}, f32[656,128]{1,0:T(8,128)S(1)}, u32[]{:S(2)}, u32[]{:S(2)}) %collective-permute-start) | collective-permute-done | bytes 335904 | tf_op jit(solution)/shard_map/ppermute | solution.py:38
  12.6 0.1 shard_map.159.total_ref
  12.7 0.2 collective-permute-start.1
  12.9 1.2 %collective-permute-start.3 = (f32[392,128]{1,0:T(8,128)S(1)}, f32[392,128]{1,0:T(8,128)S(1)}, u32[]{:S(2)}, u32[]{:S(2)}) collective-permute-start(f32[392,128]{1,0:T(8,128)S(1)} %get-tuple-element.33), channel_id=1, source_target_pairs={{0,4},{4,0},{8,12},{12,8},{1,5},{5,1},{9,13},{13,9},{2,6},{6,2},{1... | collective-permute-start | bytes 602120 | tf_op jit(solution)/shard_map/ppermute | solution.py:38
  14.1 10.8 %collective-permute-done.3.got_ref.swap_ref = f32[392,128]{1,0:T(8,128)S(1)} collective-permute-done((f32[392,128]{1,0:T(8,128)S(1)}, f32[392,128]{1,0:T(8,128)S(1)}, u32[]{:S(2)}, u32[]{:S(2)}) %collective-permute-start.3) | collective-permute-done | bytes 200736 | tf_op jit(solution)/shard_map/ppermute | solution.py:38
  24.9 0.0 copy-start
  25.0 0.0 copy-start.2
  25.0 0.0 copy-start.3
  25.0 0.0 copy-start.4
  25.0 0.0 copy-start.5
  25.0 0.0 copy-start.6
  25.0 0.3 collective-permute-start.4
  25.4 1.4 %collective-permute-done.1.got_ref = f32[656,128]{1,0:T(8,128)S(1)} collective-permute-done((f32[656,128]{1,0:T(8,128)S(1)}, f32[656,128]{1,0:T(8,128)S(1)}, u32[]{:S(2)}, u32[]{:S(2)}) %collective-permute-start.1) | collective-permute-done | bytes 335904 | tf_op jit(solution)/shard_map/ppermute | solution.py:38
  26.8 0.1 shard_map.160
  26.9 0.0 copy-start.1
  26.9 0.7 collective-permute-start.6
  27.6 0.7 collective-permute-start.7
  28.3 7.1 %collective-permute-done.4.got_ref = f32[392,128]{1,0:T(8,128)S(1)} collective-permute-done((f32[392,128]{1,0:T(8,128)S(1)}, f32[392,128]{1,0:T(8,128)S(1)}, u32[]{:S(2)}, u32[]{:S(2)}) %collective-permute-start.4) | collective-permute-done | bytes 200736 | tf_op jit(solution)/shard_map/ppermute | solution.py:38
  35.4 0.1 shard_map.163
  35.5 0.7 collective-permute-start.9
  36.2 0.0 collective-permute-done.6.next_ref
  36.2 0.0 collective-permute-done.7.far_ref
  36.2 0.1 shard_map.166.mine_ref
  36.3 1.3 %collective-permute-start.8 = (f32[2,640,128]{2,1,0:T(8,128)S(1)}, f32[2,640,128]{2,1,0:T(8,128)S(1)}, u32[]{:S(2)}, u32[]{:S(2)}) collective-permute-start(f32[2,640,128]{2,1,0:T(8,128)S(1)} %shard_map.166.mine_ref), channel_id=1, source_target_pairs={{0,1},{2,3},{5,4},{7,6},{10,11},{8,9},{15,14},{13,12},{16,17},{18,... | collective-permute-start | bytes 1966088 | tf_op jit(solution)/shard_map/ppermute | solution.py:38
  37.6 0.0 collective-permute-done.9.next_ref
  37.6 0.7 collective-permute-start.10
  38.3 0.0 collective-permute-done.10.far_ref
  38.3 0.1 shard_map.170.mine_ref
  38.3 1.3 %collective-permute-start.11 = (f32[2,384,128]{2,1,0:T(8,128)S(1)}, f32[2,384,128]{2,1,0:T(8,128)S(1)}, u32[]{:S(2)}, u32[]{:S(2)}) collective-permute-start(f32[2,384,128]{2,1,0:T(8,128)S(1)} %shard_map.170.mine_ref), channel_id=1, source_target_pairs={{0,1},{2,3},{5,4},{7,6},{10,11},{8,9},{15,14},{13,12},{16,17},{18,... | collective-permute-start | bytes 1179656 | tf_op jit(solution)/shard_map/ppermute | solution.py:38
  39.6 20.5 %collective-permute-start.2 = (f32[640,128]{1,0:T(8,128)S(1)}, f32[640,128]{1,0:T(8,128)S(1)}, u32[]{:S(2)}, u32[]{:S(2)}) collective-permute-start(f32[640,128]{1,0:T(8,128)S(1)} %get-tuple-element.28), channel_id=1, source_target_pairs={{8,12},{12,8},{0,4},{9,13},{13,9},{1,5},{10,14},{14,10},{2,6},{11,... | collective-permute-start | bytes 983048 | tf_op jit(solution)/shard_map/ppermute | solution.py:38
  60.1 1.9 %collective-permute-start.5 = (f32[384,128]{1,0:T(8,128)S(1)}, f32[384,128]{1,0:T(8,128)S(1)}, u32[]{:S(2)}, u32[]{:S(2)}) collective-permute-start(f32[384,128]{1,0:T(8,128)S(1)} %get-tuple-element.36), channel_id=1, source_target_pairs={{8,12},{12,8},{0,4},{9,13},{13,9},{1,5},{10,14},{14,10},{2,6},{11,... | collective-permute-start | bytes 589832 | tf_op jit(solution)/shard_map/ppermute | solution.py:38
  63.4 0.2 shard_map.168
  63.6 7.8 %all_gather.3 = f32[544,128]{1,0:T(8,128)S(1)} all-gather(f32[136,128]{1,0:T(8,128)S(1)} %shard_map.168), channel_id=1, replica_groups=mesh['groups'=2,'seq'=4,'beam'=4] {'beam'}, dimensions={0}, use_global_device_ids=true | all-gather | bytes 348160 | tf_op jit(solution)/shard_map/all_gather | solution.py:42
  71.4 1.7 %shard_map.169 = (f32[8,2048]{1,0:T(8,128)S(1)}, f32[8,2048]{1,0:T(8,128)S(1)}, f32[2048,128]{1,0:T(8,128)S(1)}, f32[32,128]{1,0:T(8,128)S(1)}, f32[1,4]{1,0:T(1,128)}) custom-call(f32[4,136,128]{2,1,0:T(8,128)S(1)} %bitcast.16, bf16[4,128]{1,0:T(4,128)(2,1)S(1)} %bitcast.18), custom_call_target="tpu_custom_call" | custom-call | flops 1000000 | bytes 1000000 | tf_op jit(solution)/shard_map/pallas_call | solution.py:27
  73.1 5.0 %shard_map.161 = (f32[256,2048]{1,0:T(8,128)S(1)}, f32[256,2048]{1,0:T(8,128)S(1)}) custom-call(bf16[256,2048]{1,0:T(8,128)(2,1)} %values_hbm.7, bf16[256,128]{1,0:T(8,128)(2,1)} %keys_hbm.7, bf16[256,128]{1,0:T(8,128)(2,1)} %refs_1_.1, f32[256,32]{1,0:T(8,128)S(1)} %get-tuple-element.26.sums_ref, f32[32,256]{1,0:T(8,128)S(1)} %get-tuple-element.29.turned_ref), custom_call_target="tpu_custom_call" | custom-call | flops 100000000 | bytes 1000000 | tf_op jit(solution)/shard_map/pallas_call | solution.py:27
  78.1 0.0 collective-permute-done.5.refs_2_
  78.1 2.0 %shard_map.164.refs_4_ = bf16[256,2048]{1,0:T(8,128)(2,1)} custom-call(f32[384,128]{1,0:T(8,128)S(1)} %get-tuple-element.34.refs_0_, f32[640,128]{1,0:T(8,128)S(1)} %get-tuple-element.35.refs_1_, f32[384,128]{1,0:T(8,128)S(1)} %collective-permute-done.5.refs_2_, bf16[256,128]{1,0:T(8,128)(2,1)} %refs_1_.1, ...), custom_call_target="tpu_custom_call" | custom-call | flops 1000000 | bytes 1000000 | tf_op jit(solution)/shard_map/pallas_call | solution.py:27
  80.0 0.0 collective-permute-done.2.refs_0_
  80.0 1.8 %shard_map.165 = bf16[256,2048]{1,0:T(8,128)(2,1)} custom-call(f32[640,128]{1,0:T(8,128)S(1)} %collective-permute-done.2.refs_0_, bf16[256,128]{1,0:T(8,128)(2,1)} %refs_1_.1, f32[256,2048]{1,0:T(8,128)S(1)} %get-tuple-element.30.refs_4_.refs_2_, f32[256,2048]{1,0:T(8,128)S(1)} %get-tuple-element.31.refs_5_.refs_3_, ...), custom_call_target="tpu_custom_call", output_to_operand_aliasing={{}: (4, {})} | custom-call | flops 1000000 | bytes 1000000 | tf_op jit(solution)/shard_map/pallas_call | solution.py:27
  81.9 0.0 collective-permute-done.11.got_ref
  82.0 0.8 %shard_map.172 = (f32[2048,128]{1,0:T(8,128)}, bf16[4,768]{1,0:T(4,128)(2,1)S(1)}) custom-call(f32[2,384,128]{2,1,0:T(8,128)S(1)} %shard_map.171.final_ref, bf16[4,128]{1,0:T(4,128)(2,1)S(1)} %bitcast.19, f32[8,2048]{1,0:T(8,128)S(1)} %get-tuple-element.38.grow_ref, f32[8,2048]{1,0:T(8,128)S(1)} %get-tuple-element.39.part_ref, ...), custom_call_target="tpu_custom_call" | custom-call | flops 1000000 | bytes 1000000 | tf_op jit(solution)/shard_map/pallas_call | solution.py:27
  82.8 0.0 collective-permute-done.8.got_ref
  82.8 0.1 shard_map.167.final_ref
  82.9 1.6 %shard_map.173 = (f32[2048,128]{1,0:T(8,128)}, bf16[4,2048]{1,0:T(4,128)(2,1)}) custom-call(f32[2,640,128]{2,1,0:T(8,128)S(1)} %shard_map.167.final_ref, bf16[4,128]{1,0:T(4,128)(2,1)S(1)} %bitcast.20, f32[8,2048]{1,0:T(8,128)S(1)} %get-tuple-element.38.grow_ref, f32[8,2048]{1,0:T(8,128)S(1)} %get-tuple-element.39.part_ref, ...), custom_call_target="tpu_custom_call", output_to_operand_aliasing={{0}: (7, {})} | custom-call | flops 1000000 | bytes 1000000 | tf_op jit(solution)/shard_map/pallas_call | solution.py:27
  (9 shorter events, 0.1 us)
Async XLA Ops:
  3.8 8.8 %collective-permute-start = (f32[656,128]{1,0:T(8,128)S(1)}, f32[656,128]{1,0:T(8,128)S(1)}, u32[]{:S(2)}, u32[]{:S(2)}) collective-permute-start(f32[656,128]{1,0:T(8,128)S(1)} %shard_map.158), channel_id=1, source_target_pairs={{0,4},{4,0},{8,12},{12,8},{1,5},{5,1},{9,13},{13,9},{2,6},{6,2},{1... | collective-permute-start | bytes 1007624 | tf_op jit(solution)/shard_map/ppermute | solution.py:38
  12.7 14.1 %collective-permute-start.1 = (f32[656,128]{1,0:T(8,128)S(1)}, f32[656,128]{1,0:T(8,128)S(1)}, u32[]{:S(2)}, u32[]{:S(2)}) collective-permute-start(f32[656,128]{1,0:T(8,128)S(1)} %shard_map.159.total_ref), channel_id=1, source_target_pairs={{0,8},{4,12},{8,0},{12,4},{1,9},{5,13},{9,1},{13,5},{2,10},{6,14},... | collective-permute-start | bytes 1007624 | tf_op jit(solution)/shard_map/ppermute | solution.py:38
  12.9 12.0 %collective-permute-start.3 = (f32[392,128]{1,0:T(8,128)S(1)}, f32[392,128]{1,0:T(8,128)S(1)}, u32[]{:S(2)}, u32[]{:S(2)}) collective-permute-start(f32[392,128]{1,0:T(8,128)S(1)} %get-tuple-element.33), channel_id=1, source_target_pairs={{0,4},{4,0},{8,12},{12,8},{1,5},{5,1},{9,13},{13,9},{2,6},{6,2},{1... | collective-permute-start | bytes 602120 | tf_op jit(solution)/shard_map/ppermute | solution.py:38
  24.9 38.4 %copy-start = (bf16[4,1,2048]{2,0,1:T(4,128)(2,1)S(1)}, bf16[4,1,2048]{2,0,1:T(4,128)(2,1)}, u32[]{:S(2)}) copy-start(bf16[4,1,2048]{2,0,1:T(4,128)(2,1)} %param.17) | copy-start | bytes 49156
  25.0 38.4 %copy-start.2 = (f32[4,1,32]{2,1,0:T(1,128)S(1)}, f32[4,1,32]{2,1,0:T(1,128)}, u32[]{:S(2)}) copy-start(f32[4,1,32]{2,1,0:T(1,128)} %param.20) | copy-start | bytes 1540
  25.0 38.4 %copy-start.3 = (bf16[4,1,128]{2,0,1:T(4,128)(2,1)S(1)}, bf16[4,1,128]{2,0,1:T(4,128)(2,1)}, u32[]{:S(2)}) copy-start(bf16[4,1,128]{2,0,1:T(4,128)(2,1)} %param.18) | copy-start | bytes 3076
  25.0 38.4 %copy-start.4 = (f32[4,1]{0,1:T(1,128)S(1)}, f32[4,1]{0,1:T(1,128)}, u32[]{:S(2)}) copy-start(f32[4,1]{0,1:T(1,128)} %param.21) | copy-start | bytes 52
  25.0 38.4 %copy-start.5 = (s32[4,1]{0,1:T(1,128)S(1)}, s32[4,1]{0,1:T(1,128)}, u32[]{:S(2)}) copy-start(s32[4,1]{0,1:T(1,128)} %param.22) | copy-start | bytes 52
  25.0 38.4 %copy-start.6 = (s32[4,1]{0,1:T(1,128)S(1)}, s32[4,1]{0,1:T(1,128)}, u32[]{:S(2)}) copy-start(s32[4,1]{0,1:T(1,128)} %param.23) | copy-start | bytes 52
  25.0 10.4 %collective-permute-start.4 = (f32[392,128]{1,0:T(8,128)S(1)}, f32[392,128]{1,0:T(8,128)S(1)}, u32[]{:S(2)}, u32[]{:S(2)}) collective-permute-start(f32[392,128]{1,0:T(8,128)S(1)} %shard_map.162.total_ref), channel_id=1, source_target_pairs={{0,8},{4,12},{8,0},{12,4},{1,9},{5,13},{9,1},{13,5},{2,10},{6,14},... | collective-permute-start | bytes 602120 | tf_op jit(solution)/shard_map/ppermute | solution.py:38
  26.9 44.5 %copy-start.1 = (bf16[4,1,128]{2,0,1:T(4,128)(2,1)S(1)}, bf16[4,1,128]{2,0,1:T(4,128)(2,1)}, u32[]{:S(2)}) copy-start(bf16[4,1,128]{2,0,1:T(4,128)(2,1)} %param.19) | copy-start | bytes 3076
  26.9 9.2 %collective-permute-start.6 = (f32[640,128]{1,0:T(8,128)S(1)}, f32[640,128]{1,0:T(8,128)S(1)}, u32[]{:S(2)}, u32[]{:S(2)}) collective-permute-start(f32[640,128]{1,0:T(8,128)S(1)} %get-tuple-element.37.final_ref), channel_id=1, source_target_pairs={{4,0},{1,5},{14,10},{11,15},{0,2},{5,7},{10,8},{15,13},{20,16},{17... | collective-permute-start | bytes 983048 | tf_op jit(solution)/shard_map/ppermute | solution.py:38
  27.6 8.5 %collective-permute-start.7 = (f32[640,128]{1,0:T(8,128)S(1)}, f32[640,128]{1,0:T(8,128)S(1)}, u32[]{:S(2)}, u32[]{:S(2)}) collective-permute-start(f32[640,128]{1,0:T(8,128)S(1)} %get-tuple-element.37.final_ref), channel_id=1, source_target_pairs={{4,2},{1,7},{14,8},{11,13},{20,18},{17,23},{30,24},{27,29}} | collective-permute-start | bytes 983048 | tf_op jit(solution)/shard_map/ppermute | solution.py:38
  35.5 2.1 %collective-permute-start.9 = (f32[384,128]{1,0:T(8,128)S(1)}, f32[384,128]{1,0:T(8,128)S(1)}, u32[]{:S(2)}, u32[]{:S(2)}) collective-permute-start(f32[384,128]{1,0:T(8,128)S(1)} %get-tuple-element.42.final_ref), channel_id=1, source_target_pairs={{4,0},{1,5},{14,10},{11,15},{0,2},{5,7},{10,8},{15,13},{20,16},{17... | collective-permute-start | bytes 589832 | tf_op jit(solution)/shard_map/ppermute | solution.py:38
  36.3 46.6 %collective-permute-start.8 = (f32[2,640,128]{2,1,0:T(8,128)S(1)}, f32[2,640,128]{2,1,0:T(8,128)S(1)}, u32[]{:S(2)}, u32[]{:S(2)}) collective-permute-start(f32[2,640,128]{2,1,0:T(8,128)S(1)} %shard_map.166.mine_ref), channel_id=1, source_target_pairs={{0,1},{2,3},{5,4},{7,6},{10,11},{8,9},{15,14},{13,12},{16,17},{18,... | collective-permute-start | bytes 1966088 | tf_op jit(solution)/shard_map/ppermute | solution.py:38
  37.6 0.7 collective-permute-start.10
  38.3 43.6 %collective-permute-start.11 = (f32[2,384,128]{2,1,0:T(8,128)S(1)}, f32[2,384,128]{2,1,0:T(8,128)S(1)}, u32[]{:S(2)}, u32[]{:S(2)}) collective-permute-start(f32[2,384,128]{2,1,0:T(8,128)S(1)} %shard_map.170.mine_ref), channel_id=1, source_target_pairs={{0,1},{2,3},{5,4},{7,6},{10,11},{8,9},{15,14},{13,12},{16,17},{18,... | collective-permute-start | bytes 1179656 | tf_op jit(solution)/shard_map/ppermute | solution.py:38
  39.6 40.4 %collective-permute-start.2 = (f32[640,128]{1,0:T(8,128)S(1)}, f32[640,128]{1,0:T(8,128)S(1)}, u32[]{:S(2)}, u32[]{:S(2)}) collective-permute-start(f32[640,128]{1,0:T(8,128)S(1)} %get-tuple-element.28), channel_id=1, source_target_pairs={{8,12},{12,8},{0,4},{9,13},{13,9},{1,5},{10,14},{14,10},{2,6},{11,... | collective-permute-start | bytes 983048 | tf_op jit(solution)/shard_map/ppermute | solution.py:38
  60.1 18.0 %collective-permute-start.5 = (f32[384,128]{1,0:T(8,128)S(1)}, f32[384,128]{1,0:T(8,128)S(1)}, u32[]{:S(2)}, u32[]{:S(2)}) collective-permute-start(f32[384,128]{1,0:T(8,128)S(1)} %get-tuple-element.36), channel_id=1, source_target_pairs={{8,12},{12,8},{0,4},{9,13},{13,9},{1,5},{10,14},{14,10},{2,6},{11,... | collective-permute-start | bytes 589832 | tf_op jit(solution)/shard_map/ppermute | solution.py:38

commit v5 on v4

--- a/solution.py
+++ b/solution.py
@@ -246,15 +246,21 @@
     states, (queries_ref, grown_ref, inner_ref, *_, out_hbm, held, sent) = refs[: len(parts)], refs[len(parts) :]
     copies = []
     done = 0
-    for k, ((kept, offset), state_ref) in enumerate(zip(parts, states, strict=True)):
-        lanes = state_ref.shape[0]
-        start = (half_start(kept, out_hbm.shape[1] // width) + offset) * width
-        columns = pl.ds(pl.multiple_of(start, LANES), lanes)
-        carried = lax.dot_general(queries_ref[...], state_ref[...].astype(BF16), NT, preferred_element_type=F32)
-        held[:, done : done + lanes] = (inner_ref[:, columns] + carried * grown_ref[:, columns]).astype(BF16)
-        copies.append(pltpu.make_async_copy(held.at[:, done : done + lanes], out_hbm.at[:, columns], sent.at[k]))
-        copies[-1].start()
-        done += lanes
+    for (kept, offset), state_ref in zip(parts, states, strict=True):
+        base = half_start(kept, out_hbm.shape[1] // width) * width
+        cut = state_ref.shape[0] // 2 // LANES * LANES
+        for first, lanes in ((0, cut), (cut, state_ref.shape[0] - cut)):
+            if lanes == 0:
+                continue
+            columns = pl.ds(pl.multiple_of(base + offset * width + first, LANES), lanes)
+            state = state_ref[first : first + lanes, :].astype(BF16)
+            carried = lax.dot_general(queries_ref[...], state, NT, preferred_element_type=F32)
+            held[:, done : done + lanes] = (inner_ref[:, columns] + carried * grown_ref[:, columns]).astype(BF16)
+            copies.append(
+                pltpu.make_async_copy(held.at[:, done : done + lanes], out_hbm.at[:, columns], sent.at[len(copies)])
+            )
+            copies[-1].start()
+            done += lanes
     for copy in copies:
         copy.wait()
 
@@ -312,21 +318,33 @@
         out_ref[...] = got_ref[...]
 
 
-def lineage_kernel(
-    rows_ref, queries_ref, grow_ref, part_ref, fresh_ref, shrink_ref, ranked_ref,
-    outer_ref, key_ref, scores, counts, scalar_ref, arrived, *, slots, steps, wide, width
-):
-    (copy,) = fetch(arrived, (rows_ref.at[:, pl.ds(0, 2 * steps), :], scalar_ref))
-    copy.wait()
+def stack_kernel(*refs):
+    *parts, out_ref = refs
+    done = 0
+    for part in parts:
+        out_ref[done : done + part.shape[0]] = part[...]
+        done += part.shape[0]
+
+
+def lineage_kernel(*refs, offsets, slots, steps, wide, width):
+    blocks, refs = refs[: len(offsets)], refs[len(offsets) :]
+    queries_ref, grow_ref, part_ref, fresh_ref, shrink_ref, ranked_ref = refs[:6]
+    outer_ref, key_ref, scores, counts, scalar_ref, rows_ref, arrived = refs[6:]
+    places = [(block, k, away) for block, some in zip(blocks, offsets, strict=True) for k, away in enumerate(some)]
+    copies = fetch(arrived, *((block.at[k, pl.ds(0, 2 * steps), :], scalar_ref.at[away]) for block, k, away in places))
+    for block, k, away in places:
+        rows_ref[away] = block[k]
+    for copy in copies:
+        copy.wait()
     lines = wide // LANES
     flat = lambda x: jnp.concatenate([x[k : k + 1, :] for k in range(lines)], axis=1)
     me = lax.axis_index("beam")
     ranks_row = jnp.zeros((1, LANES), F32)
-    done = lambda slot, step: scalar_ref[slot, step, 2]
-    parent = lambda slot, step: scalar_ref[slot, step, 1].astype(jnp.int32)
+    done = lambda slot, step: scalar_ref[slot ^ me, step, 2]
+    parent = lambda slot, step: scalar_ref[slot ^ me, step, 1].astype(jnp.int32)
     for slot in range(slots):
-        scores[0, slot] = scalar_ref[slot, 0, 4]
-        counts[0, slot] = scalar_ref[slot, 0, 3]
+        scores[0, slot] = scalar_ref[slot ^ me, 0, 4]
+        counts[0, slot] = scalar_ref[slot ^ me, 0, 3]
     lane = iota((1, LANES), 1)
     for step in range(steps):
         score_row = jnp.zeros((1, LANES), F32)
@@ -334,7 +352,7 @@
         for slot in range(slots):
             source = parent(slot, step)
             live = 1.0 - done(slot, step)
-            score = scores[step, source] + live * scalar_ref[slot, step, 0]
+            score = scores[step, source] + live * scalar_ref[slot ^ me, step, 0]
             tally = counts[step, source] + live
             scores[step + 1, slot] = score
             counts[step + 1, slot] = tally
@@ -357,14 +375,14 @@
         for back in range(step, -1, -1):
             start = 2 * steps + back * 2 * lines
             live = 1.0 - done(slot, back)
-            values = rows_ref[slot, start : start + lines, :]
-            key = rows_ref[slot, steps + back : steps + back + 1, :]
+            values = rows_ref[slot ^ me, start : start + lines, :]
+            key = rows_ref[slot ^ me, steps + back : steps + back + 1, :]
             weight = factor * (values * live)
             part = part + weight * jnp.sum(key * query, axis=1, keepdims=True)
             if step == steps - 1:
                 outer_ref[back : back + 1, :] = flat(weight)
                 key_ref[back : back + 1, :] = key
-            factor = factor * jnp.exp(rows_ref[slot, start + lines : start + 2 * lines, :] * live)
+            factor = factor * jnp.exp(rows_ref[slot ^ me, start + lines : start + 2 * lines, :] * live)
             slot = parent(slot, back)
         grow_ref[step : step + 1, :] = flat(factor * live_now)
         part_ref[step : step + 1, :] = flat(part * live_now)
@@ -390,22 +408,24 @@
     copies = []
     for k in range(stretches):
         start = k * stretch + offset * width
-        final = final_ref[k]
-        product = lax.dot_general(queries_ref[...], final.astype(BF16), NT, preferred_element_type=F32)
+        for h in range(count):
+            inside = slice(h * width, (h + 1) * width)
+            head = start // width + h
+            held[k, inside, :] = (
+                shrink_ref[head : head + 1, :] * final_ref[k, inside, :]
+                + fresh_ref[start + h * width : start + (h + 1) * width, :]
+            )
+        copies.append(pltpu.make_async_copy(held.at[k], states_hbm.at[pl.ds(start, rows), :], sent.at[k]))
+        copies[-1].start()
+    for k in range(stretches):
+        start = k * stretch + offset * width
+        product = lax.dot_general(queries_ref[...], final_ref[k].astype(BF16), NT, preferred_element_type=F32)
         lanes = slice(start, start + rows)
         result = (grow_ref[0:steps, lanes] * product + part_ref[0:steps, lanes]).astype(BF16)
         if last:
             out_ref[:, lanes] = result
         else:
             out_ref[:, k * rows : (k + 1) * rows] = result
-        for h in range(count):
-            inside = slice(h * width, (h + 1) * width)
-            head = start // width + h
-            held[k, inside, :] = (
-                shrink_ref[head : head + 1, :] * final[inside, :] + fresh_ref[start + h * width : start + (h + 1) * width, :]
-            )
-        copies.append(pltpu.make_async_copy(held.at[k], states_hbm.at[pl.ds(start, rows), :], sent.at[k]))
-        copies[-1].start()
         if given:
             before = earlier_ref.shape[1] // stretches
             out_ref[:, k * stretch : k * stretch + before] = earlier_ref[:, k * before : (k + 1) * before]
@@ -448,7 +468,7 @@
     unit = LANES // width
     first_count = int(half_heads // unit * SHARE) * unit
     counts = (first_count, half_heads - first_count)
-    offsets = (0, counts[0])
+    starts = (0, counts[0])
     array = lambda *shape, dtype=F32: jax.ShapeDtypeStruct(shape, dtype)
     messages = [array(count * width + -(-count // SUB) * SUB, LANES) for count in counts]
     levels = ranks.bit_length() - 1
@@ -479,7 +499,7 @@
             ],
         )
 
-    (send_b,) = more_states(False, offsets[1], (1,))
+    (send_b,) = more_states(False, starts[1], (1,))
     got_b = permute(send_b, "seq", swap)
     keep_a, keep_b = more_states(True, 0, (0, 1))
     keeps, swaps = (keep_a, keep_b), (got_a, got_b)
@@ -495,15 +515,28 @@
     )
     queries = step_queries[:, 0]
 
+    blocks, offsets, bit = [packed[None]], [[0]], slots // 2
+    while bit:
+        if len(blocks) == 1:
+            have = blocks[0]
+        else:
+            have = call(
+                stack_kernel, blocks, array(sum(len(some) for some in offsets), *packed.shape),
+                [VMEM] * len(blocks),
+            )
+        blocks.append(permute(have, "beam", [(b, b ^ bit) for b in range(slots)]))
+        offsets.append([away ^ bit for some in offsets for away in some])
+        bit //= 2
     *lines, ranked = call(
-        functools.partial(lineage_kernel, slots=slots, steps=steps, wide=wide, width=width),
-        (gather(packed).reshape(slots, -1, LANES), queries),
+        functools.partial(lineage_kernel, offsets=offsets, slots=slots, steps=steps, wide=wide, width=width),
+        (*blocks, queries),
         (array(SUB, wide), array(SUB, wide), array(wide, LANES), array(own_heads, LANES), array(1, steps)),
-        [VMEM, VMEM],
+        [VMEM] * (len(blocks) + 1),
         scratch_shapes=[
             pltpu.VMEM((SUB, wide), F32), pltpu.VMEM((SUB, LANES), F32),
             pltpu.SMEM((steps + 1, slots), F32), pltpu.SMEM((steps + 1, slots), F32),
-            pltpu.SMEM((slots, 2 * steps, LANES), F32), pltpu.SemaphoreType.DMA((1,)),
+            pltpu.SMEM((slots, 2 * steps, LANES), F32), pltpu.VMEM((slots, *packed.shape), F32),
+            pltpu.SemaphoreType.DMA((slots,)),
         ],
     )
     lines, ranked = (queries, *lines), ranked.reshape(steps, 1)
@@ -569,7 +602,7 @@
         back = permute(hand, "seq", [(k, k ^ 1) for k in range(1, ranks) if k != 1] + [(0, 1)])
         if direct:
             states, step_out = emit_states(
-                full, offsets[sub], count, width, lines, (states, step_out) if sub else None, sub == 1
+                full, starts[sub], count, width, lines, (states, step_out) if sub else None, sub == 1
             )
         owns.append(own)
         backs.append(back)
@@ -582,12 +615,13 @@
             array(tokens, heads * width, dtype=BF16),
             [VMEM] * (len(states) + 3) + [HBM] * len(given),
             out_specs=HBM,
-            scratch_shapes=[pltpu.VMEM((tokens, lanes), BF16), pltpu.SemaphoreType.DMA((len(states),))],
+            scratch_shapes=[pltpu.VMEM((tokens, lanes), BF16), pltpu.SemaphoreType.DMA((2 * len(states),))],
             input_output_aliases={len(states) + 3: 0} if given else {},
         )
 
-    out = outputs((*owns, backs[0]), ((True, offsets[0]), (True, offsets[1]), (False, offsets[0])), ())
-    out = outputs((backs[1],), ((False, offsets[1]),), (out,))
+    out = outputs((owns[0], backs[0]), ((True, starts[0]), (False, starts[0])), ())
+    out = outputs((owns[1],), ((True, starts[1]),), (out,))
+    out = outputs((backs[1],), ((False, starts[1]),), (out,))
     if not direct:
         half = jnp.concatenate(finals)
         other = lax.ppermute(half, "seq", swap)
@@ -605,7 +639,7 @@
     def body(*args):
         return on_device(*args, ranks=ranks, slots=slots)
 
-    return jax.shard_map(
+    step = jax.shard_map(
         body,
         mesh=mesh,
         in_specs=(
@@ -631,3 +665,4 @@
         ),
         check_vma=False,
     )
+    return step if ranks == slots else step

time: 85 us -> 83.3 us (0.980)
  the two profiles are of different devices: /device:TPU:17 before, /device:TPU:25 now
where the time goes in v5:
time: 83.3 us; the launch traced here: 81.6 us
  waiting for transfers between devices  39 us (47%)
  Pallas kernels  20.5 us (25%)
  starting transfers between devices  19.8 us (24%)
  between operations  2.29 us (3%)
    ppermute x14, waiting for transfers between devices, permute(): return lax.ppermute(array, axis, pairs)  39 us
    pallas_call x20, Pallas kernels, call(): pl.pallas_call(body, out_shape=out_shape, in_specs=in_specs, cost_estimat...  20.5 us
    ppermute x14, starting transfers between devices, permute(): return lax.ppermute(array, axis, pairs)  19.8 us
  transfers between devices with their start and end apart: 14, of which 9 were waited for; matrix products, arithmetic and copies ran while one was open for 0% of the time, Pallas kernels for 19%

profile of v5, /device:TPU:25, one launch (start us, length us, event | category | flops | bytes accessed | tf_op | source)
XLA Modules:
  0.0 81.6 jit_solution(8771825439742150969)
XLA Ops:
  0.6 1.6 %shard_map.156 = (f32[256,32]{1,0:T(8,128)S(1)}, f32[32,256]{1,0:T(8,128)S(1)}, f32[392,128]{1,0:T(8,128)S(1)}) custom-call(bf16[256,2048]{1,0:T(8,128)(2,1)} %values_hbm.7, bf16[256,128]{1,0:T(8,128)(2,1)} %keys_hbm.7, f32[32,256]{1,0:T(8,128)} %bitcast.29), custom_call_target="tpu_custom_call" | custom-call | flops 1000000 | bytes 1000000 | tf_op jit(solution)/shard_map/pallas_call | solution.py:27
  2.2 1.6 %shard_map.158 = f32[656,128]{1,0:T(8,128)S(1)} custom-call(bf16[256,2048]{1,0:T(8,128)(2,1)} %values_hbm.7, bf16[256,128]{1,0:T(8,128)(2,1)} %keys_hbm.7, f32[256,32]{1,0:T(8,128)S(1)} %get-tuple-element.26.sums_ref), custom_call_target="tpu_custom_call" | custom-call | flops 1000000 | bytes 1000000 | tf_op jit(solution)/shard_map/pallas_call | solution.py:27
  3.8 0.2 collective-permute-start
  4.0 2.0 %shard_map.157 = (f32[392,128]{1,0:T(8,128)S(1)}, f32[656,128]{1,0:T(8,128)S(1)}) custom-call(bf16[256,2048]{1,0:T(8,128)(2,1)} %values_hbm.7, bf16[256,128]{1,0:T(8,128)(2,1)} %keys_hbm.7, f32[256,32]{1,0:T(8,128)S(1)} %get-tuple-element.26.sums_ref), custom_call_target="tpu_custom_call" | custom-call | flops 1000000 | bytes 1000000 | tf_op jit(solution)/shard_map/pallas_call | solution.py:27
  6.0 6.6 %collective-permute-done.got_ref.swap_ref = f32[656,128]{1,0:T(8,128)S(1)} collective-permute-done((f32[656,128]{1,0:T(8,128)S(1)}, f32[656,128]{1,0:T(8,128)S(1)}, u32[]{:S(2)}, u32[]{:S(2)}) %collective-permute-start) | collective-permute-done | bytes 335904 | tf_op jit(solution)/shard_map/ppermute | solution.py:38
  12.6 0.1 shard_map.159.total_ref
  12.7 0.1 collective-permute-start.1
  12.8 0.3 collective-permute-start.3
  13.1 9.8 %collective-permute-done.3.got_ref.swap_ref = f32[392,128]{1,0:T(8,128)S(1)} collective-permute-done((f32[392,128]{1,0:T(8,128)S(1)}, f32[392,128]{1,0:T(8,128)S(1)}, u32[]{:S(2)}, u32[]{:S(2)}) %collective-permute-start.3) | collective-permute-done | bytes 200736 | tf_op jit(solution)/shard_map/ppermute | solution.py:38
  22.9 0.0 copy-start
  22.9 0.0 copy-start.2
  22.9 0.0 copy-start.3
  23.0 0.0 copy-start.4
  23.0 0.0 copy-start.5
  23.0 0.0 copy-start.6
  23.0 3.3 %collective-permute-start.4 = (f32[392,128]{1,0:T(8,128)S(1)}, f32[392,128]{1,0:T(8,128)S(1)}, u32[]{:S(2)}, u32[]{:S(2)}) collective-permute-start(f32[392,128]{1,0:T(8,128)S(1)} %shard_map.162.total_ref), channel_id=1, source_target_pairs={{0,8},{4,12},{8,0},{12,4},{1,9},{5,13},{9,1},{13,5},{2,10},{6,14},... | collective-permute-start | bytes 602120 | tf_op jit(solution)/shard_map/ppermute | solution.py:38
  26.3 8.5 %collective-permute-done.1.got_ref = f32[656,128]{1,0:T(8,128)S(1)} collective-permute-done((f32[656,128]{1,0:T(8,128)S(1)}, f32[656,128]{1,0:T(8,128)S(1)}, u32[]{:S(2)}, u32[]{:S(2)}) %collective-permute-start.1) | collective-permute-done | bytes 335904 | tf_op jit(solution)/shard_map/ppermute | solution.py:38
  34.8 0.1 shard_map.160
  34.9 1.3 %collective-permute-start.6 = (f32[640,128]{1,0:T(8,128)S(1)}, f32[640,128]{1,0:T(8,128)S(1)}, u32[]{:S(2)}, u32[]{:S(2)}) collective-permute-start(f32[640,128]{1,0:T(8,128)S(1)} %get-tuple-element.37.final_ref), channel_id=1, source_target_pairs={{4,0},{1,5},{14,10},{11,15},{0,2},{5,7},{10,8},{15,13},{20,16},{17... | collective-permute-start | bytes 983048 | tf_op jit(solution)/shard_map/ppermute | solution.py:38
  36.2 1.3 %collective-permute-start.7 = (f32[640,128]{1,0:T(8,128)S(1)}, f32[640,128]{1,0:T(8,128)S(1)}, u32[]{:S(2)}, u32[]{:S(2)}) collective-permute-start(f32[640,128]{1,0:T(8,128)S(1)} %get-tuple-element.37.final_ref), channel_id=1, source_target_pairs={{4,2},{1,7},{14,8},{11,13},{20,18},{17,23},{30,24},{27,29}} | collective-permute-start | bytes 983048 | tf_op jit(solution)/shard_map/ppermute | solution.py:38
  37.5 1.6 %collective-permute-done.4.got_ref = f32[392,128]{1,0:T(8,128)S(1)} collective-permute-done((f32[392,128]{1,0:T(8,128)S(1)}, f32[392,128]{1,0:T(8,128)S(1)}, u32[]{:S(2)}, u32[]{:S(2)}) %collective-permute-start.4) | collective-permute-done | bytes 200736 | tf_op jit(solution)/shard_map/ppermute | solution.py:38
  39.1 0.1 shard_map.163
  39.2 0.0 copy-start.1
  39.2 1.3 %collective-permute-start.11 = (f32[384,128]{1,0:T(8,128)S(1)}, f32[384,128]{1,0:T(8,128)S(1)}, u32[]{:S(2)}, u32[]{:S(2)}) collective-permute-start(f32[384,128]{1,0:T(8,128)S(1)} %get-tuple-element.42.final_ref), channel_id=1, source_target_pairs={{4,0},{1,5},{14,10},{11,15},{0,2},{5,7},{10,8},{15,13},{20,16},{17... | collective-permute-start | bytes 589832 | tf_op jit(solution)/shard_map/ppermute | solution.py:38
  40.5 2.3 %collective-permute-done.6.next_ref = f32[640,128]{1,0:T(8,128)S(1)} collective-permute-done((f32[640,128]{1,0:T(8,128)S(1)}, f32[640,128]{1,0:T(8,128)S(1)}, u32[]{:S(2)}, u32[]{:S(2)}) %collective-permute-start.6) | collective-permute-done | bytes 327712 | tf_op jit(solution)/shard_map/ppermute | solution.py:38
  42.8 4.5 %collective-permute-done.7.far_ref = f32[640,128]{1,0:T(8,128)S(1)} collective-permute-done((f32[640,128]{1,0:T(8,128)S(1)}, f32[640,128]{1,0:T(8,128)S(1)}, u32[]{:S(2)}, u32[]{:S(2)}) %collective-permute-start.7) | collective-permute-done | bytes 327712 | tf_op jit(solution)/shard_map/ppermute | solution.py:38
  47.3 0.1 shard_map.167.mine_ref
  47.4 1.3 %collective-permute-start.8 = (f32[2,640,128]{2,1,0:T(8,128)S(1)}, f32[2,640,128]{2,1,0:T(8,128)S(1)}, u32[]{:S(2)}, u32[]{:S(2)}) collective-permute-start(f32[2,640,128]{2,1,0:T(8,128)S(1)} %shard_map.167.mine_ref), channel_id=1, source_target_pairs={{0,1},{2,3},{5,4},{7,6},{10,11},{8,9},{15,14},{13,12},{16,17},{18,... | collective-permute-start | bytes 1966088 | tf_op jit(solution)/shard_map/ppermute | solution.py:38
  48.7 0.4 collective-permute-done.11.next_ref
  49.1 1.3 %collective-permute-start.12 = (f32[384,128]{1,0:T(8,128)S(1)}, f32[384,128]{1,0:T(8,128)S(1)}, u32[]{:S(2)}, u32[]{:S(2)}) collective-permute-start(f32[384,128]{1,0:T(8,128)S(1)} %collective-permute-done.11.next_ref), channel_id=1, source_target_pairs={{0,2},{5,7},{10,8},{15,13},{16,18},{21,23},{26,24},{31,29}} | collective-permute-start | bytes 589832 | tf_op jit(solution)/shard_map/ppermute | solution.py:38
  50.4 5.1 %collective-permute-done.12.far_ref = f32[384,128]{1,0:T(8,128)S(1)} collective-permute-done((f32[384,128]{1,0:T(8,128)S(1)}, f32[384,128]{1,0:T(8,128)S(1)}, u32[]{:S(2)}, u32[]{:S(2)}) %collective-permute-start.12) | collective-permute-done | bytes 196640 | tf_op jit(solution)/shard_map/ppermute | solution.py:38
  55.6 1.3 %collective-permute-start.13 = (f32[2,384,128]{2,1,0:T(8,128)S(1)}, f32[2,384,128]{2,1,0:T(8,128)S(1)}, u32[]{:S(2)}, u32[]{:S(2)}) collective-permute-start(f32[2,384,128]{2,1,0:T(8,128)S(1)} %shard_map.172.mine_ref), channel_id=1, source_target_pairs={{0,1},{2,3},{5,4},{7,6},{10,11},{8,9},{15,14},{13,12},{16,17},{18,... | collective-permute-start | bytes 1179656 | tf_op jit(solution)/shard_map/ppermute | solution.py:38
  56.9 1.9 %collective-permute-start.2 = (f32[640,128]{1,0:T(8,128)S(1)}, f32[640,128]{1,0:T(8,128)S(1)}, u32[]{:S(2)}, u32[]{:S(2)}) collective-permute-start(f32[640,128]{1,0:T(8,128)S(1)} %get-tuple-element.28), channel_id=1, source_target_pairs={{8,12},{12,8},{0,4},{9,13},{13,9},{1,5},{10,14},{14,10},{2,6},{11,... | collective-permute-start | bytes 983048 | tf_op jit(solution)/shard_map/ppermute | solution.py:38
  60.2 0.2 shard_map.169
  60.4 0.1 collective-permute-start.9
  60.5 3.4 %collective-permute-start.5 = (f32[384,128]{1,0:T(8,128)S(1)}, f32[384,128]{1,0:T(8,128)S(1)}, u32[]{:S(2)}, u32[]{:S(2)}) collective-permute-start(f32[384,128]{1,0:T(8,128)S(1)} %get-tuple-element.36), channel_id=1, source_target_pairs={{8,12},{12,8},{0,4},{9,13},{13,9},{1,5},{10,14},{14,10},{2,6},{11,... | collective-permute-start | bytes 589832 | tf_op jit(solution)/shard_map/ppermute | solution.py:38
  63.9 0.1 collective-permute-done.9.refs_1_
  63.9 2.8 %collective-permute-start.10 = (f32[2,136,128]{2,1,0:T(8,128)S(1)}, f32[2,136,128]{2,1,0:T(8,128)S(1)}, u32[]{:S(2)}, u32[]{:S(2)}) collective-permute-start(f32[2,136,128]{2,1,0:T(8,128)S(1)} %shard_map.170), channel_id=1, source_target_pairs={{0,1},{1,0},{2,3},{3,2},{4,5},{5,4},{6,7},{7,6},{8,9},{9,8},{10,11... | collective-permute-start | bytes 417800 | tf_op jit(solution)/shard_map/ppermute | solution.py:38
  66.7 5.0 %shard_map.161 = (f32[256,2048]{1,0:T(8,128)S(1)}, f32[256,2048]{1,0:T(8,128)S(1)}) custom-call(bf16[256,2048]{1,0:T(8,128)(2,1)} %values_hbm.7, bf16[256,128]{1,0:T(8,128)(2,1)} %keys_hbm.7, bf16[256,128]{1,0:T(8,128)(2,1)} %refs_1_.3, f32[256,32]{1,0:T(8,128)S(1)} %get-tuple-element.26.sums_ref, f32[32,256]{1,0:T(8,128)S(1)} %get-tuple-element.29.turned_ref), custom_call_target="tpu_custom_call" | custom-call | flops 100000000 | bytes 1000000 | tf_op jit(solution)/shard_map/pallas_call | solution.py:27
  71.7 1.7 %shard_map.171 = (f32[8,2048]{1,0:T(8,128)S(1)}, f32[8,2048]{1,0:T(8,128)S(1)}, f32[2048,128]{1,0:T(8,128)S(1)}, f32[32,128]{1,0:T(8,128)S(1)}, f32[1,4]{1,0:T(1,128)}) custom-call(f32[1,136,128]{2,1,0:T(8,128)S(1)} %bitcast.18, f32[1,136,128]{2,1,0:T(8,128)S(1)} %collective-permute-done.9.refs_1_, f32[2,136,128]{2,1,0:T(8,128)S(1)} %collective-permute-done.10.refs_2_, ...), custom_call_target="tpu_custom_call" | custom-call | flops 1000000 | bytes 1000000 | tf_op jit(solution)/shard_map/pallas_call | solution.py:27
  73.4 0.0 collective-permute-done.5.refs_1_
  73.4 1.9 %shard_map.164.refs_4_ = bf16[256,2048]{1,0:T(8,128)(2,1)} custom-call(f32[384,128]{1,0:T(8,128)S(1)} %get-tuple-element.35.refs_0_, f32[384,128]{1,0:T(8,128)S(1)} %collective-permute-done.5.refs_1_, bf16[256,128]{1,0:T(8,128)(2,1)} %refs_1_.3, f32[256,2048]{1,0:T(8,128)S(1)} %get-tuple-element.30.refs_3_.refs_2_, ...), custom_call_target="tpu_custom_call" | custom-call | flops 1000000 | bytes 1000000 | tf_op jit(solution)/shard_map/pallas_call | solution.py:27
  75.3 1.8 %shard_map.165.refs_4_ = bf16[256,2048]{1,0:T(8,128)(2,1)} custom-call(f32[640,128]{1,0:T(8,128)S(1)} %get-tuple-element.32.refs_0_, bf16[256,128]{1,0:T(8,128)(2,1)} %refs_1_.3, f32[256,2048]{1,0:T(8,128)S(1)} %get-tuple-element.30.refs_3_.refs_2_, f32[256,2048]{1,0:T(8,128)S(1)} %get-tuple-element.31.refs_4_.refs_3_, ...), custom_call_target="tpu_custom_call", output_to_operand_aliasing={{}: (4, {})} | custom-call | flops 1000000 | bytes 1000000 | tf_op jit(solution)/shard_map/pallas_call | solution.py:27
  77.2 0.0 collective-permute-done.2.refs_0_
  77.2 1.8 %shard_map.166 = bf16[256,2048]{1,0:T(8,128)(2,1)} custom-call(f32[640,128]{1,0:T(8,128)S(1)} %collective-permute-done.2.refs_0_, bf16[256,128]{1,0:T(8,128)(2,1)} %refs_1_.3, f32[256,2048]{1,0:T(8,128)S(1)} %get-tuple-element.30.refs_3_.refs_2_, f32[256,2048]{1,0:T(8,128)S(1)} %get-tuple-element.31.refs_4_.refs_3_, ...), custom_call_target="tpu_custom_call", output_to_operand_aliasing={{}: (4, {})} | custom-call | flops 1000000 | bytes 1000000 | tf_op jit(solution)/shard_map/pallas_call | solution.py:27
  79.1 0.8 %shard_map.174 = (f32[2048,128]{1,0:T(8,128)}, bf16[4,768]{1,0:T(4,128)(2,1)S(1)}) custom-call(f32[2,384,128]{2,1,0:T(8,128)S(1)} %shard_map.173.final_ref, bf16[4,128]{1,0:T(4,128)(2,1)S(1)} %bitcast.21, f32[8,2048]{1,0:T(8,128)S(1)} %get-tuple-element.38.grow_ref, f32[8,2048]{1,0:T(8,128)S(1)} %get-tuple-element.39.part_ref, ...), custom_call_target="tpu_custom_call" | custom-call | flops 1000000 | bytes 1000000 | tf_op jit(solution)/shard_map/pallas_call | solution.py:27
  79.9 0.1 shard_map.168.final_ref
  80.0 1.6 %shard_map.175 = (f32[2048,128]{1,0:T(8,128)}, bf16[4,2048]{1,0:T(4,128)(2,1)}) custom-call(f32[2,640,128]{2,1,0:T(8,128)S(1)} %shard_map.168.final_ref, bf16[4,128]{1,0:T(4,128)(2,1)S(1)} %bitcast.22, f32[8,2048]{1,0:T(8,128)S(1)} %get-tuple-element.38.grow_ref, f32[8,2048]{1,0:T(8,128)S(1)} %get-tuple-element.39.part_ref, ...), custom_call_target="tpu_custom_call", output_to_operand_aliasing={{0}: (7, {})} | custom-call | flops 1000000 | bytes 1000000 | tf_op jit(solution)/shard_map/pallas_call | solution.py:27
  (14 shorter events, 0.1 us)
Async XLA Ops:
  3.8 8.8 %collective-permute-start = (f32[656,128]{1,0:T(8,128)S(1)}, f32[656,128]{1,0:T(8,128)S(1)}, u32[]{:S(2)}, u32[]{:S(2)}) collective-permute-start(f32[656,128]{1,0:T(8,128)S(1)} %shard_map.158), channel_id=1, source_target_pairs={{0,4},{4,0},{8,12},{12,8},{1,5},{5,1},{9,13},{13,9},{2,6},{6,2},{1... | collective-permute-start | bytes 1007624 | tf_op jit(solution)/shard_map/ppermute | solution.py:38
  12.7 22.2 %collective-permute-start.1 = (f32[656,128]{1,0:T(8,128)S(1)}, f32[656,128]{1,0:T(8,128)S(1)}, u32[]{:S(2)}, u32[]{:S(2)}) collective-permute-start(f32[656,128]{1,0:T(8,128)S(1)} %shard_map.159.total_ref), channel_id=1, source_target_pairs={{0,8},{4,12},{8,0},{12,4},{1,9},{5,13},{9,1},{13,5},{2,10},{6,14},... | collective-permute-start | bytes 1007624 | tf_op jit(solution)/shard_map/ppermute | solution.py:38
  12.8 10.1 %collective-permute-start.3 = (f32[392,128]{1,0:T(8,128)S(1)}, f32[392,128]{1,0:T(8,128)S(1)}, u32[]{:S(2)}, u32[]{:S(2)}) collective-permute-start(f32[392,128]{1,0:T(8,128)S(1)} %get-tuple-element.34), channel_id=1, source_target_pairs={{0,4},{4,0},{8,12},{12,8},{1,5},{5,1},{9,13},{13,9},{2,6},{6,2},{1... | collective-permute-start | bytes 602120 | tf_op jit(solution)/shard_map/ppermute | solution.py:38
  22.9 37.2 %copy-start = (bf16[4,1,2048]{2,0,1:T(4,128)(2,1)S(1)}, bf16[4,1,2048]{2,0,1:T(4,128)(2,1)}, u32[]{:S(2)}) copy-start(bf16[4,1,2048]{2,0,1:T(4,128)(2,1)} %param.17) | copy-start | bytes 49156
  22.9 37.2 %copy-start.2 = (f32[4,1,32]{2,1,0:T(1,128)S(1)}, f32[4,1,32]{2,1,0:T(1,128)}, u32[]{:S(2)}) copy-start(f32[4,1,32]{2,1,0:T(1,128)} %param.20) | copy-start | bytes 1540
  22.9 37.2 %copy-start.3 = (bf16[4,1,128]{2,0,1:T(4,128)(2,1)S(1)}, bf16[4,1,128]{2,0,1:T(4,128)(2,1)}, u32[]{:S(2)}) copy-start(bf16[4,1,128]{2,0,1:T(4,128)(2,1)} %param.18) | copy-start | bytes 3076
  23.0 37.2 %copy-start.4 = (f32[4,1]{0,1:T(1,128)S(1)}, f32[4,1]{0,1:T(1,128)}, u32[]{:S(2)}) copy-start(f32[4,1]{0,1:T(1,128)} %param.21) | copy-start | bytes 52
  23.0 37.2 %copy-start.5 = (s32[4,1]{0,1:T(1,128)S(1)}, s32[4,1]{0,1:T(1,128)}, u32[]{:S(2)}) copy-start(s32[4,1]{0,1:T(1,128)} %param.22) | copy-start | bytes 52
  23.0 37.2 %copy-start.6 = (s32[4,1]{0,1:T(1,128)S(1)}, s32[4,1]{0,1:T(1,128)}, u32[]{:S(2)}) copy-start(s32[4,1]{0,1:T(1,128)} %param.23) | copy-start | bytes 52
  23.0 16.1 %collective-permute-start.4 = (f32[392,128]{1,0:T(8,128)S(1)}, f32[392,128]{1,0:T(8,128)S(1)}, u32[]{:S(2)}, u32[]{:S(2)}) collective-permute-start(f32[392,128]{1,0:T(8,128)S(1)} %shard_map.162.total_ref), channel_id=1, source_target_pairs={{0,8},{4,12},{8,0},{12,4},{1,9},{5,13},{9,1},{13,5},{2,10},{6,14},... | collective-permute-start | bytes 602120 | tf_op jit(solution)/shard_map/ppermute | solution.py:38
  34.9 7.8 %collective-permute-start.6 = (f32[640,128]{1,0:T(8,128)S(1)}, f32[640,128]{1,0:T(8,128)S(1)}, u32[]{:S(2)}, u32[]{:S(2)}) collective-permute-start(f32[640,128]{1,0:T(8,128)S(1)} %get-tuple-element.37.final_ref), channel_id=1, source_target_pairs={{4,0},{1,5},{14,10},{11,15},{0,2},{5,7},{10,8},{15,13},{20,16},{17... | collective-permute-start | bytes 983048 | tf_op jit(solution)/shard_map/ppermute | solution.py:38
  36.2 11.1 %collective-permute-start.7 = (f32[640,128]{1,0:T(8,128)S(1)}, f32[640,128]{1,0:T(8,128)S(1)}, u32[]{:S(2)}, u32[]{:S(2)}) collective-permute-start(f32[640,128]{1,0:T(8,128)S(1)} %get-tuple-element.37.final_ref), channel_id=1, source_target_pairs={{4,2},{1,7},{14,8},{11,13},{20,18},{17,23},{30,24},{27,29}} | collective-permute-start | bytes 983048 | tf_op jit(solution)/shard_map/ppermute | solution.py:38
  39.2 32.5 %copy-start.1 = (bf16[4,1,128]{2,0,1:T(4,128)(2,1)S(1)}, bf16[4,1,128]{2,0,1:T(4,128)(2,1)}, u32[]{:S(2)}) copy-start(bf16[4,1,128]{2,0,1:T(4,128)(2,1)} %param.19) | copy-start | bytes 3076
  39.2 9.9 %collective-permute-start.11 = (f32[384,128]{1,0:T(8,128)S(1)}, f32[384,128]{1,0:T(8,128)S(1)}, u32[]{:S(2)}, u32[]{:S(2)}) collective-permute-start(f32[384,128]{1,0:T(8,128)S(1)} %get-tuple-element.42.final_ref), channel_id=1, source_target_pairs={{4,0},{1,5},{14,10},{11,15},{0,2},{5,7},{10,8},{15,13},{20,16},{17... | collective-permute-start | bytes 589832 | tf_op jit(solution)/shard_map/ppermute | solution.py:38
  47.4 32.5 %collective-permute-start.8 = (f32[2,640,128]{2,1,0:T(8,128)S(1)}, f32[2,640,128]{2,1,0:T(8,128)S(1)}, u32[]{:S(2)}, u32[]{:S(2)}) collective-permute-start(f32[2,640,128]{2,1,0:T(8,128)S(1)} %shard_map.167.mine_ref), channel_id=1, source_target_pairs={{0,1},{2,3},{5,4},{7,6},{10,11},{8,9},{15,14},{13,12},{16,17},{18,... | collective-permute-start | bytes 1966088 | tf_op jit(solution)/shard_map/ppermute | solution.py:38
  49.1 6.4 %collective-permute-start.12 = (f32[384,128]{1,0:T(8,128)S(1)}, f32[384,128]{1,0:T(8,128)S(1)}, u32[]{:S(2)}, u32[]{:S(2)}) collective-permute-start(f32[384,128]{1,0:T(8,128)S(1)} %collective-permute-done.11.next_ref), channel_id=1, source_target_pairs={{0,2},{5,7},{10,8},{15,13},{16,18},{21,23},{26,24},{31,29}} | collective-permute-start | bytes 589832 | tf_op jit(solution)/shard_map/ppermute | solution.py:38
  55.6 23.4 %collective-permute-start.13 = (f32[2,384,128]{2,1,0:T(8,128)S(1)}, f32[2,384,128]{2,1,0:T(8,128)S(1)}, u32[]{:S(2)}, u32[]{:S(2)}) collective-permute-start(f32[2,384,128]{2,1,0:T(8,128)S(1)} %shard_map.172.mine_ref), channel_id=1, source_target_pairs={{0,1},{2,3},{5,4},{7,6},{10,11},{8,9},{15,14},{13,12},{16,17},{18,... | collective-permute-start | bytes 1179656 | tf_op jit(solution)/shard_map/ppermute | solution.py:38
  56.9 20.3 %collective-permute-start.2 = (f32[640,128]{1,0:T(8,128)S(1)}, f32[640,128]{1,0:T(8,128)S(1)}, u32[]{:S(2)}, u32[]{:S(2)}) collective-permute-start(f32[640,128]{1,0:T(8,128)S(1)} %get-tuple-element.28), channel_id=1, source_target_pairs={{8,12},{12,8},{0,4},{9,13},{13,9},{1,5},{10,14},{14,10},{2,6},{11,... | collective-permute-start | bytes 983048 | tf_op jit(solution)/shard_map/ppermute | solution.py:38
  60.4 3.5 %collective-permute-start.9 = (f32[1,136,128]{2,1,0:T(8,128)S(1)}, f32[1,136,128]{2,1,0:T(8,128)S(1)}, u32[]{:S(2)}, u32[]{:S(2)}) collective-permute-start(f32[1,136,128]{2,1,0:T(8,128)S(1)} %bitcast.16), channel_id=1, source_target_pairs={{0,2},{1,3},{2,0},{3,1},{4,6},{5,7},{6,4},{7,5},{8,10},{9,11},{10,... | collective-permute-start | bytes 208904 | tf_op jit(solution)/shard_map/ppermute | solution.py:38
  60.5 12.9 %collective-permute-start.5 = (f32[384,128]{1,0:T(8,128)S(1)}, f32[384,128]{1,0:T(8,128)S(1)}, u32[]{:S(2)}, u32[]{:S(2)}) collective-permute-start(f32[384,128]{1,0:T(8,128)S(1)} %get-tuple-element.36), channel_id=1, source_target_pairs={{8,12},{12,8},{0,4},{9,13},{13,9},{1,5},{10,14},{14,10},{2,6},{11,... | collective-permute-start | bytes 589832 | tf_op jit(solution)/shard_map/ppermute | solution.py:38
  63.9 7.8 %collective-permute-start.10 = (f32[2,136,128]{2,1,0:T(8,128)S(1)}, f32[2,136,128]{2,1,0:T(8,128)S(1)}, u32[]{:S(2)}, u32[]{:S(2)}) collective-permute-start(f32[2,136,128]{2,1,0:T(8,128)S(1)} %shard_map.170), channel_id=1, source_target_pairs={{0,1},{1,0},{2,3},{3,2},{4,5},{5,4},{6,7},{7,6},{8,9},{9,8},{10,11... | collective-permute-start | bytes 417800 | tf_op jit(solution)/shard_map/ppermute | solution.py:38
